TPU v7x, 16 devices: a whole 2x2x2 slice. The times are simulated.
16 devices in a mesh: data: 16 (over z, y, x, core).
Axes of the slice: x: 2, y: 2, z: 2, core: 2. Of those that a mesh axis runs over, the one named last changes fastest.
Arguments:
- feat_a: bfloat16 [16384, 512], P('data')
- feat_b: bfloat16 [16384, 512], P('data')
- w_in: bfloat16 [512, 2048], replicated
- w_mid: bfloat16 [2048, 2048], replicated
- w_out: bfloat16 [2048, 2048], replicated
- t_in: bfloat16 [512, 2048], replicated
- t_mid: bfloat16 [2048, 2048], replicated
- t_out: bfloat16 [2048, 2048], replicated
- gain_1: float32 [2048], replicated
- bias_1: float32 [2048], replicated
- gain_2: float32 [2048], replicated
- bias_2: float32 [2048], replicated
- off_weight: float32 [], replicated
Outputs:
- output 1: float32 [], replicated
- output 2: float32 [16384, 2048], P('data')
- output 3: float32 [512, 2048], replicated
- output 4: float32 [2048, 2048], replicated
- output 5: float32 [2048, 2048], replicated
- output 6: float32 [2048], replicated
- output 7: float32 [2048], replicated
- output 8: float32 [2048], replicated
- output 9: float32 [2048], replicated
All inputs are finite; a program needn't handle non-finite values.
Results may differ from a plain program's by a relative error of at most 0.00291604.
Values are sent between devices in bfloat16 or wider.
A program may use at most 1 GiB of HBM per device.

v0:
```python
import jax
import jax.numpy as jnp
from jax import lax
from jax.sharding import PartitionSpec as P

NORM_EPS = 1e-5
DATA_AXIS = "data"


def contract_rows(left_op, right_op):
    return lax.dot_general(left_op, right_op, (((0,), (0,)), ((), ())), preferred_element_type=jnp.float32)


def contract_cols(left_op, right_op):
    return lax.dot_general(left_op, right_op, (((1,), (1,)), ((), ())), preferred_element_type=jnp.float32)


def solution(mesh):
    shards = mesh.shape[DATA_AXIS]
    row_part = P(DATA_AXIS, None)
    replicated = P()

    def local_step(feat_a, feat_b, w_in, w_mid, w_out, t_in, t_mid, t_out, gain_1, bias_1, gain_2, bias_2, off_weight):
        row_count = feat_a.shape[0] * shards

        def norm_pair(pre_a, pre_b):
            stat_sums = jnp.stack([jnp.sum(pre_a, axis=0), jnp.sum(pre_a * pre_a, axis=0), jnp.sum(pre_b, axis=0), jnp.sum(pre_b * pre_b, axis=0)])
            stat_means = lax.psum(stat_sums, DATA_AXIS) / row_count
            inv_a = lax.rsqrt(stat_means[1] - stat_means[0] * stat_means[0] + NORM_EPS)
            inv_b = lax.rsqrt(stat_means[3] - stat_means[2] * stat_means[2] + NORM_EPS)
            return (pre_a - stat_means[0]) * inv_a, inv_a, (pre_b - stat_means[2]) * inv_b

        def hidden_pair(in_a, in_b, weight_a, weight_b, gain_vec, bias_vec):
            normed_a, inv_a, normed_b = norm_pair(jnp.dot(in_a, weight_a, preferred_element_type=jnp.float32), jnp.dot(in_b, weight_b, preferred_element_type=jnp.float32))
            pre_act = normed_a * gain_vec + bias_vec
            act_a = jnp.maximum(pre_act, 0.0).astype(jnp.bfloat16)
            act_b = jnp.maximum(normed_b * gain_vec + bias_vec, 0.0).astype(jnp.bfloat16)
            return act_a, act_b, normed_a, inv_a, pre_act > 0.0

        def norm_back(grad_n, normed, inv_std):
            stat_means = lax.psum(jnp.stack([jnp.sum(grad_n, axis=0), jnp.sum(grad_n * normed, axis=0)]), DATA_AXIS) / row_count
            return (grad_n - stat_means[0] - normed * stat_means[1]) * inv_std

        def affine_back(grad_pre, normed, inv_std, gain_vec):
            stat_sums = lax.psum(jnp.stack([jnp.sum(grad_pre * normed, axis=0), jnp.sum(grad_pre, axis=0)]), DATA_AXIS)
            grad_u = (grad_pre - stat_sums[1] / row_count - normed * (stat_sums[0] / row_count)) * (gain_vec * inv_std)
            return grad_u.astype(jnp.bfloat16), stat_sums[0], stat_sums[1]

        act_1, teach_1, normed_1, inv_1, mask_1 = hidden_pair(feat_a, feat_b, w_in, t_in, gain_1, bias_1)
        act_2, teach_2, normed_2, inv_2, mask_2 = hidden_pair(act_1, teach_1, w_mid, t_mid, gain_2, bias_2)
        zh_a, inv_z, zh_b = norm_pair(jnp.dot(act_2, w_out, preferred_element_type=jnp.float32), jnp.dot(teach_2, t_out, preferred_element_type=jnp.float32))
        emb_a = zh_a.astype(jnp.bfloat16)
        emb_b = zh_b.astype(jnp.bfloat16)
        corr_mat = lax.psum(contract_rows(emb_a, emb_b), DATA_AXIS) / row_count
        proj_width = corr_mat.shape[0]
        on_diag = lax.broadcasted_iota(jnp.int32, (proj_width, proj_width), 0) == lax.broadcasted_iota(jnp.int32, (proj_width, proj_width), 1)
        loss_value = jnp.sum(jnp.where(on_diag, jnp.square(1.0 - corr_mat), off_weight * jnp.square(corr_mat)))
        grad_c = jnp.where(on_diag, -2.0 * (1.0 - corr_mat), 2.0 * off_weight * corr_mat).astype(jnp.bfloat16)
        grad_emb = contract_cols(emb_b, grad_c) / row_count
        grad_z = norm_back(grad_emb, zh_a, inv_z).astype(jnp.bfloat16)
        grad_w_out = contract_rows(act_2, grad_z)
        grad_pre_2 = jnp.where(mask_2, contract_cols(grad_z, w_out), 0.0)
        grad_u_2, grad_gain_2, grad_bias_2 = affine_back(grad_pre_2, normed_2, inv_2, gain_2)
        grad_w_mid = contract_rows(act_1, grad_u_2)
        grad_pre_1 = jnp.where(mask_1, contract_cols(grad_u_2, w_mid), 0.0)
        grad_u_1, grad_gain_1, grad_bias_1 = affine_back(grad_pre_1, normed_1, inv_1, gain_1)
        grad_w_in = contract_rows(feat_a, grad_u_1)
        weight_grads = lax.psum((grad_w_in, grad_w_mid, grad_w_out), DATA_AXIS)
        return (loss_value, grad_emb, weight_grads[0], weight_grads[1], weight_grads[2], grad_gain_1, grad_bias_1, grad_gain_2, grad_bias_2)

    return jax.shard_map(local_step, mesh=mesh, in_specs=(row_part, row_part) + (replicated,) * 11, out_specs=(replicated, row_part) + (replicated,) * 7, check_vma=False)
```

profile of v0, /device:TPU:0, one launch (start us, length us, event | category | flops | bytes accessed | tf_op | source)
XLA Modules:
  0.0 965.6 jit_solution(4841144950243668467)
XLA Ops:
  7.2 0.0 copy-start
  7.2 0.0 copy-start.7
  7.2 0.0 all-reduce.4.cloned.1.call-start
  7.3 1.5 copy-done
  8.8 7.1 fusion.53
  15.9 0.0 copy-done.7
  15.9 0.0 copy-done.6
  15.9 5.6 fusion.52
  21.5 35.2 %psum.70 = f32[4,2048]{1,0:T(4,128)S(1)} all-reduce(f32[4,2048]{1,0:T(4,128)S(1)} %pad_maximum_fusion), channel_id=1, replica_groups=mesh['data'=16] {'data'}, use_global_device_ids=true, to_apply=%region_4.0 | all-reduce | flops 8192 | bytes 65536 | tf_op jit(solution)/shard_map/psum | solution.py:28
  56.8 0.0 copy-done.5
  56.8 0.0 copy-done.10
  56.8 0.0 copy-start.11
  56.8 16.0 %fusion.51 = (f32[2048]{0:T(1024)S(1)}, f32[2048]{0:T(1024)S(1)}, f32[1024,2048]{1,0:T(8,128)}) fusion(bf16[2048,2048]{1,0:T(8,128)(2,1)} %param.19, f32[1024,2048]{1,0:T(8,128)} %get-tuple-element.63, f32[2048]{0:T(1024)S(1)} %bitcast.91, f32[2048]{0:T(1024)S(1)} %bitcast.92, f32[2048]{0:T(1024)S(1)} %copy-done.10, f32[2048]{0:T(1024)S(1)} %copy-done.5), kind=kOutput, calls=%fused_computation.99 | convolution fusion | flops 8608804864 | bytes 25214976 | tf_op jit(solution)/shard_map/dot_general | solution.py:34
  72.8 0.0 copy-done.11
  72.8 13.3 %fusion.50 = (f32[2048]{0:T(1024)S(1)}, f32[2048]{0:T(1024)S(1)}, f32[1024,2048]{1,0:T(8,128)}) fusion(bf16[2048,2048]{1,0:T(8,128)(2,1)} %param.16, f32[1024,2048]{1,0:T(8,128)S(1)} %copy-done.11, f32[2048]{0:T(1024)S(1)} %copy-done.10, f32[2048]{0:T(1024)S(1)} %copy-done.5, f32[2048]{0:T(1024)S(1)} %bitcast.87, f32[2048]{0:T(1024)S(1)} %bitcast.80), kind=kOutput, calls=%fused_computation.98 | convolution fusion | flops 8608804864 | bytes 25214976 | tf_op jit(solution)/shard_map/dot_general | solution.py:34
  86.1 33.4 %psum.71 = f32[4,2048]{1,0:T(4,128)S(1)} all-reduce(f32[4,2048]{1,0:T(4,128)S(1)} %pad_maximum_fusion.1), channel_id=1, replica_groups=mesh['data'=16] {'data'}, use_global_device_ids=true, to_apply=%region_9.0 | all-reduce | flops 8192 | bytes 65536 | tf_op jit(solution)/shard_map/psum | solution.py:28
  119.6 0.0 copy-done.4
  119.6 15.9 %fusion.49 = (f32[2048]{0:T(1024)S(1)}, f32[2048]{0:T(1024)S(1)}, f32[1024,2048]{1,0:T(8,128)}) fusion(bf16[2048,2048]{1,0:T(8,128)(2,1)} %param.20, f32[1024,2048]{1,0:T(8,128)} %get-tuple-element.65, f32[2048]{0:T(1024)S(1)} %bitcast.93, f32[2048]{0:T(1024)S(1)} %bitcast.94, f32[2048]{0:T(1024)S(1)} %copy-done.9, f32[2048]{0:T(1024)S(1)} %copy-done.4), kind=kOutput, calls=%fused_computation.97 | convolution fusion | flops 8608804864 | bytes 25214976 | tf_op jit(solution)/shard_map/dot_general | solution.py:51
  135.5 13.3 %fusion.48 = (f32[2048]{0:T(1024)S(1)}, f32[2048]{0:T(1024)S(1)}, f32[1024,2048]{1,0:T(8,128)}) fusion(bf16[2048,2048]{1,0:T(8,128)(2,1)} %param.17, f32[1024,2048]{1,0:T(8,128)S(1)} %copy-done.3, f32[2048]{0:T(1024)S(1)} %copy-done.9, f32[2048]{0:T(1024)S(1)} %copy-done.4, f32[2048]{0:T(1024)S(1)} %bitcast.74, f32[2048]{0:T(1024)S(1)} %bitcast.61), kind=kOutput, calls=%fused_computation.96 | convolution fusion | flops 8608804864 | bytes 25214976 | tf_op jit(solution)/shard_map/dot_general | solution.py:51
  148.9 33.0 %psum.72 = f32[4,2048]{1,0:T(4,128)S(1)} all-reduce(f32[4,2048]{1,0:T(4,128)S(1)} %pad_maximum_fusion.2), channel_id=1, replica_groups=mesh['data'=16] {'data'}, use_global_device_ids=true, to_apply=%region_14.0 | all-reduce | flops 8192 | bytes 65536 | tf_op jit(solution)/shard_map/psum | solution.py:28
  182.0 17.4 %fusion.7 = f32[2048,2048]{1,0:T(8,128)} fusion(f32[1024,2048]{1,0:T(8,128)} %get-tuple-element.68, f32[2048]{0:T(1024)S(1)} %bitcast.68, f32[2048]{0:T(1024)S(1)} %bitcast.71, f32[1024,2048]{1,0:T(8,128)} %get-tuple-element.67, f32[2048]{0:T(1024)S(1)} %bitcast.109, f32[2048]{0:T(1024)S(1)} %bitcast.107), kind=kOutput, calls=%fused_computation.34 | convolution fusion | flops 8602517504 | bytes 33587200 | tf_op jit(solution)/shard_map/dot_general | solution.py:11
  199.4 0.0 all-reduce.4.cloned.1.call-update
  199.4 0.0 all-reduce.6.cloned.1.call-start
  200.1 180.1 %all-reduce.4.cloned.1.call-done = f32[2048,2048]{1,0:T(8,128)} async-done(((f32[2048,2048]{1,0:T(8,128)}), f32[2048,2048]{1,0:T(8,128)}) %all-reduce.4.cloned.1.call-update) | async-done | bytes 16777232 | tf_op jit(solution)/shard_map/psum | solution.py:54
  380.3 19.0 %fusion.47 = (f32[2048]{0:T(1024)S(1)}, f32[2048]{0:T(1024)S(1)}, f32[1024,2048]{1,0:T(8,128)}) fusion(f32[2048]{0:T(1024)S(1)} %bitcast.69, f32[1024,2048]{1,0:T(8,128)} %get-tuple-element.68, f32[2048]{0:T(1024)S(1)} %bitcast.72, f32[2048,2048]{1,0:T(8,128)} %all-reduce.4.cloned.1.call-done, f32[]{:T(128)S(6)} %mul.261, ...), kind=kOutput, calls=%fused_computation.95 | convolution fusion | flops 8638164992 | bytes 41992196 | tf_op jit(solution)/shard_map/dot_general | solution.py:15
  399.3 31.7 %psum.74 = f32[2,2048]{1,0:T(2,128)S(1)} all-reduce(f32[2,2048]{1,0:T(2,128)S(1)} %pad_maximum_fusion.3), channel_id=1, replica_groups=mesh['data'=16] {'data'}, use_global_device_ids=true, to_apply=%region_19.20 | all-reduce | flops 4096 | bytes 32768 | tf_op jit(solution)/shard_map/psum | solution.py:41
  431.0 0.0 slice-start
  431.0 7.2 multiply_convert_fusion.2
  438.2 0.0 slice-start.1
  438.2 16.0 %multiply_reduce_fusion.1 = (f32[2048]{0:T(1024)S(1)}, f32[2048]{0:T(1024)S(1)}, f32[1024,2048]{1,0:T(8,128)}) fusion(f32[1024,2048]{1,0:T(8,128)} %get-tuple-element.66, f32[2048]{0:T(1024)S(1)} %bitcast.75, f32[2048]{0:T(1024)S(1)} %bitcast.63, bf16[1024,2048]{1,0:T(8,128)(2,1)S(1)} %multiply_convert_fusion.2, bf16[2048,2048]{1,0:T(8,128)(2,1)} %param.17, ...), kind=kOutput, calls=%fused_computation.7 | convolution fusion | flops 8608804864 | bytes 29409280 | tf_op jit(solution)/shard_map/dot_general | solution.py:15
  454.3 12.2 %fusion.45 = f32[2048,2048]{1,0:T(8,128)} fusion(bf16[1024,2048]{1,0:T(8,128)(2,1)S(1)} %multiply_convert_fusion.2, f32[1024,2048]{1,0:T(8,128)S(1)} %bitcast.60, f32[2048]{0:T(1024)S(1)} %copy-done.9, f32[2048]{0:T(1024)S(1)} %copy-done.4, f32[2048]{0:T(1024)S(1)} %bitcast.76, f32[2048]{0:T(1024)S(1)} %bitcast.64), kind=kOutput, calls=%fused_computation.93 | convolution fusion | flops 8602517504 | bytes 29392896 | tf_op jit(solution)/shard_map/dot_general | solution.py:11
  466.5 33.0 %psum.75 = f32[2,2048]{1,0:T(2,128)S(1)} all-reduce(f32[2,2048]{1,0:T(2,128)S(1)} %pad_maximum_fusion.4), channel_id=1, replica_groups=mesh['data'=16] {'data'}, use_global_device_ids=true, to_apply=%region_22.23 | all-reduce | flops 4096 | bytes 32768 | tf_op jit(solution)/shard_map/psum | solution.py:45
  499.5 0.6 fusion.57
  500.1 7.2 multiply_convert_fusion.1
  507.3 0.0 slice-start.3
  507.3 16.0 %multiply_reduce_fusion = (f32[2048]{0:T(1024)S(1)}, f32[2048]{0:T(1024)S(1)}, f32[1024,2048]{1,0:T(8,128)}) fusion(f32[1024,2048]{1,0:T(8,128)} %get-tuple-element.64, f32[2048]{0:T(1024)S(1)} %bitcast.88, f32[2048]{0:T(1024)S(1)} %bitcast.82, bf16[1024,2048]{1,0:T(8,128)(2,1)S(1)} %multiply_convert_fusion.1, bf16[2048,2048]{1,0:T(8,128)(2,1)} %param.16, ...), kind=kOutput, calls=%fused_computation.5 | convolution fusion | flops 8608804864 | bytes 29409280 | tf_op jit(solution)/shard_map/dot_general | solution.py:15
  523.3 0.0 copy-start.8
  523.3 12.2 %fusion.43 = f32[2048,2048]{1,0:T(8,128)} fusion(bf16[1024,2048]{1,0:T(8,128)(2,1)S(1)} %multiply_convert_fusion.1, f32[1024,2048]{1,0:T(8,128)S(1)} %bitcast.124, f32[2048]{0:T(1024)S(1)} %copy-done.10, f32[2048]{0:T(1024)S(1)} %copy-done.5, f32[2048]{0:T(1024)S(1)} %bitcast.89, f32[2048]{0:T(1024)S(1)} %bitcast.83), kind=kOutput, calls=%fused_computation.91 | convolution fusion | flops 8602517504 | bytes 29392896 | tf_op jit(solution)/shard_map/dot_general | solution.py:11
  535.5 33.1 %psum.76 = f32[2,2048]{1,0:T(2,128)S(1)} all-reduce(f32[2,2048]{1,0:T(2,128)S(1)} %pad_maximum_fusion.5), channel_id=1, replica_groups=mesh['data'=16] {'data'}, use_global_device_ids=true, to_apply=%region_25.26 | all-reduce | flops 4096 | bytes 32768 | tf_op jit(solution)/shard_map/psum | solution.py:45
  568.6 0.6 fusion.58
  569.2 10.3 %fusion.29 = f32[512,2048]{0,1:T(8,128)} fusion(bf16[1024,512]{1,0:T(8,128)(2,1)S(1)} %copy-done.8, f32[1024,2048]{1,0:T(8,128)} %get-tuple-element.71, f32[1024,2048]{1,0:T(8,128)} %get-tuple-element.64, f32[2048]{0:T(1024)S(1)} %rsqrt_multiply_fusion, f32[2048]{0:T(1024)S(1)} %bitcast.100, f32[2048]{0:T(1024)S(1)} %bitcast.99, f32[2048]{0:T(1024)S(1)} %bitcast.90, ...), kind=kOutput, calls=%fused_computation.55 | convolution fusion | flops 2162163712 | bytes 22061056 | tf_op jit(solution)/shard_map/dot_general | solution.py:11
  579.5 0.0 all-reduce.6.cloned.1.call-update
  579.6 8.8 select_reduce_fusion
  588.3 341.9 %all-reduce.6.cloned.1.call-done = (f32[512,2048]{0,1:T(8,128)}, f32[2048,2048]{1,0:T(8,128)}, f32[2048,2048]{1,0:T(8,128)}) async-done(((f32[512,2048]{0,1:T(8,128)}, f32[2048,2048]{1,0:T(8,128)}, f32[2048,2048]{1,0:T(8,128)}), (f32[512,2048]{0,1:T(8,128)}, f32[2048,2048]{1,0:T(8,128)}, f32[2048,2048]{1,0:T(8,128)})) %all-reduce.6.cloned.1.call-update) | async-done | bytes 37748752 | tf_op jit(solution)/shard_map/psum | solution.py:68
  930.2 5.3 copy.22
  935.5 12.7 %copy.28 = f32[2048,2048]{1,0:T(8,128)} copy(f32[2048,2048]{1,0:T(8,128)} %get-tuple-element.75) | data formatting | bytes 33554432
  948.2 3.7 copy-done.2
  952.0 6.3 copy.29
  (35 shorter events, 0.4 us)
Async XLA Ops:
  7.2 1.6 copy-start
  7.2 8.7 copy-start.7
  7.2 373.0 %all-reduce.4.cloned.1.call-start = ((), (), s32[]{:S(2)}) async-start(), calls=%async_computation | async-start | bytes 33554432 | tf_op jit(solution)/shard_map/psum | solution.py:54
  8.8 7.1 copy-start.6
  15.9 40.9 %copy-start.5 = (f32[2048]{0:T(1024)S(1)}, f32[2048]{0:T(1024)}, u32[]{:S(2)}) copy-start(f32[2048]{0:T(1024)} %param.21) | copy-start | bytes 24580
  15.9 40.9 %copy-start.10 = (f32[2048]{0:T(1024)S(1)}, f32[2048]{0:T(1024)}, u32[]{:S(2)}) copy-start(f32[2048]{0:T(1024)} %param.22) | copy-start | bytes 24580
  56.8 16.0 %copy-start.11 = (f32[1024,2048]{1,0:T(8,128)S(1)}, f32[1024,2048]{1,0:T(8,128)}, u32[]{:S(2)}) copy-start(f32[1024,2048]{1,0:T(8,128)} %get-tuple-element.64) | copy-start | bytes 25165828
  72.8 46.8 %copy-start.4 = (f32[2048]{0:T(1024)S(1)}, f32[2048]{0:T(1024)}, u32[]{:S(2)}) copy-start(f32[2048]{0:T(1024)} %param.23) | copy-start | bytes 24580
  72.8 46.8 %copy-start.9 = (f32[2048]{0:T(1024)S(1)}, f32[2048]{0:T(1024)}, u32[]{:S(2)}) copy-start(f32[2048]{0:T(1024)} %param.24) | copy-start | bytes 24580
  119.6 15.9 %copy-start.3 = (f32[1024,2048]{1,0:T(8,128)S(1)}, f32[1024,2048]{1,0:T(8,128)}, u32[]{:S(2)}) copy-start(f32[1024,2048]{1,0:T(8,128)} %get-tuple-element.66) | copy-start | bytes 25165828
  199.4 730.8 %all-reduce.6.cloned.1.call-start = ((), (), s32[]{:S(2)}) async-start(), calls=%async_computation.1 | async-start | bytes 75497472 | tf_op jit(solution)/shard_map/psum | solution.py:68
  431.0 23.3 %slice-start = ((s8[8388608]{0:T(1024)(128)(4,1)}), s8[4194304]{0:T(1024)(128)(4,1)S(1)}, s32[]{:S(2)}) async-start(s8[8388608]{0:T(1024)(128)(4,1)} %bitcast.59), calls=%async_computation.2 | async-start | bytes 8388608
  438.2 16.0 %slice-start.1 = ((s8[8388608]{0:T(1024)(128)(4,1)}), s8[4194304]{0:T(1024)(128)(4,1)S(1)}, s32[]{:S(2)}) async-start(s8[8388608]{0:T(1024)(128)(4,1)} %bitcast.59), calls=%async_computation.3 | async-start | bytes 8388608
  500.1 23.2 %slice-start.2 = ((s8[8388608]{0:T(1024)(128)(4,1)}), s8[4194304]{0:T(1024)(128)(4,1)S(1)}, s32[]{:S(2)}) async-start(s8[8388608]{0:T(1024)(128)(4,1)} %bitcast.123), calls=%async_computation.4 | async-start | bytes 8388608
  507.3 16.0 %slice-start.3 = ((s8[8388608]{0:T(1024)(128)(4,1)}), s8[4194304]{0:T(1024)(128)(4,1)S(1)}, s32[]{:S(2)}) async-start(s8[8388608]{0:T(1024)(128)(4,1)} %bitcast.123), calls=%async_computation.5 | async-start | bytes 8388608
  523.3 45.9 %copy-start.8 = (bf16[1024,512]{1,0:T(8,128)(2,1)S(1)}, bf16[1024,512]{1,0:T(8,128)(2,1)}, u32[]{:S(2)}) copy-start(bf16[1024,512]{1,0:T(8,128)(2,1)} %param.13) | copy-start | bytes 3145732
  935.5 16.4 %copy-start.2 = (f32[2048,2048]{1,0:T(8,128)S(1)}, f32[2048,2048]{1,0:T(8,128)}, u32[]{:S(2)}) copy-start(f32[2048,2048]{1,0:T(8,128)} %get-tuple-element.76) | copy-start | bytes 50331652
  952.0 6.3 copy-start.1
Sparse Core Ops, SparseCore 0:
  199.5 180.7 all-reduce.3
  579.7 350.4 all-reduce.5
where the time goes:
time: 970 us; the launch traced here: 966 us
  waiting for transfers between devices  522 us (54%)
  blocking collectives  199 us (21%)
  matrix products  174 us (18%)
  local copies, waits for them, and re-layouts  29.7 us (3%)
  other arithmetic  24.8 us (3%)
  between operations  15.4 us (2%)
    psum x1, waiting for transfers between devices, local_step(): weight_grads = lax.psum((grad_w_in, grad_w_mid, grad_w_out), DATA_AXIS)  342 us
    psum x1, waiting for transfers between devices, local_step(): corr_mat = lax.psum(contract_rows(emb_a, emb_b), DATA_AXIS) / row_count  180 us
    psum x3, blocking collectives, norm_pair(): stat_means = lax.psum(stat_sums, DATA_AXIS) / row_count  102 us
    psum x2, blocking collectives, affine_back(): lax.psum(jnp.stack([jnp.sum(grad_pre * normed, axis=0), jnp.sum(grad_pre,...  66.1 us
    dot_general x4, matrix products, contract_rows(): lax.dot_general(left_op, right_op, (((0,), (0,)), ((), ())), preferred_el...  52.1 us
    dot_general x3, matrix products, contract_cols(): lax.dot_general(left_op, right_op, (((1,), (1,)), ((), ())), preferred_el...  51 us
    psum x1, blocking collectives, norm_back(): lax.psum(jnp.stack([jnp.sum(grad_n, axis=0), jnp.sum(grad_n * normed, axi...  31.7 us
    unnamed x35, local copies, waits for them, and re-layouts  29.6 us
  transfers between devices with their start and end apart: 2, of which 2 were waited for; matrix products, arithmetic and copies ran while one was open for 1% of the time, Pallas kernels for 0%

commit v1 on v0

v1 whole, which is shorter than its diff:
```python
import functools

import jax
import jax.numpy as jnp
from jax import lax
from jax.experimental import pallas as pl
from jax.experimental.pallas import tpu as pltpu
from jax.sharding import PartitionSpec as P

NORM_EPS = 1e-5
DATA_AXIS = "data"
MESH_ID = pl.DeviceIdType.MESH
UNIT = 128
VMEM_LIMIT = 66_000_000


def contract_rows(left_op, right_op):
    return lax.dot_general(left_op, right_op, (((0,), (0,)), ((), ())), preferred_element_type=jnp.float32)


def contract_cols(left_op, right_op):
    return lax.dot_general(left_op, right_op, (((1,), (1,)), ((), ())), preferred_element_type=jnp.float32)


def flip(me, mask):
    bit = lax.rem(lax.div(me, mask), 2)
    return me + mask * (1 - 2 * bit), bit


def stats_kernel(shards, x_ref, out_ref, parts, send_a, recv_a, send_b, recv_b):
    me = lax.axis_index(DATA_AXIS)
    lanes = x_ref.shape[1] // shards
    barrier = pltpu.get_barrier_semaphore()
    for step in range(1, shards):
        peer = lax.rem(me + step, shards)
        pl.semaphore_signal(barrier, inc=1, device_id=(peer,), device_id_type=MESH_ID)
    pl.semaphore_wait(barrier, shards - 1)

    def lane_block(index):
        return pl.ds(pl.multiple_of(index * lanes, lanes), lanes)

    def scatter(step):
        peer = lax.rem(me + step, shards)
        return pltpu.make_async_remote_copy(src_ref=x_ref.at[:, lane_block(peer)], dst_ref=parts.at[step], send_sem=send_a.at[step], recv_sem=recv_a.at[step], device_id=(peer,), device_id_type=MESH_ID)

    def gather(step):
        peer = lax.rem(me + step, shards)
        mine = lane_block(me)
        return pltpu.make_async_remote_copy(src_ref=parts.at[0], dst_ref=out_ref.at[:, mine], send_sem=send_b.at[step], recv_sem=recv_b.at[step], device_id=(peer,), device_id_type=MESH_ID)

    for step in range(1, shards):
        scatter(step).start()
    total = x_ref[:, lane_block(me)]
    for step in range(1, shards):
        scatter(step).wait()
        total = total + parts[step]
    parts[0] = total
    out_ref[:, lane_block(me)] = total
    for step in range(1, shards):
        gather(step).start()
    for step in range(1, shards):
        gather(step).wait()


def stats_all_reduce(rows, shards):
    pad = [jnp.zeros_like(rows[0])] * (8 - len(rows))
    packed = jnp.stack(list(rows) + pad)
    lanes = packed.shape[1] // shards
    vmem = pl.BlockSpec(memory_space=pltpu.VMEM)
    return pl.pallas_call(
        functools.partial(stats_kernel, shards),
        out_shape=jax.ShapeDtypeStruct(packed.shape, jnp.float32),
        in_specs=[vmem],
        out_specs=vmem,
        scratch_shapes=[pltpu.VMEM((shards, 8, lanes), jnp.float32)] + [pltpu.SemaphoreType.DMA((shards,))] * 4,
        compiler_params=pltpu.CompilerParams(collective_id=1, has_side_effects=True),
        name="stats_all_reduce",
    )(packed)


PAIR, RS1, RS2, RS3, AG3, AG2, AG1, AGP, LOCAL = range(9)


class Exchange:
    def __init__(self, me, ring, halves, gathered, recv_pair, recv_1, recv_2, recv_3, total, send_sems, recv_sems, row_of):
        self.me, self.ring, self.halves, self.gathered = me, ring, halves, gathered
        self.recv_pair, self.recv_1, self.recv_2, self.recv_3, self.total = recv_pair, recv_1, recv_2, recv_3, total
        self.send_sems, self.recv_sems, self.row_of = send_sems, recv_sems, row_of

    def axes(self, unit):
        def mask(shift):
            axis = lax.rem(unit + shift, 3)
            return 2 + axis + axis * axis

        (p1, b1), (p2, b2), (p3, b3) = (flip(self.me, mask(shift)) for shift in range(3))
        return (p1, p2, p3), (b1, b2, b3)

    def copy(self, unit, kind):
        (p1, p2, p3), (b1, b2, b3) = self.axes(unit)
        partner, half = flip(self.me, 1)

        def rows(start, size):
            return pl.ds(pl.multiple_of(start, 16), size)

        total = self.total.at[unit]
        row = self.row_of(unit, half)
        if kind == PAIR:
            src, dst, peer = self.halves.at[lax.rem(unit, self.ring)], self.recv_pair.at[unit], partner
        elif kind == RS1:
            src, dst, peer = total.at[rows((1 - b1) * 64, 64)], self.recv_1.at[unit], p1
        elif kind == RS2:
            src, dst, peer = total.at[rows(b1 * 64 + (1 - b2) * 32, 32)], self.recv_2.at[unit], p2
        elif kind == RS3:
            src, dst, peer = total.at[rows(b1 * 64 + b2 * 32 + (1 - b3) * 16, 16)], self.recv_3.at[unit], p3
        else:
            start, size, peer = {
                AG3: (b1 * 64 + b2 * 32 + b3 * 16, 16, p3),
                AG2: (b1 * 64 + b2 * 32, 32, p2),
                AG1: (b1 * 64, 64, p1),
                AGP: (0, 128, partner),
            }[kind]
            src = dst = self.gathered.at[rows(row + start, size)]
        return pltpu.make_async_remote_copy(src_ref=src, dst_ref=dst, send_sem=self.send_sems.at[unit, kind], recv_sem=self.recv_sems.at[unit, kind], device_id=(peer,), device_id_type=MESH_ID)

    def reduce_step(self, unit, kind):
        _, (b1, b2, b3) = self.axes(unit)
        self.copy(unit, kind).wait()
        if kind == PAIR:
            start, size, landed = 0, 128, self.recv_pair
        elif kind == RS1:
            start, size, landed = b1 * 64, 64, self.recv_1
        else:
            start, size, landed = b1 * 64 + b2 * 32, 32, self.recv_2
        keep = pl.ds(pl.multiple_of(start, 16), size)
        self.total[unit, keep] = self.total[unit, keep] + landed[unit]
        self.copy(unit, kind + 1).start()

    def owned(self, unit):
        _, (b1, b2, b3) = self.axes(unit)
        return b1 * 64 + b2 * 32 + b3 * 16


def enter(me):
    barrier = pltpu.get_barrier_semaphore()
    for mask in (1, 2, 4, 8):
        pl.semaphore_signal(barrier, inc=1, device_id=(flip(me, mask)[0],), device_id_type=MESH_ID)
    pl.semaphore_wait(barrier, 4)


def pipeline(units, lags, stages):
    def step(now, carry):
        for lag, stage in zip(lags, stages):
            unit = now - lag

            @pl.when((unit >= 0) & (unit < units))
            def _():
                stage(unit)

        return carry

    lax.fori_loop(0, units + max(lags), step, 0)


def product_unit(left_ref, right_ref, col_other, col_mine, halves, total, slot, unit, blocks):
    left = jnp.concatenate([left_ref[:, pl.ds(pl.multiple_of(col_other, UNIT), UNIT)], left_ref[:, pl.ds(pl.multiple_of(col_mine, UNIT), UNIT)]], axis=1)
    width = right_ref.shape[1] // blocks
    for block in range(blocks):
        cols = pl.ds(block * width, width)
        out = contract_rows(left, right_ref[:, cols])
        halves[slot, :, cols] = out[:UNIT]
        total[unit, :, cols] = out[UNIT:]


RING = 3
CORR_LAGS = (0, 1, 3, 5, 7, 8, 9, 10, 11)


def corr_kernel(row_count, off_ref, left_ref, right_ref, grad_ref, loss_ref, halves, recv_pair, recv_1, recv_2, recv_3, total, send_sems, recv_sems):
    me = lax.axis_index(DATA_AXIS)
    width = right_ref.shape[1]
    half_rows = left_ref.shape[1] // 2
    units = half_rows // UNIT
    _, half = flip(me, 1)
    enter(me)
    ex = Exchange(me, RING, halves, grad_ref, recv_pair, recv_1, recv_2, recv_3, total, send_sems, recv_sems, lambda unit, h: h * half_rows + unit * UNIT)
    loss_ref[...] = jnp.zeros_like(loss_ref)

    def produce(unit):
        @pl.when(unit >= RING)
        def _():
            ex.copy(unit - RING, PAIR).wait_send()

        product_unit(left_ref, right_ref, (1 - half) * half_rows + unit * UNIT, half * half_rows + unit * UNIT, halves, total, lax.rem(unit, RING), unit, 4)
        ex.copy(unit, PAIR).start()

    def pair_step(unit):
        ex.copy(unit, PAIR).wait_recv()
        total[unit] = total[unit] + recv_pair[unit]
        ex.copy(unit, RS1).start()

    def finish(unit):
        ex.copy(unit, RS3).wait()
        start = ex.owned(unit)
        keep = pl.ds(pl.multiple_of(start, 16), 16)
        corr = (total[unit, keep] + recv_3[unit]) * (1.0 / row_count)
        row = half * half_rows + unit * UNIT + start
        on_diag = lax.broadcasted_iota(jnp.int32, (16, width), 0) + row == lax.broadcasted_iota(jnp.int32, (16, width), 1)
        off_weight = off_ref[0, 0]
        miss = 1.0 - corr
        terms = jnp.where(on_diag, miss * miss, off_weight * (corr * corr))
        loss_ref[...] += terms[:8] + terms[8:]
        grad = jnp.where(on_diag, -2.0 * miss, 2.0 * off_weight * corr).astype(jnp.bfloat16)
        grad_ref[pl.ds(pl.multiple_of(row, 16), 16)] = grad
        ex.copy(unit, AG3).start()

    def forward(kind):
        def stage(unit):
            ex.copy(unit, kind).wait()
            if kind != AGP:
                ex.copy(unit, kind + 1).start()

        return stage

    pipeline(units, CORR_LAGS, [produce, pair_step, lambda u: ex.reduce_step(u, RS1), lambda u: ex.reduce_step(u, RS2), finish, forward(AG3), forward(AG2), forward(AG1), forward(AGP)])
    for unit in range(units - RING, units):
        ex.copy(unit, PAIR).wait_send()


def exchange_scratch(units, width):
    return [
        pltpu.VMEM((RING, UNIT, width), jnp.float32),
        pltpu.VMEM((units, UNIT, width), jnp.float32),
        pltpu.VMEM((units, 64, width), jnp.float32),
        pltpu.VMEM((units, 32, width), jnp.float32),
        pltpu.VMEM((units, 16, width), jnp.float32),
        pltpu.VMEM((units, UNIT, width), jnp.float32),
        pltpu.SemaphoreType.DMA((units, 9)),
        pltpu.SemaphoreType.DMA((units, 9)),
    ]


def corr_grad(emb_a, emb_b, off_weight, row_count):
    rows, width = emb_a.shape
    vmem = pl.BlockSpec(memory_space=pltpu.VMEM)
    return pl.pallas_call(
        functools.partial(corr_kernel, row_count),
        out_shape=(jax.ShapeDtypeStruct((width, width), jnp.bfloat16), jax.ShapeDtypeStruct((8, width), jnp.float32)),
        in_specs=[pl.BlockSpec(memory_space=pltpu.SMEM), vmem, vmem],
        out_specs=(vmem, vmem),
        scratch_shapes=exchange_scratch(width // 2 // UNIT, width),
        compiler_params=pltpu.CompilerParams(collective_id=2, has_side_effects=True, vmem_limit_bytes=VMEM_LIMIT),
        cost_estimate=pl.CostEstimate(flops=2 * rows * width * width, bytes_accessed=4 * width * width, transcendentals=0),
        name="corr_grad",
    )(off_weight.reshape(1, 1), emb_a, emb_b)


WEIGHT_LAGS = (0, 1, 3, 5, 7, 8, 9, 10, 11)


def weight_kernel(sizes, *refs):
    count = len(sizes)
    lefts, rights = refs[:count], refs[count : 2 * count]
    out_ref, halves, recv_pair, recv_1, recv_2, recv_3, total, send_sems, recv_sems = refs[2 * count :]
    me = lax.axis_index(DATA_AXIS)
    _, half = flip(me, 1)
    firsts, bases, units, base = [], [], 0, 0
    for size in sizes:
        firsts.append(units)
        bases.append(base)
        units += size // 2 // UNIT
        base += size
    enter(me)

    def row_of(unit, h):
        row = bases[0] + h * (sizes[0] // 2) + unit * UNIT
        for index in range(1, count):
            inside = lax.div(unit + units - firsts[index], units)
            inside = lax.min(inside, 1)
            row = row + inside * (bases[index] + h * (sizes[index] // 2) + (unit - firsts[index]) * UNIT - row)
        return row

    ex = Exchange(me, RING, halves, out_ref, recv_pair, recv_1, recv_2, recv_3, total, send_sems, recv_sems, row_of)

    def produce(unit):
        @pl.when(unit >= RING)
        def _():
            ex.copy(unit - RING, PAIR).wait_send()

        for index in range(count):
            last = firsts[index] + sizes[index] // 2 // UNIT

            @pl.when((unit >= firsts[index]) & (unit < last))
            def _():
                local = (unit - firsts[index]) * UNIT
                part = sizes[index] // 2
                product_unit(lefts[index], rights[index], (1 - half) * part + local, half * part + local, halves, total, lax.rem(unit, RING), unit, 4)

        ex.copy(unit, PAIR).start()

    def pair_step(unit):
        ex.copy(unit, PAIR).wait_recv()
        total[unit] = total[unit] + recv_pair[unit]
        ex.copy(unit, RS1).start()

    def to_out(unit):
        start = ex.owned(unit)
        return pltpu.make_async_copy(total.at[unit, pl.ds(pl.multiple_of(start, 16), 16)], out_ref.at[pl.ds(pl.multiple_of(row_of(unit, half) + start, 16), 16)], send_sems.at[unit, LOCAL])

    def finish(unit):
        ex.copy(unit, RS3).wait()
        keep = pl.ds(pl.multiple_of(ex.owned(unit), 16), 16)
        total[unit, keep] = total[unit, keep] + recv_3[unit]
        to_out(unit).start()
        to_out(unit).wait()
        ex.copy(unit, AG3).start()

    def forward(kind):
        def stage(unit):
            ex.copy(unit, kind).wait()
            if kind != AGP:
                ex.copy(unit, kind + 1).start()

        return stage

    pipeline(units, WEIGHT_LAGS, [produce, pair_step, lambda u: ex.reduce_step(u, RS1), lambda u: ex.reduce_step(u, RS2), finish, forward(AG3), forward(AG2), forward(AG1), forward(AGP)])
    for unit in range(units - RING, units):
        ex.copy(unit, PAIR).wait_send()


def weight_sums(lefts, rights, call_id):
    sizes = tuple(left.shape[1] for left in lefts)
    width = rights[0].shape[1]
    units = sum(size // 2 // UNIT for size in sizes)
    vmem = pl.BlockSpec(memory_space=pltpu.VMEM)
    return pl.pallas_call(
        functools.partial(weight_kernel, sizes),
        out_shape=jax.ShapeDtypeStruct((sum(sizes), width), jnp.float32),
        in_specs=[vmem] * (2 * len(sizes)),
        out_specs=pl.BlockSpec(memory_space=pl.ANY),
        scratch_shapes=exchange_scratch(units, width),
        compiler_params=pltpu.CompilerParams(collective_id=call_id, has_side_effects=True, vmem_limit_bytes=VMEM_LIMIT),
        cost_estimate=pl.CostEstimate(flops=2 * lefts[0].shape[0] * sum(sizes) * width, bytes_accessed=8 * sum(sizes) * width, transcendentals=0),
        name=f"weight_sums_{call_id}",
    )(*lefts, *rights)


def solution(mesh):
    shards = mesh.shape[DATA_AXIS]
    row_part = P(DATA_AXIS, None)
    replicated = P()

    def local_step(feat_a, feat_b, w_in, w_mid, w_out, t_in, t_mid, t_out, gain_1, bias_1, gain_2, bias_2, off_weight):
        row_count = feat_a.shape[0] * shards

        def norm_pair(pre_a, pre_b):
            stat_means = stats_all_reduce([jnp.sum(pre_a, axis=0), jnp.sum(pre_a * pre_a, axis=0), jnp.sum(pre_b, axis=0), jnp.sum(pre_b * pre_b, axis=0)], shards) / row_count
            inv_a = lax.rsqrt(stat_means[1] - stat_means[0] * stat_means[0] + NORM_EPS)
            inv_b = lax.rsqrt(stat_means[3] - stat_means[2] * stat_means[2] + NORM_EPS)
            return (pre_a - stat_means[0]) * inv_a, inv_a, (pre_b - stat_means[2]) * inv_b

        def hidden_pair(in_a, in_b, weight_a, weight_b, gain_vec, bias_vec):
            normed_a, inv_a, normed_b = norm_pair(jnp.dot(in_a, weight_a, preferred_element_type=jnp.float32), jnp.dot(in_b, weight_b, preferred_element_type=jnp.float32))
            pre_act = normed_a * gain_vec + bias_vec
            act_a = jnp.maximum(pre_act, 0.0).astype(jnp.bfloat16)
            act_b = jnp.maximum(normed_b * gain_vec + bias_vec, 0.0).astype(jnp.bfloat16)
            return act_a, act_b, normed_a, inv_a, pre_act > 0.0

        def affine_back(grad_pre, normed, inv_std, gain_vec):
            stat_sums = stats_all_reduce([jnp.sum(grad_pre * normed, axis=0), jnp.sum(grad_pre, axis=0)], shards)
            grad_u = (grad_pre - stat_sums[1] / row_count - normed * (stat_sums[0] / row_count)) * (gain_vec * inv_std)
            return grad_u.astype(jnp.bfloat16), stat_sums[0], stat_sums[1]

        act_1, teach_1, normed_1, inv_1, mask_1 = hidden_pair(feat_a, feat_b, w_in, t_in, gain_1, bias_1)
        act_2, teach_2, normed_2, inv_2, mask_2 = hidden_pair(act_1, teach_1, w_mid, t_mid, gain_2, bias_2)
        zh_a, inv_z, zh_b = norm_pair(jnp.dot(act_2, w_out, preferred_element_type=jnp.float32), jnp.dot(teach_2, t_out, preferred_element_type=jnp.float32))
        emb_a = zh_a.astype(jnp.bfloat16)
        emb_b = zh_b.astype(jnp.bfloat16)
        grad_c, loss_part = corr_grad(emb_a, emb_b, off_weight, row_count)
        grad_emb = contract_cols(emb_b, grad_c) / row_count
        stat_sums = stats_all_reduce([jnp.sum(grad_emb, axis=0), jnp.sum(grad_emb * zh_a, axis=0), jnp.sum(loss_part, axis=0)], shards)
        loss_value = jnp.sum(stat_sums[2])
        grad_z = ((grad_emb - stat_sums[0] / row_count - zh_a * (stat_sums[1] / row_count)) * inv_z).astype(jnp.bfloat16)
        grad_pre_2 = jnp.where(mask_2, contract_cols(grad_z, w_out), 0.0)
        grad_u_2, grad_gain_2, grad_bias_2 = affine_back(grad_pre_2, normed_2, inv_2, gain_2)
        grad_pre_1 = jnp.where(mask_1, contract_cols(grad_u_2, w_mid), 0.0)
        grad_u_1, grad_gain_1, grad_bias_1 = affine_back(grad_pre_1, normed_1, inv_1, gain_1)
        sums_out = weight_sums([act_2], [grad_z], 3)
        sums_rest = weight_sums([act_1, feat_a], [grad_u_2, grad_u_1], 4)
        width = w_mid.shape[0]
        return (loss_value, grad_emb, sums_rest[width:], sums_rest[:width], sums_out, grad_gain_1, grad_bias_1, grad_gain_2, grad_bias_2)

    return jax.shard_map(local_step, mesh=mesh, in_specs=(row_part, row_part) + (replicated,) * 11, out_specs=(replicated, row_part) + (replicated,) * 7, check_vma=False)
```

time: 970 us -> 707 us (0.73)
  waiting for transfers between devices: 522 us -> 0 us
  Pallas kernels: 0 us -> 495 us
  blocking collectives: 199 us -> 0 us
  matrix products: 174 us -> 122 us
  other arithmetic: 24.8 us -> 51.7 us
  between operations: 15.4 us -> 2.03 us
    psum x2 -> x0, waiting for transfers between devices: 522 us -> none  [the longest x1 342 us: local_step(): weight_grads = lax.psum((grad_w_in, grad_w_mid, grad_w_out), DATA_AXIS)]
    pallas_call x0 -> x9, Pallas kernels: none -> 495 us  [the longest x2 312 us: weight_sums(): pl.pallas_call(functools.partial(weight_kernel, sizes), out_shape=jax.Sha...]
    psum x6 -> x0, blocking collectives: 199 us -> none  [the longest x3 102 us: norm_pair(): stat_means = lax.psum(stat_sums, DATA_AXIS) / row_count]
    dot_general x4 -> x0, matrix products: 52.1 us -> none  [contract_rows(): lax.dot_general(left_op, right_op, (((0,), (0,)), ((), ())), preferred_el...]
    convert_element_type x1 -> x4, other arithmetic: 7.21 us -> 26.5 us  [the longest x2 10.2 us: hidden_pair(): act_a = jnp.maximum(pre_act, 0.0).astype(jnp.bfloat16)]
    unnamed x35 -> x33, local copies, waits for them, and re-layouts: 29.6 us -> 11.9 us
    slice x1 -> x2, local copies, waits for them, and re-layouts: 0.01 us -> 16.5 us  [the longest x1 11.8 us: local_step(): sums_rest[:width]]
  transfers between devices with their start and end apart: 2 -> 0, of which waited for: 2 -> 0; matrix products, arithmetic and copies ran while one was open for 1% -> 0% of each run, Pallas kernels for 0% -> 0%
where the time goes in v1:
time: 707 us; the launch traced here: 702 us
  Pallas kernels  495 us (70%)
  matrix products  122 us (17%)
  other arithmetic  51.7 us (7%)
  local copies, waits for them, and re-layouts  31.2 us (4%)
    pallas_call x2, Pallas kernels, weight_sums(): pl.pallas_call(functools.partial(weight_kernel, sizes), out_shape=jax.Sha...  312 us
    pallas_call x1, Pallas kernels, corr_grad(): pl.pallas_call(functools.partial(corr_kernel, row_count), out_shape=(jax....  112 us
    pallas_call x6, Pallas kernels, stats_all_reduce(): pl.pallas_call(functools.partial(stats_kernel, shards), out_shape=jax.Sha...  70.5 us
    dot_general x3, matrix products, contract_cols(): lax.dot_general(left_op, right_op, (((1,), (1,)), ((), ())), preferred_el...  51.1 us
    dot_general x2, matrix products, hidden_pair(): jnp.dot(in_a, weight_a, preferred_element_type=jnp.float32)  23.3 us
    dot_general x2, matrix products, hidden_pair(): jnp.dot(in_b, weight_b, preferred_element_type=jnp.float32)  19.2 us
    convert_element_type x2, other arithmetic, affine_back(): return (grad_u.astype(jnp.bfloat16), stat_sums[0], stat_sums[1])  15.9 us
    dot_general x1, matrix products, local_step(): jnp.dot(act_2, w_out, preferred_element_type=jnp.float32)  15 us

profile of v1, /device:TPU:0, one launch (start us, length us, event | category | flops | bytes accessed | tf_op | source)
XLA Modules:
  0.0 701.7 jit_solution(2818178543154700455)
XLA Ops:
  0.7 7.8 %multiply_reduce_fusion.8 = (f32[2048]{0:T(1024)S(1)}, f32[2048]{0:T(1024)S(1)}, f32[1024,2048]{1,0:T(8,128)}) fusion(bf16[1024,512]{1,0:T(8,128)(2,1)} %refs_1_.1, bf16[512,2048]{1,0:T(8,128)(2,1)} %param.15), kind=kOutput, calls=%fused_computation.21 | convolution fusion | flops 2153771008 | bytes 11550720 | tf_op jit(solution)/shard_map/dot_general | solution.py:362
  8.5 5.7 multiply_reduce_fusion.7
  14.2 0.7 stack.79.x_ref
  14.9 14.5 %stats_all_reduce.6 = f32[8,2048]{1,0:T(8,128)} custom-call(f32[8,2048]{1,0:T(8,128)} %stack.79.x_ref), custom_call_target="tpu_custom_call" | custom-call | tf_op jit(solution)/shard_map/stats_all_reduce/pallas_call | solution.py:70
  29.5 0.8 broadcast_multiply_fusion.2
  30.3 0.6 fusion.25
  30.9 5.1 maximum_convert_fusion.2.refs_0_
  36.0 0.0 slice-start.1
  36.1 15.5 %multiply_reduce_fusion.6 = (f32[2048]{0:T(1024)S(1)}, f32[2048]{0:T(1024)S(1)}, f32[1024,2048]{1,0:T(8,128)}) fusion(bf16[1024,2048]{1,0:T(8,128)(2,1)S(1)} %maximum_convert_fusion.2.refs_0_, bf16[2048,2048]{1,0:T(8,128)(2,1)} %param.16), kind=kOutput, calls=%fused_computation.15 | convolution fusion | flops 8596221952 | bytes 20987904 | tf_op jit(solution)/shard_map/dot_general | solution.py:362
  51.6 0.0 copy-start.5
  51.6 0.0 copy-start.8
  51.6 13.4 %multiply_reduce_fusion.5 = (f32[2048]{0:T(1024)S(1)}, f32[2048]{0:T(1024)S(1)}, f32[1024,2048]{1,0:T(8,128)}) fusion(bf16[2048,2048]{1,0:T(8,128)(2,1)S(1)} %bitcast.119, f32[1024,2048]{1,0:T(8,128)} %get-tuple-element.57, f32[2048]{0:T(1024)S(1)} %copy-done.9, f32[2048]{0:T(1024)S(1)} %copy-done.6, f32[2048]{0:T(1024)S(1)} %bitcast.96, f32[2048]{0:T(1024)S(1)} %bitcast.97), kind=kOutput, calls=%fused_computation.14 | convolution fusion | flops 8608804864 | bytes 25214976 | tf_op jit(solution)/shard_map/dot_general | solution.py:362
  65.0 0.7 stack.84.x_ref
  65.7 10.3 %stats_all_reduce.7 = f32[8,2048]{1,0:T(8,128)} custom-call(f32[8,2048]{1,0:T(8,128)} %stack.84.x_ref), custom_call_target="tpu_custom_call" | custom-call | tf_op jit(solution)/shard_map/stats_all_reduce/pallas_call | solution.py:70
  76.0 0.8 broadcast_multiply_fusion.1
  77.0 0.0 slice-start.2
  77.0 5.1 maximum_convert_fusion.refs_0_
  82.1 0.0 slice-start.3
  82.1 15.0 %multiply_reduce_fusion.4 = (f32[2048]{0:T(1024)S(1)}, f32[2048]{0:T(1024)S(1)}, f32[1024,2048]{1,0:T(8,128)}) fusion(bf16[1024,2048]{1,0:T(8,128)(2,1)S(1)} %maximum_convert_fusion.refs_0_, bf16[2048,2048]{1,0:T(8,128)(2,1)} %param.17), kind=kOutput, calls=%fused_computation.9 | convolution fusion | flops 8596221952 | bytes 20987904 | tf_op jit(solution)/shard_map/dot_general | solution.py:375
  97.1 13.5 %multiply_reduce_fusion.3 = (f32[2048]{0:T(1024)S(1)}, f32[2048]{0:T(1024)S(1)}, f32[1024,2048]{1,0:T(8,128)}) fusion(bf16[2048,2048]{1,0:T(8,128)(2,1)S(1)} %bitcast.121, f32[1024,2048]{1,0:T(8,128)} %get-tuple-element.59, f32[2048]{0:T(1024)S(1)} %copy-done.8, f32[2048]{0:T(1024)S(1)} %copy-done.5, f32[2048]{0:T(1024)S(1)} %bitcast.98, f32[2048]{0:T(1024)S(1)} %bitcast.99), kind=kOutput, calls=%fused_computation.8 | convolution fusion | flops 8608804864 | bytes 25214976 | tf_op jit(solution)/shard_map/dot_general | solution.py:375
  110.6 0.7 stack.89.x_ref
  111.3 12.2 %stats_all_reduce.8 = f32[8,2048]{1,0:T(8,128)} custom-call(f32[8,2048]{1,0:T(8,128)} %stack.89.x_ref), custom_call_target="tpu_custom_call" | custom-call | tf_op jit(solution)/shard_map/stats_all_reduce/pallas_call | solution.py:70
  123.5 0.8 broadcast_multiply_fusion
  124.4 9.3 %multiply_convert_fusion.3 = (bf16[1024,2048]{1,0:T(8,128)(2,1)}, bf16[1024,2048]{1,0:T(8,128)(2,1)}) fusion(f32[1024,2048]{1,0:T(8,128)} %get-tuple-element.61, f32[2048]{0:T(1024)S(1)} %bitcast.87, f32[2048]{0:T(1024)S(1)} %bitcast.88, f32[2048]{0:T(1024)S(1)} %bitcast.72, f32[1024,2048]{1,0:T(8,128)} %get-tuple-element.60, f32[2048]{0:T(1024)S(1)} %bitcast.69), kind=kLoop, calls=%fused_computation.7 | loop fusion | flops 12582912 | bytes 25198592 | tf_op jit(solution)/shard_map/convert_element_type | solution.py:377
  134.4 111.9 %corr_grad.1 = (bf16[2048,2048]{1,0:T(8,128)(2,1)}, f32[8,2048]{1,0:T(8,128)}) custom-call(f32[1,1]{1,0:T(1,128)} %bitcast.60.off_ref, bf16[1024,2048]{1,0:T(8,128)(2,1)} %get-tuple-element.66.left_ref, bf16[1024,2048]{1,0:T(8,128)(2,1)} %get-tuple-element.65.right_ref), custom_call_target="tpu_custom_call" | custom-call | flops 8589934592 | bytes 16777216 | tf_op jit(solution)/shard_map/corr_grad/pallas_call | solution.py:245
  246.3 16.4 %multiply_reduce_fusion.2 = (f32[2048]{0:T(1024)S(1)}, f32[2048]{0:T(1024)S(1)}, f32[1024,2048]{1,0:T(8,128)}) fusion(f32[1024,2048]{1,0:T(8,128)} %get-tuple-element.60, f32[2048]{0:T(1024)S(1)} %bitcast.73, f32[2048]{0:T(1024)S(1)} %bitcast.70, bf16[1024,2048]{1,0:T(8,128)(2,1)} %get-tuple-element.65.right_ref, bf16[2048,2048]{1,0:T(8,128)(2,1)} %get-tuple-element.11), kind=kOutput, calls=%fused_computation.5 | convolution fusion | flops 8602513408 | bytes 29392896 | tf_op jit(solution)/shard_map/dot_general | solution.py:22
  262.7 0.7 stack.93.x_ref
  263.4 11.0 %stats_all_reduce.9 = f32[8,2048]{1,0:T(8,128)} custom-call(f32[8,2048]{1,0:T(8,128)} %stack.93.x_ref), custom_call_target="tpu_custom_call" | custom-call | tf_op jit(solution)/shard_map/stats_all_reduce/pallas_call | solution.py:70
  274.4 1.6 slice_multiply_fusion.1
  276.0 7.1 %multiply_convert_fusion.2.refs_1_ = bf16[1024,2048]{1,0:T(8,128)(2,1)S(1)} fusion(f32[1024,2048]{1,0:T(8,128)} %get-tuple-element.77, f32[1024,2048]{1,0:T(8,128)} %get-tuple-element.60, f32[2048]{0:T(1024)S(1)} %bitcast.82, f32[2048]{0:T(1024)S(1)} %bitcast.81, f32[2048]{0:T(1024)S(1)} %bitcast.74, f32[2048]{0:T(1024)S(1)} %bitcast.71), kind=kLoop, calls=%fused_computation.4 | loop fusion | flops 14680064 | bytes 21004288 | tf_op jit(solution)/shard_map/convert_element_type | solution.py:382
  283.1 17.3 %multiply_reduce_fusion.1 = (f32[2048]{0:T(1024)S(1)}, f32[2048]{0:T(1024)S(1)}, f32[1024,2048]{1,0:T(8,128)}) fusion(f32[1024,2048]{1,0:T(8,128)} %get-tuple-element.58, f32[2048]{0:T(1024)S(1)} %bitcast.79, f32[2048]{0:T(1024)S(1)} %bitcast.66, bf16[1024,2048]{1,0:T(8,128)(2,1)S(1)} %multiply_convert_fusion.2.refs_1_, bf16[2048,2048]{1,0:T(8,128)(2,1)} %param.17, ...), kind=kOutput, calls=%fused_computation.3 | convolution fusion | flops 8608804864 | bytes 29409280 | tf_op jit(solution)/shard_map/dot_general | solution.py:22
  300.4 0.1 pad.6.clone
  300.5 0.7 pad_maximum_fusion.1.x_ref
  301.2 11.5 %stats_all_reduce.10 = f32[8,2048]{1,0:T(8,128)} custom-call(f32[8,2048]{1,0:T(8,128)} %pad_maximum_fusion.1.x_ref), custom_call_target="tpu_custom_call" | custom-call | tf_op jit(solution)/shard_map/stats_all_reduce/pallas_call | solution.py:70
  312.7 1.5 fusion.23
  314.3 7.1 %multiply_convert_fusion.1.refs_2_ = bf16[1024,2048]{1,0:T(8,128)(2,1)S(1)} fusion(f32[1024,2048]{1,0:T(8,128)} %get-tuple-element.63, f32[1024,2048]{1,0:T(8,128)} %get-tuple-element.58, f32[2048]{0:T(1024)S(1)} %rsqrt_multiply_fusion.1, f32[2048]{0:T(1024)S(1)} %bitcast.84, f32[2048]{0:T(1024)S(1)} %bitcast.83, f32[2048]{0:T(1024)S(1)} %bitcast.80, ...), kind=kLoop, calls=%fused_computation.2 | loop fusion | flops 14680064 | bytes 21012480 | tf_op jit(solution)/shard_map/convert_element_type | solution.py:371
  321.3 0.0 copy-start.3
  321.4 0.0 copy-start.7
  321.4 17.4 %multiply_reduce_fusion = (f32[2048]{0:T(1024)S(1)}, f32[2048]{0:T(1024)S(1)}, f32[1024,2048]{1,0:T(8,128)}) fusion(f32[1024,2048]{1,0:T(8,128)} %get-tuple-element.56, f32[2048]{0:T(1024)S(1)} %bitcast.76, f32[2048]{0:T(1024)S(1)} %bitcast.62, bf16[1024,2048]{1,0:T(8,128)(2,1)S(1)} %multiply_convert_fusion.1.refs_2_, bf16[2048,2048]{1,0:T(8,128)(2,1)} %param.16, ...), kind=kOutput, calls=%fused_computation.1 | convolution fusion | flops 8608804864 | bytes 29409280 | tf_op jit(solution)/shard_map/dot_general | solution.py:22
  338.7 0.7 pad_maximum_fusion.x_ref
  339.4 11.0 %stats_all_reduce.11 = f32[8,2048]{1,0:T(8,128)} custom-call(f32[8,2048]{1,0:T(8,128)} %pad_maximum_fusion.x_ref), custom_call_target="tpu_custom_call" | custom-call | tf_op jit(solution)/shard_map/stats_all_reduce/pallas_call | solution.py:70
  350.4 1.5 fusion.24
  352.0 8.8 %multiply_convert_fusion.refs_3_ = bf16[1024,2048]{1,0:T(8,128)(2,1)} fusion(f32[1024,2048]{1,0:T(8,128)} %get-tuple-element.64, f32[1024,2048]{1,0:T(8,128)} %get-tuple-element.56, f32[2048]{0:T(1024)S(1)} %rsqrt_multiply_fusion, f32[2048]{0:T(1024)S(1)} %bitcast.86, f32[2048]{0:T(1024)S(1)} %bitcast.85, f32[2048]{0:T(1024)S(1)} %bitcast.77, f32[2048]{0:T(1024)S(1)} %bitcast.64), kind=kLoop, calls=%fused_computation | loop fusion | flops 14680064 | bytes 21012480 | tf_op jit(solution)/shard_map/convert_element_type | solution.py:371
  360.7 170.0 %weight_sums_4.1 = f32[2560,2048]{1,0:T(8,128)} custom-call(bf16[1024,2048]{1,0:T(8,128)(2,1)} %copy-done, bf16[1024,512]{1,0:T(8,128)(2,1)} %refs_1_.1, bf16[1024,2048]{1,0:T(8,128)(2,1)} %copy-done.3, bf16[1024,2048]{1,0:T(8,128)(2,1)} %multiply_convert_fusion.refs_3_), custom_call_target="tpu_custom_call" | custom-call | flops 10737418240 | bytes 41943040 | tf_op jit(solution)/shard_map/weight_sums_4/pallas_call | solution.py:335
  530.8 4.7 slice.98
  535.5 11.8 %slice.99 = f32[2048,2048]{1,0:T(8,128)} slice(f32[2560,2048]{1,0:T(8,128)} %weight_sums_4.1), slice={[0:2048], [0:2048]} | slice | bytes 33554432 | tf_op jit(solution)/shard_map/slice | solution.py:390
  547.3 142.2 %weight_sums_3.1 = f32[2048,2048]{1,0:T(8,128)} custom-call(bf16[1024,2048]{1,0:T(8,128)(2,1)} %copy-done.1, bf16[1024,2048]{1,0:T(8,128)(2,1)} %copy-done.2), custom_call_target="tpu_custom_call" | custom-call | flops 8589934592 | bytes 33554432 | tf_op jit(solution)/shard_map/weight_sums_3/pallas_call | solution.py:335
  689.4 11.8 %copy.24 = f32[2048,2048]{1,0:T(8,128)} copy(f32[2048,2048]{1,0:T(8,128)} %weight_sums_3.1) | data formatting | bytes 33554432
  (35 shorter events, 0.2 us)
Async XLA Ops:
  0.6 7.8 %copy-start.11 = (bf16[1024,512]{1,0:T(8,128)(2,1)S(1)}, bf16[1024,512]{1,0:T(8,128)(2,1)}, u32[]{:S(2)}) copy-start(bf16[1024,512]{1,0:T(8,128)(2,1)} %param.14) | copy-start | bytes 3145732
  0.7 7.8 %copy-start.10 = (bf16[512,2048]{1,0:T(8,128)(2,1)S(1)}, bf16[512,2048]{1,0:T(8,128)(2,1)}, u32[]{:S(2)}) copy-start(bf16[512,2048]{1,0:T(8,128)(2,1)} %param.18) | copy-start | bytes 6291460
  8.5 22.5 %copy-start.6 = (f32[2048]{0:T(1024)S(1)}, f32[2048]{0:T(1024)}, u32[]{:S(2)}) copy-start(f32[2048]{0:T(1024)} %param.21) | copy-start | bytes 24580
  8.5 22.5 %copy-start.9 = (f32[2048]{0:T(1024)S(1)}, f32[2048]{0:T(1024)}, u32[]{:S(2)}) copy-start(f32[2048]{0:T(1024)} %param.22) | copy-start | bytes 24580
  30.9 20.6 %slice-start = ((s8[8388608]{0:T(1024)(128)(4,1)}), s8[4194304]{0:T(1024)(128)(4,1)S(1)}, s32[]{:S(2)}) async-start(s8[8388608]{0:T(1024)(128)(4,1)} %bitcast.118), calls=%async_computation | async-start | bytes 8388608
  36.0 15.5 %copy-start = (bf16[1024,2048]{1,0:T(8,128)(2,1)}, bf16[1024,2048]{1,0:T(8,128)(2,1)S(1)}, u32[]{:S(2)}) copy-start(bf16[1024,2048]{1,0:T(8,128)(2,1)S(1)} %maximum_convert_fusion.2.refs_0_) | copy-start | bytes 12582916
  36.0 15.5 %slice-start.1 = ((s8[8388608]{0:T(1024)(128)(4,1)}), s8[4194304]{0:T(1024)(128)(4,1)S(1)}, s32[]{:S(2)}) async-start(s8[8388608]{0:T(1024)(128)(4,1)} %bitcast.118), calls=%async_computation.1 | async-start | bytes 8388608
  51.6 25.4 %copy-start.5 = (f32[2048]{0:T(1024)S(1)}, f32[2048]{0:T(1024)}, u32[]{:S(2)}) copy-start(f32[2048]{0:T(1024)} %param.23) | copy-start | bytes 24580
  51.6 25.4 %copy-start.8 = (f32[2048]{0:T(1024)S(1)}, f32[2048]{0:T(1024)}, u32[]{:S(2)}) copy-start(f32[2048]{0:T(1024)} %param.24) | copy-start | bytes 24580
  77.0 20.1 %slice-start.2 = ((s8[8388608]{0:T(1024)(128)(4,1)}), s8[4194304]{0:T(1024)(128)(4,1)S(1)}, s32[]{:S(2)}) async-start(s8[8388608]{0:T(1024)(128)(4,1)} %bitcast.120), calls=%async_computation.2 | async-start | bytes 8388608
  82.1 15.0 %copy-start.1 = (bf16[1024,2048]{1,0:T(8,128)(2,1)}, bf16[1024,2048]{1,0:T(8,128)(2,1)S(1)}, u32[]{:S(2)}) copy-start(bf16[1024,2048]{1,0:T(8,128)(2,1)S(1)} %maximum_convert_fusion.refs_0_) | copy-start | bytes 12582916
  82.1 15.0 %slice-start.3 = ((s8[8388608]{0:T(1024)(128)(4,1)}), s8[4194304]{0:T(1024)(128)(4,1)S(1)}, s32[]{:S(2)}) async-start(s8[8388608]{0:T(1024)(128)(4,1)} %bitcast.120), calls=%async_computation.3 | async-start | bytes 8388608
  246.3 16.4 %copy-start.4 = (f32[8,2048]{1,0:T(8,128)S(1)}, f32[8,2048]{1,0:T(8,128)}, u32[]{:S(2)}) copy-start(f32[8,2048]{1,0:T(8,128)} %get-tuple-element.12) | copy-start | bytes 196612
  283.1 17.3 %copy-start.2 = (bf16[1024,2048]{1,0:T(8,128)(2,1)}, bf16[1024,2048]{1,0:T(8,128)(2,1)S(1)}, u32[]{:S(2)}) copy-start(bf16[1024,2048]{1,0:T(8,128)(2,1)S(1)} %multiply_convert_fusion.2.refs_1_) | copy-start | bytes 12582916
  321.3 17.4 %copy-start.3 = (bf16[1024,2048]{1,0:T(8,128)(2,1)}, bf16[1024,2048]{1,0:T(8,128)(2,1)S(1)}, u32[]{:S(2)}) copy-start(bf16[1024,2048]{1,0:T(8,128)(2,1)S(1)} %multiply_convert_fusion.1.refs_2_) | copy-start | bytes 12582916
  321.4 17.4 %copy-start.7 = (f32[1,2048]{1,0:T(1,128)S(1)}, f32[1,2048]{1,0:T(1,128)}, u32[]{:S(2)}) copy-start(f32[1,2048]{1,0:T(1,128)} %get-tuple-element.39) | copy-start | bytes 24580

commit v2 on v1

--- a/solution.py
+++ b/solution.py
@@ -82,7 +82,8 @@
 
 
 class Exchange:
-    def __init__(self, me, ring, halves, gathered, recv_pair, recv_1, recv_2, recv_3, total, send_sems, recv_sems, row_of):
+    def __init__(self, me, ring, halves, gathered, recv_pair, recv_1, recv_2, recv_3, total, send_sems, recv_sems, row_of, depth, send_total=False):
+        self.depth, self.send_total = depth, send_total
         self.me, self.ring, self.halves, self.gathered = me, ring, halves, gathered
         self.recv_pair, self.recv_1, self.recv_2, self.recv_3, self.total = recv_pair, recv_1, recv_2, recv_3, total
         self.send_sems, self.recv_sems, self.row_of = send_sems, recv_sems, row_of
@@ -102,16 +103,17 @@
         def rows(start, size):
             return pl.ds(pl.multiple_of(start, 16), size)
 
-        total = self.total.at[unit]
+        slot = lax.rem(unit, self.depth)
+        total = self.total.at[slot]
         row = self.row_of(unit, half)
         if kind == PAIR:
-            src, dst, peer = self.halves.at[lax.rem(unit, self.ring)], self.recv_pair.at[unit], partner
+            src, dst, peer = self.halves.at[lax.rem(unit, self.ring)], self.recv_pair.at[slot], partner
         elif kind == RS1:
-            src, dst, peer = total.at[rows((1 - b1) * 64, 64)], self.recv_1.at[unit], p1
+            src, dst, peer = total.at[rows((1 - b1) * 64, 64)], self.recv_1.at[slot], p1
         elif kind == RS2:
-            src, dst, peer = total.at[rows(b1 * 64 + (1 - b2) * 32, 32)], self.recv_2.at[unit], p2
+            src, dst, peer = total.at[rows(b1 * 64 + (1 - b2) * 32, 32)], self.recv_2.at[slot], p2
         elif kind == RS3:
-            src, dst, peer = total.at[rows(b1 * 64 + b2 * 32 + (1 - b3) * 16, 16)], self.recv_3.at[unit], p3
+            src, dst, peer = total.at[rows(b1 * 64 + b2 * 32 + (1 - b3) * 16, 16)], self.recv_3.at[slot], p3
         else:
             start, size, peer = {
                 AG3: (b1 * 64 + b2 * 32 + b3 * 16, 16, p3),
@@ -120,7 +122,9 @@
                 AGP: (0, 128, partner),
             }[kind]
             src = dst = self.gathered.at[rows(row + start, size)]
-        return pltpu.make_async_remote_copy(src_ref=src, dst_ref=dst, send_sem=self.send_sems.at[unit, kind], recv_sem=self.recv_sems.at[unit, kind], device_id=(peer,), device_id_type=MESH_ID)
+            if kind == AG3 and self.send_total:
+                src = total.at[rows(start, size)]
+        return pltpu.make_async_remote_copy(src_ref=src, dst_ref=dst, send_sem=self.send_sems.at[slot, kind], recv_sem=self.recv_sems.at[slot, kind], device_id=(peer,), device_id_type=MESH_ID)
 
     def reduce_step(self, unit, kind):
         _, (b1, b2, b3) = self.axes(unit)
@@ -132,7 +136,8 @@
         else:
             start, size, landed = b1 * 64 + b2 * 32, 32, self.recv_2
         keep = pl.ds(pl.multiple_of(start, 16), size)
-        self.total[unit, keep] = self.total[unit, keep] + landed[unit]
+        slot = lax.rem(unit, self.depth)
+        self.total[slot, keep] = self.total[slot, keep] + landed[slot]
         self.copy(unit, kind + 1).start()
 
     def owned(self, unit):
@@ -172,7 +177,7 @@
 
 
 RING = 3
-CORR_LAGS = (0, 1, 3, 5, 7, 8, 9, 10, 11)
+CORR_LAGS = (0, 1, 4, 6, 8, 10, 13, 17, 19)
 
 
 def corr_kernel(row_count, off_ref, left_ref, right_ref, grad_ref, loss_ref, halves, recv_pair, recv_1, recv_2, recv_3, total, send_sems, recv_sems):
@@ -182,7 +187,7 @@
     units = half_rows // UNIT
     _, half = flip(me, 1)
     enter(me)
-    ex = Exchange(me, RING, halves, grad_ref, recv_pair, recv_1, recv_2, recv_3, total, send_sems, recv_sems, lambda unit, h: h * half_rows + unit * UNIT)
+    ex = Exchange(me, RING, halves, grad_ref, recv_pair, recv_1, recv_2, recv_3, total, send_sems, recv_sems, lambda unit, h: h * half_rows + unit * UNIT, units)
     loss_ref[...] = jnp.zeros_like(loss_ref)
 
     def produce(unit):
@@ -254,94 +259,263 @@
     )(off_weight.reshape(1, 1), emb_a, emb_b)
 
 
-WEIGHT_LAGS = (0, 1, 3, 5, 7, 8, 9, 10, 11)
-
-
-def weight_kernel(sizes, *refs):
-    count = len(sizes)
-    lefts, rights = refs[:count], refs[count : 2 * count]
-    out_ref, halves, recv_pair, recv_1, recv_2, recv_3, total, send_sems, recv_sems = refs[2 * count :]
+DEPTH = 12
+PERIOD = 12
+BLOCK = 256
+BACK_LAGS = (1, 4, 6, 7, 9, 12, 15, 16)
+
+
+def backward_kernel(shards, row_count, left_2, grad_z, w_out, normed_2, left_1, w_mid, normed_1, feat, vecs, out_ref, stat_ref, left, feat_in, grad, weight, normed, deriv, halves, mine, total, recv_1, recv_2, recv_3, stat_part, stat_in, send_sems, recv_sems, load_sems, weight_sems, normed_sems, stat_sems):
     me = lax.axis_index(DATA_AXIS)
     _, half = flip(me, 1)
-    firsts, bases, units, base = [], [], 0, 0
-    for size in sizes:
-        firsts.append(units)
-        bases.append(base)
-        units += size // 2 // UNIT
-        base += size
-    enter(me)
+    rows, width = left.shape
+    blocks = width // BLOCK
+    units_full = width // 2 // UNIT
+    units_last = feat_in.shape[1] // 2 // UNIT
+    enters = 2 * PERIOD + units_last
+    ticks = enters + max(BACK_LAGS)
+
+    load_left = pltpu.make_async_copy(left_2, left, load_sems.at[0])
+    load_grad = pltpu.make_async_copy(grad_z, grad, load_sems.at[1])
+    load_feat = pltpu.make_async_copy(feat, feat_in, load_sems.at[2])
+
+    def block_of(index):
+        return pl.ds(pl.multiple_of(index * BLOCK, BLOCK), BLOCK)
+
+    def load_weight(source, index):
+        return pltpu.make_async_copy(source.at[block_of(index)], weight.at[block_of(index)], weight_sems.at[index])
+
+    def load_normed(source, index):
+        return pltpu.make_async_copy(source.at[:, block_of(index)], normed.at[:, block_of(index)], normed_sems.at[index])
+
+    load_left.start()
+    load_grad.start()
+    for index in range(blocks):
+        load_weight(w_out, index).start()
+        load_normed(normed_2, index).start()
+    load_feat.start()
+
+    barrier = pltpu.get_barrier_semaphore()
+    for shift in range(1, shards):
+        pl.semaphore_signal(barrier, inc=1, device_id=(lax.rem(me + shift, shards),), device_id_type=MESH_ID)
+    pl.semaphore_wait(barrier, shards - 1)
 
     def row_of(unit, h):
-        row = bases[0] + h * (sizes[0] // 2) + unit * UNIT
-        for index in range(1, count):
-            inside = lax.div(unit + units - firsts[index], units)
-            inside = lax.min(inside, 1)
-            row = row + inside * (bases[index] + h * (sizes[index] // 2) + (unit - firsts[index]) * UNIT - row)
-        return row
-
-    ex = Exchange(me, RING, halves, out_ref, recv_pair, recv_1, recv_2, recv_3, total, send_sems, recv_sems, row_of)
-
-    def produce(unit):
-        @pl.when(unit >= RING)
+        layer = lax.div(unit, units_full)
+        part = width // 2 - (width // 2 - feat_in.shape[1] // 2) * lax.div(layer, 2)
+        return layer * width + h * part + lax.rem(unit, units_full) * UNIT
+
+    ex = Exchange(me, 2, halves, out_ref, total, recv_1, recv_2, recv_3, total, send_sems, recv_sems, row_of, DEPTH, send_total=True)
+
+    def produce(unit, source, part):
+        @pl.when(unit >= 2)
         def _():
-            ex.copy(unit - RING, PAIR).wait_send()
-
-        for index in range(count):
-            last = firsts[index] + sizes[index] // 2 // UNIT
-
-            @pl.when((unit >= firsts[index]) & (unit < last))
-            def _():
-                local = (unit - firsts[index]) * UNIT
-                part = sizes[index] // 2
-                product_unit(lefts[index], rights[index], (1 - half) * part + local, half * part + local, halves, total, lax.rem(unit, RING), unit, 4)
-
+            ex.copy(unit - 2, PAIR).wait_send()
+
+        local = lax.rem(unit, units_full) * UNIT
+        ring = lax.rem(unit, 2)
+        col_other, col_mine = (1 - half) * part + local, half * part + local
+        lhs = jnp.concatenate([source[:, pl.ds(pl.multiple_of(col_other, UNIT), UNIT)], source[:, pl.ds(pl.multiple_of(col_mine, UNIT), UNIT)]], axis=1)
+        chunk = width // 4
+        for index in range(4):
+            cols = pl.ds(index * chunk, chunk)
+            prod = contract_rows(lhs, grad[:, cols])
+            halves[ring, :, cols] = prod[:UNIT]
+            mine[ring, :, cols] = prod[UNIT:]
         ex.copy(unit, PAIR).start()
 
     def pair_step(unit):
+        slot = lax.rem(unit, DEPTH)
         ex.copy(unit, PAIR).wait_recv()
-        total[unit] = total[unit] + recv_pair[unit]
+        total[slot] = total[slot] + mine[lax.rem(unit, 2)]
         ex.copy(unit, RS1).start()
 
     def to_out(unit):
         start = ex.owned(unit)
-        return pltpu.make_async_copy(total.at[unit, pl.ds(pl.multiple_of(start, 16), 16)], out_ref.at[pl.ds(pl.multiple_of(row_of(unit, half) + start, 16), 16)], send_sems.at[unit, LOCAL])
+        slot = lax.rem(unit, DEPTH)
+        return pltpu.make_async_copy(total.at[slot, pl.ds(pl.multiple_of(start, 16), 16)], out_ref.at[pl.ds(pl.multiple_of(row_of(unit, half) + start, 16), 16)], send_sems.at[slot, LOCAL])
 
     def finish(unit):
         ex.copy(unit, RS3).wait()
+        slot = lax.rem(unit, DEPTH)
         keep = pl.ds(pl.multiple_of(ex.owned(unit), 16), 16)
-        total[unit, keep] = total[unit, keep] + recv_3[unit]
+        total[slot, keep] = total[slot, keep] + recv_3[slot]
         to_out(unit).start()
-        to_out(unit).wait()
         ex.copy(unit, AG3).start()
 
     def forward(kind):
         def stage(unit):
+            if kind == AG3:
+                to_out(unit).wait()
             ex.copy(unit, kind).wait()
             if kind != AGP:
                 ex.copy(unit, kind + 1).start()
 
         return stage
 
-    pipeline(units, WEIGHT_LAGS, [produce, pair_step, lambda u: ex.reduce_step(u, RS1), lambda u: ex.reduce_step(u, RS2), finish, forward(AG3), forward(AG2), forward(AG1), forward(AGP)])
-    for unit in range(units - RING, units):
+    stages = [pair_step, lambda u: ex.reduce_step(u, RS1), lambda u: ex.reduce_step(u, RS2), finish, forward(AG3), forward(AG2), forward(AG1), forward(AGP)]
+
+    def derivative(layer, index):
+        load_weight(w_out, index).wait()
+        load_normed(normed_2, index).wait()
+        cols = block_of(index)
+        gain, bias = vecs[layer, 0:1, cols], vecs[layer, 1:2, cols]
+        rhs = weight[cols]
+        sum_n = jnp.zeros((1, BLOCK), jnp.float32)
+        sum_d = jnp.zeros((1, BLOCK), jnp.float32)
+        for chunk in range(rows // BLOCK):
+            part = pl.ds(chunk * BLOCK, BLOCK)
+            n = normed[part, cols]
+            d = jnp.where(n * gain + bias > 0.0, contract_cols(grad[part], rhs), 0.0)
+            deriv[part, cols] = d
+            sum_n = sum_n + jnp.sum(d * n, axis=0, keepdims=True)
+            sum_d = sum_d + jnp.sum(d, axis=0, keepdims=True)
+        stat_part[layer, 0:1, cols] = sum_n
+        stat_part[layer, 1:2, cols] = sum_d
+
+    lanes = width // shards
+
+    def lane_block(index):
+        return pl.ds(pl.multiple_of(index * lanes, lanes), lanes)
+
+    def stat_scatter(layer, shift):
+        peer = lax.rem(me + shift, shards)
+        return pltpu.make_async_remote_copy(src_ref=stat_part.at[layer, :, lane_block(peer)], dst_ref=stat_in.at[layer, shift], send_sem=stat_sems.at[0, layer, shift], recv_sem=stat_sems.at[1, layer, shift], device_id=(peer,), device_id_type=MESH_ID)
+
+    def stat_gather(layer, shift):
+        peer = lax.rem(me + shift, shards)
+        return pltpu.make_async_remote_copy(src_ref=stat_in.at[layer, 0], dst_ref=stat_ref.at[layer, :, lane_block(me)], send_sem=stat_sems.at[2, layer, shift], recv_sem=stat_sems.at[3, layer, shift], device_id=(peer,), device_id_type=MESH_ID)
+
+    def stat_send(layer):
+        for shift in range(1, shards):
+            stat_scatter(layer, shift).start()
+
+    def stat_reduce(layer):
+        summed = stat_part[layer, :, lane_block(me)]
+        for shift in range(1, shards):
+            stat_scatter(layer, shift).wait()
+            summed = summed + stat_in[layer, shift]
+        stat_in[layer, 0] = summed
+        stat_ref[layer, :, lane_block(me)] = summed
+        for shift in range(1, shards):
+            stat_gather(layer, shift).start()
+
+    def next_grad(layer):
+        for shift in range(1, shards):
+            stat_gather(layer, shift).wait()
+
+        def one(index, carry):
+            cols = block_of(index)
+            mean_n = stat_ref[layer, 0:1, cols] / row_count
+            mean_d = stat_ref[layer, 1:2, cols] / row_count
+            scale = vecs[layer, 0:1, cols] * vecs[layer, 2:3, cols]
+            for chunk in range(rows // BLOCK):
+                part = pl.ds(chunk * BLOCK, BLOCK)
+                grad[part, cols] = ((deriv[part, cols] - mean_d - normed[part, cols] * mean_n) * scale).astype(jnp.bfloat16)
+
+            @pl.when(layer == 0)
+            def _():
+                load_normed(normed_1, index).start()
+
+            return carry
+
+        lax.fori_loop(0, blocks, one, 0)
+
+    stat_part[...] = jnp.zeros_like(stat_part)
+
+    def tick(now, carry):
+        for lag, stage in reversed(list(zip(BACK_LAGS, stages))):
+            entered = now - lag
+            layer, place = lax.div(entered, PERIOD), lax.rem(entered, PERIOD)
+
+            @pl.when((entered >= 0) & (entered < enters) & (place < units_full))
+            def _(stage=stage, layer=layer, place=place):
+                stage(layer * units_full + place)
+
+        layer, place = lax.div(now, PERIOD), lax.rem(now, PERIOD)
+
+        @pl.when((layer < 2) & (place < units_full))
+        def _():
+            @pl.when(place == 0)
+            def _():
+                load_left.wait()
+
+                @pl.when(layer == 0)
+                def _():
+                    load_grad.wait()
+
+            produce(layer * units_full + place, left, width // 2)
+            derivative(layer, place)
+
+        @pl.when((now >= 2 * PERIOD) & (now < enters))
+        def _():
+            @pl.when(place == 0)
+            def _():
+                load_feat.wait()
+
+            produce(layer * units_full + place, feat_in, feat_in.shape[1] // 2)
+
+        @pl.when((layer < 2) & (place == units_full))
+        def _():
+            stat_send(layer)
+
+            @pl.when(layer == 0)
+            def _():
+                pltpu.make_async_copy(left_1, left, load_sems.at[0]).start()
+                for index in range(blocks):
+                    load_weight(w_mid, index).start()
+
+            stat_reduce(layer)
+
+        @pl.when((layer < 2) & (place == units_full + 3))
+        def _():
+            next_grad(layer)
+
+        return carry
+
+    lax.fori_loop(0, ticks, tick, 0)
+    last = 2 * units_full + units_last
+    for unit in (last - 2, last - 1):
         ex.copy(unit, PAIR).wait_send()
 
 
-def weight_sums(lefts, rights, call_id):
-    sizes = tuple(left.shape[1] for left in lefts)
-    width = rights[0].shape[1]
-    units = sum(size // 2 // UNIT for size in sizes)
+def backward(act_2, grad_z, w_out, normed_2, act_1, w_mid, normed_1, feat, vecs, shards, row_count):
+    rows, width = act_2.shape
+    feat_dim = feat.shape[1]
+    total_rows = 2 * width + feat_dim
     vmem = pl.BlockSpec(memory_space=pltpu.VMEM)
+    hbm = pl.BlockSpec(memory_space=pl.ANY)
     return pl.pallas_call(
-        functools.partial(weight_kernel, sizes),
-        out_shape=jax.ShapeDtypeStruct((sum(sizes), width), jnp.float32),
-        in_specs=[vmem] * (2 * len(sizes)),
-        out_specs=pl.BlockSpec(memory_space=pl.ANY),
-        scratch_shapes=exchange_scratch(units, width),
-        compiler_params=pltpu.CompilerParams(collective_id=call_id, has_side_effects=True, vmem_limit_bytes=VMEM_LIMIT),
-        cost_estimate=pl.CostEstimate(flops=2 * lefts[0].shape[0] * sum(sizes) * width, bytes_accessed=8 * sum(sizes) * width, transcendentals=0),
-        name=f"weight_sums_{call_id}",
-    )(*lefts, *rights)
+        functools.partial(backward_kernel, shards, row_count),
+        out_shape=(jax.ShapeDtypeStruct((total_rows, width), jnp.float32), jax.ShapeDtypeStruct((2, 8, width), jnp.float32)),
+        in_specs=[hbm] * 8 + [vmem],
+        out_specs=(hbm, vmem),
+        scratch_shapes=[
+            pltpu.VMEM((rows, width), jnp.bfloat16),
+            pltpu.VMEM((rows, feat_dim), jnp.bfloat16),
+            pltpu.VMEM((rows, width), jnp.bfloat16),
+            pltpu.VMEM((width, width), jnp.bfloat16),
+            pltpu.VMEM((rows, width), jnp.float32),
+            pltpu.VMEM((rows, width), jnp.float32),
+            pltpu.VMEM((2, UNIT, width), jnp.float32),
+            pltpu.VMEM((2, UNIT, width), jnp.float32),
+            pltpu.VMEM((DEPTH, UNIT, width), jnp.float32),
+            pltpu.VMEM((DEPTH, 64, width), jnp.float32),
+            pltpu.VMEM((DEPTH, 32, width), jnp.float32),
+            pltpu.VMEM((DEPTH, 16, width), jnp.float32),
+            pltpu.VMEM((2, 8, width), jnp.float32),
+            pltpu.VMEM((2, shards, 8, width // shards), jnp.float32),
+            pltpu.SemaphoreType.DMA((DEPTH, 9)),
+            pltpu.SemaphoreType.DMA((DEPTH, 9)),
+            pltpu.SemaphoreType.DMA((3,)),
+            pltpu.SemaphoreType.DMA((width // BLOCK,)),
+            pltpu.SemaphoreType.DMA((width // BLOCK,)),
+            pltpu.SemaphoreType.DMA((4, 2, shards)),
+        ],
+        compiler_params=pltpu.CompilerParams(collective_id=3, has_side_effects=True, vmem_limit_bytes=VMEM_LIMIT),
+        cost_estimate=pl.CostEstimate(flops=2 * rows * width * (2 * width + total_rows), bytes_accessed=16 * width * width, transcendentals=0),
+        name="backward",
+    )(act_2, grad_z, w_out, normed_2, act_1, w_mid, normed_1, feat, vecs)
 
 
 def solution(mesh):
@@ -363,15 +537,10 @@
             pre_act = normed_a * gain_vec + bias_vec
             act_a = jnp.maximum(pre_act, 0.0).astype(jnp.bfloat16)
             act_b = jnp.maximum(normed_b * gain_vec + bias_vec, 0.0).astype(jnp.bfloat16)
-            return act_a, act_b, normed_a, inv_a, pre_act > 0.0
-
-        def affine_back(grad_pre, normed, inv_std, gain_vec):
-            stat_sums = stats_all_reduce([jnp.sum(grad_pre * normed, axis=0), jnp.sum(grad_pre, axis=0)], shards)
-            grad_u = (grad_pre - stat_sums[1] / row_count - normed * (stat_sums[0] / row_count)) * (gain_vec * inv_std)
-            return grad_u.astype(jnp.bfloat16), stat_sums[0], stat_sums[1]
-
-        act_1, teach_1, normed_1, inv_1, mask_1 = hidden_pair(feat_a, feat_b, w_in, t_in, gain_1, bias_1)
-        act_2, teach_2, normed_2, inv_2, mask_2 = hidden_pair(act_1, teach_1, w_mid, t_mid, gain_2, bias_2)
+            return act_a, act_b, normed_a, inv_a
+
+        act_1, teach_1, normed_1, inv_1 = hidden_pair(feat_a, feat_b, w_in, t_in, gain_1, bias_1)
+        act_2, teach_2, normed_2, inv_2 = hidden_pair(act_1, teach_1, w_mid, t_mid, gain_2, bias_2)
         zh_a, inv_z, zh_b = norm_pair(jnp.dot(act_2, w_out, preferred_element_type=jnp.float32), jnp.dot(teach_2, t_out, preferred_element_type=jnp.float32))
         emb_a = zh_a.astype(jnp.bfloat16)
         emb_b = zh_b.astype(jnp.bfloat16)
@@ -380,13 +549,10 @@
         stat_sums = stats_all_reduce([jnp.sum(grad_emb, axis=0), jnp.sum(grad_emb * zh_a, axis=0), jnp.sum(loss_part, axis=0)], shards)
         loss_value = jnp.sum(stat_sums[2])
         grad_z = ((grad_emb - stat_sums[0] / row_count - zh_a * (stat_sums[1] / row_count)) * inv_z).astype(jnp.bfloat16)
-        grad_pre_2 = jnp.where(mask_2, contract_cols(grad_z, w_out), 0.0)
-        grad_u_2, grad_gain_2, grad_bias_2 = affine_back(grad_pre_2, normed_2, inv_2, gain_2)
-        grad_pre_1 = jnp.where(mask_1, contract_cols(grad_u_2, w_mid), 0.0)
-        grad_u_1, grad_gain_1, grad_bias_1 = affine_back(grad_pre_1, normed_1, inv_1, gain_1)
-        sums_out = weight_sums([act_2], [grad_z], 3)
-        sums_rest = weight_sums([act_1, feat_a], [grad_u_2, grad_u_1], 4)
+        pad = jnp.zeros((5,) + gain_1.shape, jnp.float32)
+        vecs = jnp.stack([jnp.concatenate([jnp.stack([gain_2, bias_2, inv_2]), pad]), jnp.concatenate([jnp.stack([gain_1, bias_1, inv_1]), pad])])
+        sums, stats = backward(act_2, grad_z, w_out, normed_2, act_1, w_mid, normed_1, feat_a, vecs, shards, row_count)
         width = w_mid.shape[0]
-        return (loss_value, grad_emb, sums_rest[width:], sums_rest[:width], sums_out, grad_gain_1, grad_bias_1, grad_gain_2, grad_bias_2)
+        return (loss_value, grad_emb, sums[2 * width :], sums[width : 2 * width], sums[:width], stats[1, 0], stats[1, 1], stats[0, 0], stats[0, 1])
 
     return jax.shard_map(local_step, mesh=mesh, in_specs=(row_part, row_part) + (replicated,) * 11, out_specs=(replicated, row_part) + (replicated,) * 7, check_vma=False)

time: 707 us -> 609 us (0.86)
  Pallas kernels: 495 us -> 448 us
  matrix products: 122 us -> 92 us
  other arithmetic: 51.7 us -> 32.1 us
    dot_general x3 -> x1, matrix products: 51.1 us -> 16.4 us  [contract_cols(): lax.dot_general(left_op, right_op, (((1,), (1,)), ((), ())), preferred_el...]
    pallas_call x6 -> x4, Pallas kernels: 70.5 us -> 48 us  [stats_all_reduce(): pl.pallas_call(functools.partial(stats_kernel, shards), out_shape=jax.Sha...]
    pallas_call x2 -> x1, Pallas kernels: 312 us -> 296 us  [backward(): pl.pallas_call(functools.partial(backward_kernel, shards, row_count), out...]
    convert_element_type x2 -> x0, other arithmetic: 15.9 us -> none  [affine_back(): return (grad_u.astype(jnp.bfloat16), stat_sums[0], stat_sums[1])]
    unnamed x33 -> x22, local copies, waits for them, and re-layouts: 11.9 us -> 0.05 us
    slice x2 -> x3, local copies, waits for them, and re-layouts: 16.5 us -> 27.5 us  [the longest x1 21.2 us: local_step(): sums[:width]]
    pallas_call x1, Pallas kernels: 112 us -> 104 us  [corr_grad(): pl.pallas_call(functools.partial(corr_kernel, row_count), out_shape=(jax....]
where the time goes in v2:
time: 609 us; the launch traced here: 604 us
  Pallas kernels  448 us (74%)
  matrix products  92 us (15%)
  other arithmetic  32.1 us (5%)
  local copies, waits for them, and re-layouts  30.4 us (5%)
    pallas_call x1, Pallas kernels, backward(): pl.pallas_call(functools.partial(backward_kernel, shards, row_count), out...  296 us
    pallas_call x1, Pallas kernels, corr_grad(): pl.pallas_call(functools.partial(corr_kernel, row_count), out_shape=(jax....  104 us
    pallas_call x4, Pallas kernels, stats_all_reduce(): pl.pallas_call(functools.partial(stats_kernel, shards), out_shape=jax.Sha...  48 us
    dot_general x2, matrix products, hidden_pair(): jnp.dot(in_b, weight_b, preferred_element_type=jnp.float32)  23.9 us
    slice x1, local copies, waits for them, and re-layouts, local_step(): sums[:width]  21.2 us
    dot_general x2, matrix products, hidden_pair(): jnp.dot(in_a, weight_a, preferred_element_type=jnp.float32)  20.5 us
    dot_general x1, matrix products, local_step(): jnp.dot(teach_2, t_out, preferred_element_type=jnp.float32)  16.4 us
    dot_general x1, matrix products, contract_cols(): lax.dot_general(left_op, right_op, (((1,), (1,)), ((), ())), preferred_el...  16.4 us

profile of v2, /device:TPU:0, one launch (start us, length us, event | category | flops | bytes accessed | tf_op | source)
XLA Modules:
  0.0 604.3 jit_solution(13968070607113051547)
XLA Ops:
  0.6 0.0 copy-start.10
  0.7 0.0 copy-start.9
  1.5 0.1 pad.9.clone
  1.5 7.7 %multiply_reduce_fusion.5 = (f32[2048]{0:T(1024)S(1)}, f32[2048]{0:T(1024)S(1)}, f32[1024,2048]{1,0:T(8,128)}) fusion(bf16[1024,512]{1,0:T(8,128)(2,1)} %param.14, bf16[512,2048]{1,0:T(8,128)(2,1)} %param.18), kind=kOutput, calls=%fused_computation.14 | convolution fusion | flops 2153771008 | bytes 11550720 | tf_op jit(solution)/shard_map/dot_general | solution.py:536
  9.3 0.0 copy-start.5
  9.3 0.0 copy-done.10
  9.3 0.0 copy-done.9
  9.3 5.8 multiply_reduce_fusion.6
  15.0 0.7 stack.76.x_ref
  15.7 14.5 %stats_all_reduce.4 = f32[8,2048]{1,0:T(8,128)} custom-call(f32[8,2048]{1,0:T(8,128)} %stack.76.x_ref), custom_call_target="tpu_custom_call" | custom-call | tf_op jit(solution)/shard_map/stats_all_reduce/pallas_call | solution.py:70
  30.2 0.8 broadcast_multiply_fusion.2
  31.1 0.0 copy-done.5
  31.1 0.0 copy-done.6
  31.2 0.0 copy-start.1
  31.2 16.2 %multiply_reduce_fusion.3 = (f32[2048]{0:T(1024)S(1)}, f32[2048]{0:T(1024)S(1)}, f32[1024,2048]{1,0:T(8,128)}) fusion(bf16[2048,2048]{1,0:T(8,128)(2,1)} %param.19, f32[1024,2048]{1,0:T(8,128)} %get-tuple-element.59, f32[2048]{0:T(1024)S(1)} %copy-done.5, f32[2048]{0:T(1024)S(1)} %copy-done.6, f32[2048]{0:T(1024)S(1)} %bitcast.92, f32[2048]{0:T(1024)S(1)} %bitcast.93), kind=kOutput, calls=%fused_computation.9 | convolution fusion | flops 8608804864 | bytes 25214976 | tf_op jit(solution)/shard_map/dot_general | solution.py:536
  47.4 0.0 copy-done.1
  47.4 4.6 maximum_convert_fusion.2
  52.0 14.8 %multiply_reduce_fusion.4 = (f32[2048]{0:T(1024)S(1)}, f32[2048]{0:T(1024)S(1)}, f32[1024,2048]{1,0:T(8,128)}) fusion(bf16[1024,2048]{1,0:T(8,128)(2,1)S(1)} %get-tuple-element.33.left_1, bf16[2048,2048]{1,0:T(8,128)(2,1)} %w_mid.1), kind=kOutput, calls=%fused_computation.10 | convolution fusion | flops 8596221952 | bytes 20987904 | tf_op jit(solution)/shard_map/dot_general | solution.py:536
  66.7 0.0 copy-done.2
  66.8 0.7 stack.81.x_ref
  67.4 10.3 %stats_all_reduce.5 = f32[8,2048]{1,0:T(8,128)} custom-call(f32[8,2048]{1,0:T(8,128)} %stack.81.x_ref), custom_call_target="tpu_custom_call" | custom-call | tf_op jit(solution)/shard_map/stats_all_reduce/pallas_call | solution.py:70
  77.8 0.8 broadcast_multiply_fusion.1
  78.6 0.0 copy-done.7
  78.7 0.0 copy-done.8
  78.7 0.0 copy-start
  78.7 16.4 %multiply_reduce_fusion.1 = (f32[2048]{0:T(1024)S(1)}, f32[2048]{0:T(1024)S(1)}, f32[1024,2048]{1,0:T(8,128)}) fusion(bf16[2048,2048]{1,0:T(8,128)(2,1)} %param.20, f32[1024,2048]{1,0:T(8,128)} %get-tuple-element.61, f32[2048]{0:T(1024)S(1)} %copy-done.7, f32[2048]{0:T(1024)S(1)} %copy-done.8, f32[2048]{0:T(1024)S(1)} %bitcast.94, f32[2048]{0:T(1024)S(1)} %bitcast.95), kind=kOutput, calls=%fused_computation.4 | convolution fusion | flops 8608804864 | bytes 25214976 | tf_op jit(solution)/shard_map/dot_general | solution.py:544
  95.1 0.1 maximum_bitcast_fusion
  95.2 0.7 pad_maximum_fusion.vecs
  95.8 0.0 copy-done
  95.8 4.6 maximum_convert_fusion
  100.4 14.7 %multiply_reduce_fusion.2 = (f32[2048]{0:T(1024)S(1)}, f32[2048]{0:T(1024)S(1)}, f32[1024,2048]{1,0:T(8,128)}) fusion(bf16[1024,2048]{1,0:T(8,128)(2,1)S(1)} %get-tuple-element.31.left_2, bf16[2048,2048]{1,0:T(8,128)(2,1)} %w_out.1), kind=kOutput, calls=%fused_computation.5 | convolution fusion | flops 8596221952 | bytes 20987904 | tf_op jit(solution)/shard_map/dot_general | solution.py:544
  115.1 0.0 copy-done.3
  115.1 0.7 stack.86.x_ref
  115.8 12.2 %stats_all_reduce.6 = f32[8,2048]{1,0:T(8,128)} custom-call(f32[8,2048]{1,0:T(8,128)} %stack.86.x_ref), custom_call_target="tpu_custom_call" | custom-call | tf_op jit(solution)/shard_map/stats_all_reduce/pallas_call | solution.py:70
  128.0 0.8 broadcast_multiply_fusion
  128.9 9.3 %multiply_convert_fusion.1 = (bf16[1024,2048]{1,0:T(8,128)(2,1)}, bf16[1024,2048]{1,0:T(8,128)(2,1)}) fusion(f32[1024,2048]{1,0:T(8,128)} %get-tuple-element.63, f32[2048]{0:T(1024)S(1)} %bitcast.71, f32[2048]{0:T(1024)S(1)} %bitcast.72, f32[2048]{0:T(1024)S(1)} %bitcast.58, f32[1024,2048]{1,0:T(8,128)} %get-tuple-element.62, f32[2048]{0:T(1024)S(1)} %bitcast.55), kind=kLoop, calls=%fused_computation.3 | loop fusion | flops 12582912 | bytes 25198592 | tf_op jit(solution)/shard_map/convert_element_type | solution.py:546
  138.2 104.2 %corr_grad.1 = (bf16[2048,2048]{1,0:T(8,128)(2,1)}, f32[8,2048]{1,0:T(8,128)}) custom-call(f32[1,1]{1,0:T(1,128)} %bitcast.54.off_ref, bf16[1024,2048]{1,0:T(8,128)(2,1)} %get-tuple-element.66.left_ref, bf16[1024,2048]{1,0:T(8,128)(2,1)} %get-tuple-element.65.right_ref), custom_call_target="tpu_custom_call" | custom-call | flops 8589934592 | bytes 16777216 | tf_op jit(solution)/shard_map/corr_grad/pallas_call | solution.py:250
  242.4 0.0 copy-start.4
  242.4 16.4 %multiply_reduce_fusion = (f32[2048]{0:T(1024)S(1)}, f32[2048]{0:T(1024)S(1)}, f32[1024,2048]{1,0:T(8,128)}) fusion(f32[1024,2048]{1,0:T(8,128)} %get-tuple-element.62, f32[2048]{0:T(1024)S(1)} %bitcast.59, f32[2048]{0:T(1024)S(1)} %bitcast.56, bf16[1024,2048]{1,0:T(8,128)(2,1)} %get-tuple-element.65.right_ref, bf16[2048,2048]{1,0:T(8,128)(2,1)} %get-tuple-element.13), kind=kOutput, calls=%fused_computation.1 | convolution fusion | flops 8602513408 | bytes 29392896 | tf_op jit(solution)/shard_map/dot_general | solution.py:22
  258.7 0.0 copy-done.4
  258.8 0.7 stack.90.x_ref
  259.5 11.0 %stats_all_reduce.7 = f32[8,2048]{1,0:T(8,128)} custom-call(f32[8,2048]{1,0:T(8,128)} %stack.90.x_ref), custom_call_target="tpu_custom_call" | custom-call | tf_op jit(solution)/shard_map/stats_all_reduce/pallas_call | solution.py:70
  270.5 1.6 slice_multiply_fusion.1
  272.0 8.7 %multiply_convert_fusion.grad_z = bf16[1024,2048]{1,0:T(8,128)(2,1)} fusion(f32[1024,2048]{1,0:T(8,128)} %get-tuple-element.64, f32[1024,2048]{1,0:T(8,128)} %get-tuple-element.62, f32[2048]{0:T(1024)S(1)} %bitcast.68, f32[2048]{0:T(1024)S(1)} %bitcast.67, f32[2048]{0:T(1024)S(1)} %bitcast.60, f32[2048]{0:T(1024)S(1)} %bitcast.57), kind=kLoop, calls=%fused_computation | loop fusion | flops 14680064 | bytes 21004288 | tf_op jit(solution)/shard_map/convert_element_type | solution.py:551
  280.8 295.9 %backward.1 = (f32[4608,2048]{1,0:T(8,128)}, f32[2,8,2048]{2,1,0:T(8,128)}) custom-call(bf16[1024,2048]{1,0:T(8,128)(2,1)} %copy-done.3, bf16[1024,2048]{1,0:T(8,128)(2,1)} %multiply_convert_fusion.grad_z, bf16[2048,2048]{1,0:T(8,128)(2,1)} %w_out.1, f32[1024,2048]{1,0:T(8,128)} %get-tuple-element.32.normed_2, bf16[1024,2048]{1,0:T(8,128)(2,1)} %copy-done.2, ...), custom_call_target="tpu_custom_call" | custom-call | flops 36507222016 | bytes 67108864 | tf_op jit(solution)/shard_map/backward/pallas_call | solution.py:488
  576.7 1.6 fusion.28
  578.2 4.7 slice.93
  582.9 21.2 %fusion.27 = (f32[2048,2048]{1,0:T(8,128)}, f32[2048,2048]{1,0:T(8,128)}) fusion(f32[4608,2048]{1,0:T(8,128)} %get-tuple-element.15), kind=kLoop, calls=%fused_computation.59 | loop fusion | bytes 67108864 | tf_op jit(solution)/shard_map/slice | solution.py:556
  (12 shorter events, 0.2 us)
Async XLA Ops:
  0.6 8.6 %copy-start.10 = (bf16[1024,512]{1,0:T(8,128)(2,1)S(1)}, bf16[1024,512]{1,0:T(8,128)(2,1)}, u32[]{:S(2)}) copy-start(bf16[1024,512]{1,0:T(8,128)(2,1)} %feat.1) | copy-start | bytes 3145732
  0.7 8.6 %copy-start.9 = (bf16[512,2048]{1,0:T(8,128)(2,1)S(1)}, bf16[512,2048]{1,0:T(8,128)(2,1)}, u32[]{:S(2)}) copy-start(bf16[512,2048]{1,0:T(8,128)(2,1)} %param.15) | copy-start | bytes 6291460
  9.3 21.9 %copy-start.5 = (f32[2048]{0:T(1024)S(1)}, f32[2048]{0:T(1024)}, u32[]{:S(2)}) copy-start(f32[2048]{0:T(1024)} %param.22) | copy-start | bytes 24580
  9.3 21.9 %copy-start.6 = (f32[2048]{0:T(1024)S(1)}, f32[2048]{0:T(1024)}, u32[]{:S(2)}) copy-start(f32[2048]{0:T(1024)} %param.21) | copy-start | bytes 24580
  31.2 16.2 %copy-start.1 = (f32[1024,2048]{1,0:T(8,128)S(1)}, f32[1024,2048]{1,0:T(8,128)}, u32[]{:S(2)}) copy-start(f32[1024,2048]{1,0:T(8,128)} %get-tuple-element.58) | copy-start | bytes 25165828
  51.9 14.8 %copy-start.2 = (bf16[1024,2048]{1,0:T(8,128)(2,1)}, bf16[1024,2048]{1,0:T(8,128)(2,1)S(1)}, u32[]{:S(2)}) copy-start(bf16[1024,2048]{1,0:T(8,128)(2,1)S(1)} %get-tuple-element.33.left_1) | copy-start | bytes 12582916
  51.9 26.7 %copy-start.7 = (f32[2048]{0:T(1024)S(1)}, f32[2048]{0:T(1024)}, u32[]{:S(2)}) copy-start(f32[2048]{0:T(1024)} %param.24) | copy-start | bytes 24580
  51.9 26.7 %copy-start.8 = (f32[2048]{0:T(1024)S(1)}, f32[2048]{0:T(1024)}, u32[]{:S(2)}) copy-start(f32[2048]{0:T(1024)} %param.23) | copy-start | bytes 24580
  78.7 17.2 %copy-start = (f32[1024,2048]{1,0:T(8,128)S(1)}, f32[1024,2048]{1,0:T(8,128)}, u32[]{:S(2)}) copy-start(f32[1024,2048]{1,0:T(8,128)} %get-tuple-element.60) | copy-start | bytes 25165828
  100.4 14.7 %copy-start.3 = (bf16[1024,2048]{1,0:T(8,128)(2,1)}, bf16[1024,2048]{1,0:T(8,128)(2,1)S(1)}, u32[]{:S(2)}) copy-start(bf16[1024,2048]{1,0:T(8,128)(2,1)S(1)} %get-tuple-element.31.left_2) | copy-start | bytes 12582916
  242.4 16.4 %copy-start.4 = (f32[8,2048]{1,0:T(8,128)S(1)}, f32[8,2048]{1,0:T(8,128)}, u32[]{:S(2)}) copy-start(f32[8,2048]{1,0:T(8,128)} %get-tuple-element.14) | copy-start | bytes 196612

commit v3 on v2

--- a/solution.py
+++ b/solution.py
@@ -27,55 +27,166 @@
     return me + mask * (1 - 2 * bit), bit
 
 
-def stats_kernel(shards, x_ref, out_ref, parts, send_a, recv_a, send_b, recv_b):
+class SumExchange:
+    def __init__(self, me, shards, slots, send_sems, recv_sems):
+        self.me, self.shards, self.slots, self.send_sems, self.recv_sems = me, shards, slots, send_sems, recv_sems
+
+    def copy(self, index, peer, slot):
+        return pltpu.make_async_remote_copy(src_ref=self.slots.at[index, self.me], dst_ref=self.slots.at[index, slot], send_sem=self.send_sems.at[index, peer], recv_sem=self.recv_sems.at[index, slot], device_id=(peer,), device_id_type=MESH_ID)
+
+    def peers(self):
+        return [lax.rem(self.me + shift, self.shards) for shift in range(1, self.shards)]
+
+    def start(self, index):
+        for peer in self.peers():
+            self.copy(index, peer, self.me).start()
+
+    def finish(self, index):
+        for peer in self.peers():
+            self.copy(index, peer, peer).wait_recv()
+            self.copy(index, peer, self.me).wait_send()
+        summed = self.slots[index, 0]
+        for slot in range(1, self.shards):
+            summed = summed + self.slots[index, slot]
+        return summed
+
+
+def enter_all(me, shards):
+    barrier = pltpu.get_barrier_semaphore()
+    for shift in range(1, shards):
+        pl.semaphore_signal(barrier, inc=1, device_id=(lax.rem(me + shift, shards),), device_id_type=MESH_ID)
+    pl.semaphore_wait(barrier, shards - 1)
+
+
+COLS = 512
+ROWS = 256
+
+
+def forward_kernel(shards, row_count, feat_a, feat_b, w_in, t_in, w_mid, t_mid, w_out, t_out, affine, act_1, act_2, normed_1, normed_2, normed_z, emb_a, emb_b, inv_ref, pre, act, feat, weight_in, weight, slots, sums, send_sems, recv_sems, load_sems, store_sems):
     me = lax.axis_index(DATA_AXIS)
-    lanes = x_ref.shape[1] // shards
-    barrier = pltpu.get_barrier_semaphore()
-    for step in range(1, shards):
-        peer = lax.rem(me + step, shards)
-        pl.semaphore_signal(barrier, inc=1, device_id=(peer,), device_id_type=MESH_ID)
-    pl.semaphore_wait(barrier, shards - 1)
-
-    def lane_block(index):
-        return pl.ds(pl.multiple_of(index * lanes, lanes), lanes)
-
-    def scatter(step):
-        peer = lax.rem(me + step, shards)
-        return pltpu.make_async_remote_copy(src_ref=x_ref.at[:, lane_block(peer)], dst_ref=parts.at[step], send_sem=send_a.at[step], recv_sem=recv_a.at[step], device_id=(peer,), device_id_type=MESH_ID)
-
-    def gather(step):
-        peer = lax.rem(me + step, shards)
-        mine = lane_block(me)
-        return pltpu.make_async_remote_copy(src_ref=parts.at[0], dst_ref=out_ref.at[:, mine], send_sem=send_b.at[step], recv_sem=recv_b.at[step], device_id=(peer,), device_id_type=MESH_ID)
-
-    for step in range(1, shards):
-        scatter(step).start()
-    total = x_ref[:, lane_block(me)]
-    for step in range(1, shards):
-        scatter(step).wait()
-        total = total + parts[step]
-    parts[0] = total
-    out_ref[:, lane_block(me)] = total
-    for step in range(1, shards):
-        gather(step).start()
-    for step in range(1, shards):
-        gather(step).wait()
-
-
-def stats_all_reduce(rows, shards):
-    pad = [jnp.zeros_like(rows[0])] * (8 - len(rows))
-    packed = jnp.stack(list(rows) + pad)
-    lanes = packed.shape[1] // shards
+    rows, width = act_1.shape
+    groups = width // COLS
+    copies = [pltpu.make_async_copy(src, dst, load_sems.at[index]) for index, (src, dst) in enumerate([(feat_a, feat.at[0]), (w_in, weight_in.at[0]), (feat_b, feat.at[1]), (t_in, weight_in.at[1]), (w_mid, weight.at[0]), (t_mid, weight.at[1]), (w_out, weight.at[0]), (t_out, weight.at[1])])]
+    for index in range(6):
+        copies[index].start()
+    enter_all(me, shards)
+    ex = SumExchange(me, shards, slots, send_sems, recv_sems)
+
+    def product(index, source, matrix, target):
+        def group(number, carry):
+            cols = pl.ds(pl.multiple_of(number * COLS, COLS), COLS)
+            total = jnp.zeros((1, COLS), jnp.float32)
+            squares = jnp.zeros((1, COLS), jnp.float32)
+            for chunk in range(rows // ROWS):
+                part = pl.ds(chunk * ROWS, ROWS)
+                out = jnp.dot(source[part], matrix[:, cols], preferred_element_type=jnp.float32)
+                target[part, cols] = out
+                total = total + jnp.sum(out, axis=0, keepdims=True)
+                squares = squares + jnp.sum(out * out, axis=0, keepdims=True)
+            slots[index, me, pl.ds(number, 1)] = total
+            slots[index, me, pl.ds(number + groups, 1)] = squares
+            return carry
+
+        lax.fori_loop(0, groups, group, 0)
+        ex.start(index)
+
+    def normalise(index, source, target, layer, keep):
+        summed = ex.finish(index) / row_count
+        mean = summed[:groups]
+        inv = lax.rsqrt(summed[groups:] - mean * mean + NORM_EPS)
+        sums[index, :groups] = mean
+        sums[index, groups:] = inv
+        if keep is not None:
+            inv_ref[layer, :groups] = inv
+
+        def group(number, carry):
+            cols = pl.ds(pl.multiple_of(number * COLS, COLS), COLS)
+            col_mean = sums[index, pl.ds(number, 1)]
+            col_inv = sums[index, pl.ds(number + groups, 1)]
+            for chunk in range(rows // ROWS):
+                part = pl.ds(chunk * ROWS, ROWS)
+                out = (source[part, cols] - col_mean) * col_inv
+                if keep is not None:
+                    source[part, cols] = out
+                if layer < 2:
+                    out = jnp.maximum(out * affine[2 * layer : 2 * layer + 1, cols] + affine[2 * layer + 1 : 2 * layer + 2, cols], 0.0)
+                target[part, cols] = out.astype(jnp.bfloat16)
+            return carry
+
+        lax.fori_loop(0, groups, group, 0)
+
+    def store(number, src, dst):
+        copy = pltpu.make_async_copy(src, dst, store_sems.at[number])
+        copy.start()
+        return copy
+
+    copies[0].wait()
+    copies[1].wait()
+    product(0, feat.at[0], weight_in.at[0], pre.at[0])
+    copies[2].wait()
+    copies[3].wait()
+    product(1, feat.at[1], weight_in.at[1], pre.at[1])
+    normalise(0, pre.at[0], act.at[0], 0, normed_1)
+    out_n1 = store(0, pre.at[0], normed_1)
+    out_x1 = store(1, act.at[0], act_1)
+    copies[4].wait()
+    product(2, act.at[0], weight.at[0], pre.at[2])
+    copies[6].start()
+    normalise(1, pre.at[1], act.at[1], 0, None)
+    copies[5].wait()
+    out_n1.wait()
+    product(3, act.at[1], weight.at[1], pre.at[0])
+    copies[7].start()
+    out_x1.wait()
+    normalise(2, pre.at[2], act.at[0], 1, normed_2)
+    out_n2 = store(2, pre.at[2], normed_2)
+    out_x2 = store(3, act.at[0], act_2)
+    copies[6].wait()
+    product(4, act.at[0], weight.at[0], pre.at[1])
+    normalise(3, pre.at[0], act.at[1], 1, None)
+    copies[7].wait()
+    out_n2.wait()
+    product(5, act.at[1], weight.at[1], pre.at[2])
+    out_x2.wait()
+    normalise(4, pre.at[1], act.at[0], 2, normed_z)
+    out_z = store(4, pre.at[1], normed_z)
+    out_a = store(5, act.at[0], emb_a)
+    normalise(5, pre.at[2], act.at[1], 2, None)
+    out_b = store(6, act.at[1], emb_b)
+    for copy in (out_z, out_a, out_b):
+        copy.wait()
+
+
+def forward_pass(feat_a, feat_b, w_in, t_in, w_mid, t_mid, w_out, t_out, affine, shards, row_count):
+    rows, feat_dim = feat_a.shape
+    width = w_mid.shape[0]
+    groups = width // COLS
     vmem = pl.BlockSpec(memory_space=pltpu.VMEM)
+    hbm = pl.BlockSpec(memory_space=pl.ANY)
+    half_out = jax.ShapeDtypeStruct((rows, width), jnp.bfloat16)
+    full_out = jax.ShapeDtypeStruct((rows, width), jnp.float32)
     return pl.pallas_call(
-        functools.partial(stats_kernel, shards),
-        out_shape=jax.ShapeDtypeStruct(packed.shape, jnp.float32),
-        in_specs=[vmem],
-        out_specs=vmem,
-        scratch_shapes=[pltpu.VMEM((shards, 8, lanes), jnp.float32)] + [pltpu.SemaphoreType.DMA((shards,))] * 4,
-        compiler_params=pltpu.CompilerParams(collective_id=1, has_side_effects=True),
-        name="stats_all_reduce",
-    )(packed)
+        functools.partial(forward_kernel, shards, row_count),
+        out_shape=(half_out, half_out, full_out, full_out, full_out, half_out, half_out, jax.ShapeDtypeStruct((3, 8, COLS), jnp.float32)),
+        in_specs=[hbm] * 8 + [vmem],
+        out_specs=(hbm,) * 7 + (vmem,),
+        scratch_shapes=[
+            pltpu.VMEM((3, rows, width), jnp.float32),
+            pltpu.VMEM((2, rows, width), jnp.bfloat16),
+            pltpu.VMEM((2, rows, feat_dim), jnp.bfloat16),
+            pltpu.VMEM((2, feat_dim, width), jnp.bfloat16),
+            pltpu.VMEM((2, width, width), jnp.bfloat16),
+            pltpu.VMEM((6, shards, 2 * groups, COLS), jnp.float32),
+            pltpu.VMEM((6, 2 * groups, COLS), jnp.float32),
+            pltpu.SemaphoreType.DMA((6, shards)),
+            pltpu.SemaphoreType.DMA((6, shards)),
+            pltpu.SemaphoreType.DMA((8,)),
+            pltpu.SemaphoreType.DMA((7,)),
+        ],
+        compiler_params=pltpu.CompilerParams(collective_id=4, has_side_effects=True, vmem_limit_bytes=VMEM_LIMIT),
+        cost_estimate=pl.CostEstimate(flops=4 * rows * width * (2 * width + feat_dim), bytes_accessed=24 * width * width, transcendentals=0),
+        name="forward",
+    )(feat_a, feat_b, w_in, t_in, w_mid, t_mid, w_out, t_out, affine)
 
 
 PAIR, RS1, RS2, RS3, AG3, AG2, AG1, AGP, LOCAL = range(9)
@@ -154,11 +265,11 @@
 
 def pipeline(units, lags, stages):
     def step(now, carry):
-        for lag, stage in zip(lags, stages):
+        for lag, stage in reversed(list(zip(lags, stages))):
             unit = now - lag
 
             @pl.when((unit >= 0) & (unit < units))
-            def _():
+            def _(unit=unit, stage=stage):
                 stage(unit)
 
         return carry
@@ -177,18 +288,20 @@
 
 
 RING = 3
-CORR_LAGS = (0, 1, 4, 6, 8, 10, 13, 17, 19)
-
-
-def corr_kernel(row_count, off_ref, left_ref, right_ref, grad_ref, loss_ref, halves, recv_pair, recv_1, recv_2, recv_3, total, send_sems, recv_sems):
+CORR_LAGS = (0, 1, 4, 6, 8, 10, 13, 17, 18)
+
+
+def corr_kernel(shards, row_count, off_ref, inv_ref, left_ref, right_ref, normed, emb_out, back_out, loss_ref, grad_ref, emb_grad, back, norm_in, loss_acc, wide, slots, halves, recv_pair, recv_1, recv_2, recv_3, total, send_sems, recv_sems, sum_send, sum_recv, norm_sems, store_sems):
     me = lax.axis_index(DATA_AXIS)
-    width = right_ref.shape[1]
-    half_rows = left_ref.shape[1] // 2
+    rows, width = right_ref.shape
+    half_rows = width // 2
     units = half_rows // UNIT
+    groups = width // COLS
     _, half = flip(me, 1)
-    enter(me)
+    enter_all(me, shards)
     ex = Exchange(me, RING, halves, grad_ref, recv_pair, recv_1, recv_2, recv_3, total, send_sems, recv_sems, lambda unit, h: h * half_rows + unit * UNIT, units)
-    loss_ref[...] = jnp.zeros_like(loss_ref)
+    sums = SumExchange(me, shards, slots, sum_send, sum_recv)
+    loss_acc[...] = jnp.zeros_like(loss_acc)
 
     def produce(unit):
         @pl.when(unit >= RING)
@@ -213,7 +326,7 @@
         off_weight = off_ref[0, 0]
         miss = 1.0 - corr
         terms = jnp.where(on_diag, miss * miss, off_weight * (corr * corr))
-        loss_ref[...] += terms[:8] + terms[8:]
+        loss_acc[...] += terms[:8] + terms[8:]
         grad = jnp.where(on_diag, -2.0 * miss, 2.0 * off_weight * corr).astype(jnp.bfloat16)
         grad_ref[pl.ds(pl.multiple_of(row, 16), 16)] = grad
         ex.copy(unit, AG3).start()
@@ -224,11 +337,93 @@
             if kind != AGP:
                 ex.copy(unit, kind + 1).start()
 
+            if kind == AG1:
+                for side in range(2):
+                    load_norm(row_of(unit, side), lax.rem(unit, 2), side).start()
+
         return stage
 
-    pipeline(units, CORR_LAGS, [produce, pair_step, lambda u: ex.reduce_step(u, RS1), lambda u: ex.reduce_step(u, RS2), finish, forward(AG3), forward(AG2), forward(AG1), forward(AGP)])
+    def row_of(unit, side):
+        return (half + side * (1 - 2 * half)) * half_rows + unit * UNIT
+
+    def lanes(start):
+        return pl.ds(pl.multiple_of(start, UNIT), UNIT)
+
+    def load_norm(start, slot, side):
+        return pltpu.make_async_copy(normed.at[:, lanes(start)], norm_in.at[slot, side], norm_sems.at[slot, side])
+
+    def embed(unit):
+        ex.copy(unit, AGP).wait()
+        slot = lax.rem(unit, 2)
+        starts = [row_of(unit, side) for side in range(2)]
+        rhs = jnp.concatenate([grad_ref[lanes(start)] for start in starts], axis=0)
+        for side in range(2):
+            load_norm(starts[side], slot, side).wait()
+        plain = [jnp.zeros((1, UNIT), jnp.float32)] * 2
+        crossed = [jnp.zeros((1, UNIT), jnp.float32)] * 2
+        for chunk in range(rows // ROWS):
+            part = pl.ds(chunk * ROWS, ROWS)
+            out = contract_cols(right_ref[part], rhs) * (1.0 / row_count)
+            for side in range(2):
+                piece = out[:, side * UNIT : (side + 1) * UNIT]
+                emb_grad[part, lanes(starts[side])] = piece
+                plain[side] = plain[side] + jnp.sum(piece, axis=0, keepdims=True)
+                crossed[side] = crossed[side] + jnp.sum(piece * norm_in[slot, side, part], axis=0, keepdims=True)
+        for side in range(2):
+            wide[0:1, lanes(starts[side])] = plain[side]
+            wide[1:2, lanes(starts[side])] = crossed[side]
+
+    pipeline(units, CORR_LAGS, [produce, pair_step, lambda u: ex.reduce_step(u, RS1), lambda u: ex.reduce_step(u, RS2), finish, forward(AG3), forward(AG2), forward(AG1), embed])
     for unit in range(units - RING, units):
         ex.copy(unit, PAIR).wait_send()
+    folded = loss_acc[:, :UNIT]
+    for index in range(1, width // UNIT):
+        folded = folded + loss_acc[:, index * UNIT : (index + 1) * UNIT]
+    slots[0, me, :, COLS:] = folded
+    for index in range(groups):
+        cols = pl.ds(index * COLS, COLS)
+        slots[0, me, index : index + 1, :COLS] = wide[0:1, cols]
+        slots[0, me, groups + index : groups + index + 1, :COLS] = wide[1:2, cols]
+    sums.start(0)
+    store_emb = pltpu.make_async_copy(emb_grad, emb_out, store_sems.at[0])
+    store_emb.start()
+
+    def load_block(index, slot):
+        return [load_norm((2 * index + side) * UNIT, slot, side) for side in range(2)]
+
+    for copy in load_block(0, 0) + load_block(1, 1):
+        copy.start()
+    summed = sums.finish(0)
+    loss_ref[...] = summed[:, COLS:]
+    means = summed[:, :COLS] / row_count
+    for index in range(groups):
+        cols = pl.ds(index * COLS, COLS)
+        wide[0:1, cols] = means[index : index + 1]
+        wide[1:2, cols] = means[groups + index : groups + index + 1]
+        wide[2:3, cols] = inv_ref[2, index : index + 1]
+
+    def norm_back(index, carry):
+        slot = lax.rem(index, 2)
+        for side, copy in enumerate(load_block(index, slot)):
+            copy.wait()
+            start = (2 * index + side) * UNIT
+            mean_g, mean_gn, inv = wide[0:1, lanes(start)], wide[1:2, lanes(start)], wide[2:3, lanes(start)]
+            for chunk in range(rows // ROWS):
+                part = pl.ds(chunk * ROWS, ROWS)
+                back[part, lanes(start)] = ((emb_grad[part, lanes(start)] - mean_g - norm_in[slot, side, part] * mean_gn) * inv).astype(jnp.bfloat16)
+
+        @pl.when(index + 2 < width // (2 * UNIT))
+        def _():
+            for copy in load_block(index + 2, slot):
+                copy.start()
+
+        return carry
+
+    lax.fori_loop(0, width // (2 * UNIT), norm_back, 0)
+    store_back = pltpu.make_async_copy(back, back_out, store_sems.at[1])
+    store_back.start()
+    store_emb.wait()
+    store_back.wait()
 
 
 def exchange_scratch(units, width):
@@ -244,19 +439,30 @@
     ]
 
 
-def corr_grad(emb_a, emb_b, off_weight, row_count):
+def corr_grad(emb_a, emb_b, normed, inv_std, off_weight, shards, row_count):
     rows, width = emb_a.shape
     vmem = pl.BlockSpec(memory_space=pltpu.VMEM)
+    hbm = pl.BlockSpec(memory_space=pl.ANY)
     return pl.pallas_call(
-        functools.partial(corr_kernel, row_count),
-        out_shape=(jax.ShapeDtypeStruct((width, width), jnp.bfloat16), jax.ShapeDtypeStruct((8, width), jnp.float32)),
-        in_specs=[pl.BlockSpec(memory_space=pltpu.SMEM), vmem, vmem],
-        out_specs=(vmem, vmem),
-        scratch_shapes=exchange_scratch(width // 2 // UNIT, width),
+        functools.partial(corr_kernel, shards, row_count),
+        out_shape=(jax.ShapeDtypeStruct((rows, width), jnp.float32), jax.ShapeDtypeStruct((rows, width), jnp.bfloat16), jax.ShapeDtypeStruct((8, UNIT), jnp.float32)),
+        in_specs=[pl.BlockSpec(memory_space=pltpu.SMEM), vmem, vmem, vmem, hbm],
+        out_specs=(hbm, hbm, vmem),
+        scratch_shapes=[
+            pltpu.VMEM((width, width), jnp.bfloat16),
+            pltpu.VMEM((rows, width), jnp.float32),
+            pltpu.VMEM((rows, width), jnp.bfloat16),
+            pltpu.VMEM((2, 2, rows, UNIT), jnp.float32),
+            pltpu.VMEM((8, width), jnp.float32),
+            pltpu.VMEM((8, width), jnp.float32),
+            pltpu.VMEM((1, shards, 8, COLS + UNIT), jnp.float32),
+        ]
+        + exchange_scratch(width // 2 // UNIT, width)
+        + [pltpu.SemaphoreType.DMA((1, shards)), pltpu.SemaphoreType.DMA((1, shards)), pltpu.SemaphoreType.DMA((2, 2)), pltpu.SemaphoreType.DMA((2,))],
         compiler_params=pltpu.CompilerParams(collective_id=2, has_side_effects=True, vmem_limit_bytes=VMEM_LIMIT),
-        cost_estimate=pl.CostEstimate(flops=2 * rows * width * width, bytes_accessed=4 * width * width, transcendentals=0),
+        cost_estimate=pl.CostEstimate(flops=4 * rows * width * width, bytes_accessed=8 * width * width, transcendentals=0),
         name="corr_grad",
-    )(off_weight.reshape(1, 1), emb_a, emb_b)
+    )(off_weight.reshape(1, 1), inv_std, emb_a, emb_b, normed)
 
 
 DEPTH = 12
@@ -526,33 +732,15 @@
     def local_step(feat_a, feat_b, w_in, w_mid, w_out, t_in, t_mid, t_out, gain_1, bias_1, gain_2, bias_2, off_weight):
         row_count = feat_a.shape[0] * shards
 
-        def norm_pair(pre_a, pre_b):
-            stat_means = stats_all_reduce([jnp.sum(pre_a, axis=0), jnp.sum(pre_a * pre_a, axis=0), jnp.sum(pre_b, axis=0), jnp.sum(pre_b * pre_b, axis=0)], shards) / row_count
-            inv_a = lax.rsqrt(stat_means[1] - stat_means[0] * stat_means[0] + NORM_EPS)
-            inv_b = lax.rsqrt(stat_means[3] - stat_means[2] * stat_means[2] + NORM_EPS)
-            return (pre_a - stat_means[0]) * inv_a, inv_a, (pre_b - stat_means[2]) * inv_b
-
-        def hidden_pair(in_a, in_b, weight_a, weight_b, gain_vec, bias_vec):
-            normed_a, inv_a, normed_b = norm_pair(jnp.dot(in_a, weight_a, preferred_element_type=jnp.float32), jnp.dot(in_b, weight_b, preferred_element_type=jnp.float32))
-            pre_act = normed_a * gain_vec + bias_vec
-            act_a = jnp.maximum(pre_act, 0.0).astype(jnp.bfloat16)
-            act_b = jnp.maximum(normed_b * gain_vec + bias_vec, 0.0).astype(jnp.bfloat16)
-            return act_a, act_b, normed_a, inv_a
-
-        act_1, teach_1, normed_1, inv_1 = hidden_pair(feat_a, feat_b, w_in, t_in, gain_1, bias_1)
-        act_2, teach_2, normed_2, inv_2 = hidden_pair(act_1, teach_1, w_mid, t_mid, gain_2, bias_2)
-        zh_a, inv_z, zh_b = norm_pair(jnp.dot(act_2, w_out, preferred_element_type=jnp.float32), jnp.dot(teach_2, t_out, preferred_element_type=jnp.float32))
-        emb_a = zh_a.astype(jnp.bfloat16)
-        emb_b = zh_b.astype(jnp.bfloat16)
-        grad_c, loss_part = corr_grad(emb_a, emb_b, off_weight, row_count)
-        grad_emb = contract_cols(emb_b, grad_c) / row_count
-        stat_sums = stats_all_reduce([jnp.sum(grad_emb, axis=0), jnp.sum(grad_emb * zh_a, axis=0), jnp.sum(loss_part, axis=0)], shards)
-        loss_value = jnp.sum(stat_sums[2])
-        grad_z = ((grad_emb - stat_sums[0] / row_count - zh_a * (stat_sums[1] / row_count)) * inv_z).astype(jnp.bfloat16)
+        affine = jnp.stack([gain_1, bias_1, gain_2, bias_2])
+        act_1, act_2, normed_1, normed_2, zh_a, emb_a, emb_b, inv_std = forward_pass(feat_a, feat_b, w_in, t_in, w_mid, t_mid, w_out, t_out, affine, shards, row_count)
+        width = w_mid.shape[0]
+        inv_1, inv_2 = inv_std[:2, : width // COLS].reshape(2, width)
+        grad_emb, grad_z, loss_sums = corr_grad(emb_a, emb_b, zh_a, inv_std, off_weight, shards, row_count)
+        loss_value = jnp.sum(loss_sums)
         pad = jnp.zeros((5,) + gain_1.shape, jnp.float32)
         vecs = jnp.stack([jnp.concatenate([jnp.stack([gain_2, bias_2, inv_2]), pad]), jnp.concatenate([jnp.stack([gain_1, bias_1, inv_1]), pad])])
         sums, stats = backward(act_2, grad_z, w_out, normed_2, act_1, w_mid, normed_1, feat_a, vecs, shards, row_count)
-        width = w_mid.shape[0]
         return (loss_value, grad_emb, sums[2 * width :], sums[width : 2 * width], sums[:width], stats[1, 0], stats[1, 1], stats[0, 0], stats[0, 1])
 
     return jax.shard_map(local_step, mesh=mesh, in_specs=(row_part, row_part) + (replicated,) * 11, out_specs=(replicated, row_part) + (replicated,) * 7, check_vma=False)

time: 609 us -> 532 us (0.87)
  matrix products: 92 us -> 0 us
  Pallas kernels: 448 us -> 494 us
  other arithmetic: 32.1 us -> 3.43 us
    dot_general x7 -> x0, matrix products: 92 us -> none  [the longest x2 23.9 us: hidden_pair(): jnp.dot(in_b, weight_b, preferred_element_type=jnp.float32)]
    pallas_call x5 -> x2, Pallas kernels: 152 us -> 197 us  [the longest x1 127 us: corr_grad(): pl.pallas_call(functools.partial(corr_kernel, shards, row_count), out_sha...]
    convert_element_type x4 -> x0, other arithmetic: 27.1 us -> none  [the longest x1 9.27 us: local_step(): emb_b = zh_b.astype(jnp.bfloat16)]
where the time goes in v3:
time: 532 us
  Pallas kernels  494 us (93%)
  local copies, waits for them, and re-layouts  32.7 us (6%)
    pallas_call x1, Pallas kernels, backward(): pl.pallas_call(functools.partial(backward_kernel, shards, row_count), out...  297 us
    pallas_call x1, Pallas kernels, corr_grad(): pl.pallas_call(functools.partial(corr_kernel, shards, row_count), out_sha...  127 us
    pallas_call x1, Pallas kernels, forward_pass(): pl.pallas_call(functools.partial(forward_kernel, shards, row_count), out_...  69.8 us
    slice x1, local copies, waits for them, and re-layouts, local_step(): sums[:width]  22 us

profile of v3, /device:TPU:0, one launch (start us, length us, event | category | flops | bytes accessed | tf_op | source)
XLA Modules:
  0.0 531.5 jit_solution(2558026091099240194)
XLA Ops:
  1.3 0.1 pad.9.clone
  1.4 1.4 pad_maximum_fusion.1.affine
  2.8 69.8 %forward.1 = (bf16[1024,2048]{1,0:T(8,128)(2,1)}, bf16[1024,2048]{1,0:T(8,128)(2,1)}, f32[1024,2048]{1,0:T(8,128)}, f32[1024,2048]{1,0:T(8,128)}, f32[1024,2048]...) custom-call(bf16[1024,512]{1,0:T(8,128)(2,1)} %feat.1, ...), custom_call_target="tpu_custom_call" | custom-call | flops 38654705664 | bytes 100663296 | tf_op jit(solution)/shard_map/forward/pallas_call | solution.py:168
  72.6 0.0 copy-start
  72.6 0.0 copy-start.1
  72.6 0.0 copy-start.2
  72.6 0.0 copy-start.3
  72.7 127.0 %corr_grad.1 = (f32[1024,2048]{1,0:T(8,128)}, bf16[1024,2048]{1,0:T(8,128)(2,1)}, f32[8,128]{1,0:T(8,128)}) custom-call(f32[1,1]{1,0:T(1,128)} %bitcast.19.off_ref, f32[3,8,512]{2,1,0:T(8,128)} %get-tuple-element.22.inv_ref, bf16[1024,2048]{1,0:T(8,128)(2,1)} %get-tuple-element.23.left_ref, bf16[1024,2048]{1,0:T(8,128)(2,1)} %get-tuple-element.24.right_ref, ...), custom_call_target="tpu_custom_call" | custom-call | flops 17179869184 | bytes 33554432 | tf_op jit(solution)/shard_map/corr_grad/pallas_call | solution.py:446
  199.7 0.7 slice_bitcast_fusion.1
  200.5 1.3 reduce_sum.9
  201.8 0.0 copy-done
  201.8 0.0 copy-done.1
  201.8 0.0 copy-done.2
  201.8 0.0 copy-done.3
  201.8 0.1 maximum_bitcast_fusion
  201.9 0.7 pad_maximum_fusion.vecs
  202.5 297.1 %backward.1 = (f32[4608,2048]{1,0:T(8,128)}, f32[2,8,2048]{2,1,0:T(8,128)}) custom-call(bf16[1024,2048]{1,0:T(8,128)(2,1)} %get-tuple-element.28.left_2, bf16[1024,2048]{1,0:T(8,128)(2,1)} %get-tuple-element.29.grad_z, bf16[2048,2048]{1,0:T(8,128)(2,1)} %w_out.3, f32[1024,2048]{1,0:T(8,128)} %get-tuple-element.30.normed_2, ...), custom_call_target="tpu_custom_call" | custom-call | flops 36507222016 | bytes 67108864 | tf_op jit(solution)/shard_map/backward/pallas_call | solution.py:694
  499.7 1.6 fusion.1
  501.2 0.0 slice-start
  501.2 4.8 slice.26
  506.1 0.0 slice-start.1
  506.1 22.0 %fusion = (f32[2048,2048]{1,0:T(8,128)}, f32[2048,2048]{1,0:T(8,128)}) fusion(f32[4608,2048]{1,0:T(8,128)} %get-tuple-element.33), kind=kLoop, calls=%fused_computation.6 | loop fusion | bytes 67108864 | tf_op jit(solution)/shard_map/slice | solution.py:744
  528.1 0.0 slice-done
  528.1 0.0 slice-done.1
  528.1 3.4 copy.26
  (4 shorter events, 0.0 us)
Async XLA Ops:
  72.6 129.2 %copy-start = (f32[2048]{0:T(1024)S(1)}, f32[2048]{0:T(1024)}, u32[]{:S(2)}) copy-start(f32[2048]{0:T(1024)} %param.24) | copy-start | bytes 24580
  72.6 129.2 %copy-start.1 = (f32[2048]{0:T(1024)S(1)}, f32[2048]{0:T(1024)}, u32[]{:S(2)}) copy-start(f32[2048]{0:T(1024)} %param.23) | copy-start | bytes 24580
  72.6 129.1 %copy-start.2 = (f32[2048]{0:T(1024)S(1)}, f32[2048]{0:T(1024)}, u32[]{:S(2)}) copy-start(f32[2048]{0:T(1024)} %param.22) | copy-start | bytes 24580
  72.6 129.1 %copy-start.3 = (f32[2048]{0:T(1024)S(1)}, f32[2048]{0:T(1024)}, u32[]{:S(2)}) copy-start(f32[2048]{0:T(1024)} %param.21) | copy-start | bytes 24580
  501.2 26.9 %slice-start = ((s8[8388608]{0:T(1024)(128)(4,1)}), s8[4194304]{0:T(1024)(128)(4,1)S(1)}, s32[]{:S(2)}) async-start(s8[8388608]{0:T(1024)(128)(4,1)} %bitcast.20), calls=%async_computation | async-start | bytes 8388608
  506.1 22.0 %slice-start.1 = ((s8[8388608]{0:T(1024)(128)(4,1)}), s8[4194304]{0:T(1024)(128)(4,1)S(1)}, s32[]{:S(2)}) async-start(s8[8388608]{0:T(1024)(128)(4,1)} %bitcast.20), calls=%async_computation.1 | async-start | bytes 8388608

commit v4 on v3

--- a/solution.py
+++ b/solution.py
@@ -59,10 +59,10 @@
 
 
 COLS = 512
-ROWS = 256
-
-
-def forward_kernel(shards, row_count, feat_a, feat_b, w_in, t_in, w_mid, t_mid, w_out, t_out, affine, act_1, act_2, normed_1, normed_2, normed_z, emb_a, emb_b, inv_ref, pre, act, feat, weight_in, weight, slots, sums, send_sems, recv_sems, load_sems, store_sems):
+ROWS = 1024
+
+
+def forward_kernel(shards, row_count, feat_a, feat_b, w_in, t_in, w_mid, t_mid, w_out, t_out, gain_1, bias_1, gain_2, bias_2, act_1, act_2, normed_1, normed_2, normed_z, emb_a, emb_b, inv_ref, pre, act, feat, weight_in, weight, slots, sums, send_sems, recv_sems, load_sems, store_sems):
     me = lax.axis_index(DATA_AXIS)
     rows, width = act_1.shape
     groups = width // COLS
@@ -109,7 +109,8 @@
                 if keep is not None:
                     source[part, cols] = out
                 if layer < 2:
-                    out = jnp.maximum(out * affine[2 * layer : 2 * layer + 1, cols] + affine[2 * layer + 1 : 2 * layer + 2, cols], 0.0)
+                    gain, bias = ((gain_1, bias_1), (gain_2, bias_2))[layer]
+                    out = jnp.maximum(out * gain[:, cols] + bias[:, cols], 0.0)
                 target[part, cols] = out.astype(jnp.bfloat16)
             return carry
 
@@ -157,7 +158,7 @@
         copy.wait()
 
 
-def forward_pass(feat_a, feat_b, w_in, t_in, w_mid, t_mid, w_out, t_out, affine, shards, row_count):
+def forward_pass(feat_a, feat_b, w_in, t_in, w_mid, t_mid, w_out, t_out, vectors, shards, row_count):
     rows, feat_dim = feat_a.shape
     width = w_mid.shape[0]
     groups = width // COLS
@@ -168,7 +169,7 @@
     return pl.pallas_call(
         functools.partial(forward_kernel, shards, row_count),
         out_shape=(half_out, half_out, full_out, full_out, full_out, half_out, half_out, jax.ShapeDtypeStruct((3, 8, COLS), jnp.float32)),
-        in_specs=[hbm] * 8 + [vmem],
+        in_specs=[hbm] * 8 + [vmem] * 4,
         out_specs=(hbm,) * 7 + (vmem,),
         scratch_shapes=[
             pltpu.VMEM((3, rows, width), jnp.float32),
@@ -186,7 +187,7 @@
         compiler_params=pltpu.CompilerParams(collective_id=4, has_side_effects=True, vmem_limit_bytes=VMEM_LIMIT),
         cost_estimate=pl.CostEstimate(flops=4 * rows * width * (2 * width + feat_dim), bytes_accessed=24 * width * width, transcendentals=0),
         name="forward",
-    )(feat_a, feat_b, w_in, t_in, w_mid, t_mid, w_out, t_out, affine)
+    )(feat_a, feat_b, w_in, t_in, w_mid, t_mid, w_out, t_out, *vectors)
 
 
 PAIR, RS1, RS2, RS3, AG3, AG2, AG1, AGP, LOCAL = range(9)
@@ -220,11 +221,11 @@
         if kind == PAIR:
             src, dst, peer = self.halves.at[lax.rem(unit, self.ring)], self.recv_pair.at[slot], partner
         elif kind == RS1:
-            src, dst, peer = total.at[rows((1 - b1) * 64, 64)], self.recv_1.at[slot], p1
+            src, dst, peer = total.at[rows((1 - b1) * 64, 64)], self.recv_1.at[lax.rem(unit, self.recv_1.shape[0])], p1
         elif kind == RS2:
-            src, dst, peer = total.at[rows(b1 * 64 + (1 - b2) * 32, 32)], self.recv_2.at[slot], p2
+            src, dst, peer = total.at[rows(b1 * 64 + (1 - b2) * 32, 32)], self.recv_2.at[lax.rem(unit, self.recv_2.shape[0])], p2
         elif kind == RS3:
-            src, dst, peer = total.at[rows(b1 * 64 + b2 * 32 + (1 - b3) * 16, 16)], self.recv_3.at[slot], p3
+            src, dst, peer = total.at[rows(b1 * 64 + b2 * 32 + (1 - b3) * 16, 16)], self.recv_3.at[lax.rem(unit, self.recv_3.shape[0])], p3
         else:
             start, size, peer = {
                 AG3: (b1 * 64 + b2 * 32 + b3 * 16, 16, p3),
@@ -248,7 +249,7 @@
             start, size, landed = b1 * 64 + b2 * 32, 32, self.recv_2
         keep = pl.ds(pl.multiple_of(start, 16), size)
         slot = lax.rem(unit, self.depth)
-        self.total[slot, keep] = self.total[slot, keep] + landed[slot]
+        self.total[slot, keep] = self.total[slot, keep] + landed[lax.rem(unit, landed.shape[0])]
         self.copy(unit, kind + 1).start()
 
     def owned(self, unit):
@@ -288,7 +289,7 @@
 
 
 RING = 3
-CORR_LAGS = (0, 1, 4, 6, 8, 10, 13, 17, 18)
+CORR_LAGS = (0, 1, 4, 6, 9, 12, 15, 18, 20)
 
 
 def corr_kernel(shards, row_count, off_ref, inv_ref, left_ref, right_ref, normed, emb_out, back_out, loss_ref, grad_ref, emb_grad, back, norm_in, loss_acc, wide, slots, halves, recv_pair, recv_1, recv_2, recv_3, total, send_sems, recv_sems, sum_send, sum_recv, norm_sems, store_sems):
@@ -394,7 +395,7 @@
     for copy in load_block(0, 0) + load_block(1, 1):
         copy.start()
     summed = sums.finish(0)
-    loss_ref[...] = summed[:, COLS:]
+    loss_ref[0, 0] = jnp.sum(summed[:, COLS:])
     means = summed[:, :COLS] / row_count
     for index in range(groups):
         cols = pl.ds(index * COLS, COLS)
@@ -445,9 +446,9 @@
     hbm = pl.BlockSpec(memory_space=pl.ANY)
     return pl.pallas_call(
         functools.partial(corr_kernel, shards, row_count),
-        out_shape=(jax.ShapeDtypeStruct((rows, width), jnp.float32), jax.ShapeDtypeStruct((rows, width), jnp.bfloat16), jax.ShapeDtypeStruct((8, UNIT), jnp.float32)),
+        out_shape=(jax.ShapeDtypeStruct((rows, width), jnp.float32), jax.ShapeDtypeStruct((rows, width), jnp.bfloat16), jax.ShapeDtypeStruct((1, 1), jnp.float32)),
         in_specs=[pl.BlockSpec(memory_space=pltpu.SMEM), vmem, vmem, vmem, hbm],
-        out_specs=(hbm, hbm, vmem),
+        out_specs=(hbm, hbm, pl.BlockSpec(memory_space=pltpu.SMEM)),
         scratch_shapes=[
             pltpu.VMEM((width, width), jnp.bfloat16),
             pltpu.VMEM((rows, width), jnp.float32),
@@ -465,46 +466,73 @@
     )(off_weight.reshape(1, 1), inv_std, emb_a, emb_b, normed)
 
 
-DEPTH = 12
-PERIOD = 12
+DEPTH = 18
+DEPTH_1, DEPTH_2, DEPTH_3 = 15, 9, 6
+CHAIN = 6
+PER_TICK = 2
 BLOCK = 256
-BACK_LAGS = (1, 4, 6, 7, 9, 12, 15, 16)
-
-
-def backward_kernel(shards, row_count, left_2, grad_z, w_out, normed_2, left_1, w_mid, normed_1, feat, vecs, out_ref, stat_ref, left, feat_in, grad, weight, normed, deriv, halves, mine, total, recv_1, recv_2, recv_3, stat_part, stat_in, send_sems, recv_sems, load_sems, weight_sems, normed_sems, stat_sems):
+NORM_SLOTS = 3
+WEIGHT_SLOTS = 3
+BACK_LAGS = (1, 4, 6, 7, 9, 12, 16, 18)
+
+
+def backward_kernel(shards, row_count, left_2, grad_z, w_out, normed_2, left_1, w_mid, normed_1, feat, gain_1, bias_1, gain_2, bias_2, inv_ref, out_ref, stat_ref, vecs, left, feat_in, grad, weight, normed, deriv, halves, mine, total, recv_1, recv_2, recv_3, wide, slots, send_sems, recv_sems, load_sems, weight_sems, normed_sems, sum_send, sum_recv):
     me = lax.axis_index(DATA_AXIS)
     _, half = flip(me, 1)
     rows, width = left.shape
+    groups = width // COLS
     blocks = width // BLOCK
     units_full = width // 2 // UNIT
     units_last = feat_in.shape[1] // 2 // UNIT
-    enters = 2 * PERIOD + units_last
-    ticks = enters + max(BACK_LAGS)
+    units = 2 * units_full + units_last
+    ticks = units + max(BACK_LAGS)
 
     load_left = pltpu.make_async_copy(left_2, left, load_sems.at[0])
-    load_grad = pltpu.make_async_copy(grad_z, grad, load_sems.at[1])
+    load_grad = pltpu.make_async_copy(grad_z, grad.at[0], load_sems.at[1])
     load_feat = pltpu.make_async_copy(feat, feat_in, load_sems.at[2])
 
     def block_of(index):
         return pl.ds(pl.multiple_of(index * BLOCK, BLOCK), BLOCK)
 
-    def load_weight(source, index):
-        return pltpu.make_async_copy(source.at[block_of(index)], weight.at[block_of(index)], weight_sems.at[index])
-
-    def load_normed(source, index):
-        return pltpu.make_async_copy(source.at[:, block_of(index)], normed.at[:, block_of(index)], normed_sems.at[index])
+    def weight_copy(source, number):
+        slot = lax.rem(number, WEIGHT_SLOTS)
+        return pltpu.make_async_copy(source.at[block_of(lax.rem(number, blocks))], weight.at[slot], weight_sems.at[slot])
+
+    def weight_start(number):
+        @pl.when(number < blocks)
+        def _():
+            weight_copy(w_out, number).start()
+
+        @pl.when((number >= blocks) & (number < 2 * blocks))
+        def _():
+            weight_copy(w_mid, number).start()
+
+    def normed_copy(source, number):
+        slot = lax.rem(number, NORM_SLOTS)
+        return pltpu.make_async_copy(source.at[:, block_of(lax.rem(number, blocks))], normed.at[slot], normed_sems.at[slot])
+
+    def normed_start(number):
+        @pl.when(number < 2 * blocks)
+        def _():
+            normed_copy(normed_2, number).start()
+
+        @pl.when((number >= 2 * blocks) & (number < 4 * blocks))
+        def _():
+            normed_copy(normed_1, number).start()
 
     load_left.start()
     load_grad.start()
-    for index in range(blocks):
-        load_weight(w_out, index).start()
-        load_normed(normed_2, index).start()
+    for number in range(WEIGHT_SLOTS):
+        weight_copy(w_out, number).start()
+    for number in range(NORM_SLOTS):
+        normed_copy(normed_2, number).start()
     load_feat.start()
-
-    barrier = pltpu.get_barrier_semaphore()
-    for shift in range(1, shards):
-        pl.semaphore_signal(barrier, inc=1, device_id=(lax.rem(me + shift, shards),), device_id_type=MESH_ID)
-    pl.semaphore_wait(barrier, shards - 1)
+    for layer, (gain, bias) in enumerate(((gain_2, bias_2), (gain_1, bias_1))):
+        vecs[layer, 0:1] = gain[...]
+        vecs[layer, 1:2] = bias[...]
+        for index in range(groups):
+            vecs[layer, 2:3, index * COLS : (index + 1) * COLS] = inv_ref[1 - layer, index : index + 1]
+    enter_all(me, shards)
 
     def row_of(unit, h):
         layer = lax.div(unit, units_full)
@@ -512,12 +540,14 @@
         return layer * width + h * part + lax.rem(unit, units_full) * UNIT
 
     ex = Exchange(me, 2, halves, out_ref, total, recv_1, recv_2, recv_3, total, send_sems, recv_sems, row_of, DEPTH, send_total=True)
+    sums = SumExchange(me, shards, slots, sum_send, sum_recv)
 
     def produce(unit, source, part):
         @pl.when(unit >= 2)
         def _():
             ex.copy(unit - 2, PAIR).wait_send()
 
+        which = lax.rem(lax.div(unit, units_full), 2)
         local = lax.rem(unit, units_full) * UNIT
         ring = lax.rem(unit, 2)
         col_other, col_mine = (1 - half) * part + local, half * part + local
@@ -525,7 +555,7 @@
         chunk = width // 4
         for index in range(4):
             cols = pl.ds(index * chunk, chunk)
-            prod = contract_rows(lhs, grad[:, cols])
+            prod = contract_rows(lhs, grad[which, :, cols])
             halves[ring, :, cols] = prod[:UNIT]
             mine[ring, :, cols] = prod[UNIT:]
         ex.copy(unit, PAIR).start()
@@ -545,7 +575,7 @@
         ex.copy(unit, RS3).wait()
         slot = lax.rem(unit, DEPTH)
         keep = pl.ds(pl.multiple_of(ex.owned(unit), 16), 16)
-        total[slot, keep] = total[slot, keep] + recv_3[slot]
+        total[slot, keep] = total[slot, keep] + recv_3[lax.rem(unit, DEPTH_3)]
         to_out(unit).start()
         ex.copy(unit, AG3).start()
 
@@ -562,130 +592,118 @@
     stages = [pair_step, lambda u: ex.reduce_step(u, RS1), lambda u: ex.reduce_step(u, RS2), finish, forward(AG3), forward(AG2), forward(AG1), forward(AGP)]
 
     def derivative(layer, index):
-        load_weight(w_out, index).wait()
-        load_normed(normed_2, index).wait()
+        number = layer * blocks + index
+        stream = 2 * layer * blocks + index
+        weight_copy(w_out, number).wait()
+        normed_copy(normed_2, stream).wait()
+        slot, weight_slot = lax.rem(stream, NORM_SLOTS), lax.rem(number, WEIGHT_SLOTS)
         cols = block_of(index)
         gain, bias = vecs[layer, 0:1, cols], vecs[layer, 1:2, cols]
-        rhs = weight[cols]
+        rhs = weight[weight_slot]
         sum_n = jnp.zeros((1, BLOCK), jnp.float32)
         sum_d = jnp.zeros((1, BLOCK), jnp.float32)
         for chunk in range(rows // BLOCK):
             part = pl.ds(chunk * BLOCK, BLOCK)
-            n = normed[part, cols]
-            d = jnp.where(n * gain + bias > 0.0, contract_cols(grad[part], rhs), 0.0)
+            n = normed[slot, part]
+            d = jnp.where(n * gain + bias > 0.0, contract_cols(grad[layer, part], rhs), 0.0)
             deriv[part, cols] = d
             sum_n = sum_n + jnp.sum(d * n, axis=0, keepdims=True)
             sum_d = sum_d + jnp.sum(d, axis=0, keepdims=True)
-        stat_part[layer, 0:1, cols] = sum_n
-        stat_part[layer, 1:2, cols] = sum_d
-
-    lanes = width // shards
-
-    def lane_block(index):
-        return pl.ds(pl.multiple_of(index * lanes, lanes), lanes)
-
-    def stat_scatter(layer, shift):
-        peer = lax.rem(me + shift, shards)
-        return pltpu.make_async_remote_copy(src_ref=stat_part.at[layer, :, lane_block(peer)], dst_ref=stat_in.at[layer, shift], send_sem=stat_sems.at[0, layer, shift], recv_sem=stat_sems.at[1, layer, shift], device_id=(peer,), device_id_type=MESH_ID)
-
-    def stat_gather(layer, shift):
-        peer = lax.rem(me + shift, shards)
-        return pltpu.make_async_remote_copy(src_ref=stat_in.at[layer, 0], dst_ref=stat_ref.at[layer, :, lane_block(me)], send_sem=stat_sems.at[2, layer, shift], recv_sem=stat_sems.at[3, layer, shift], device_id=(peer,), device_id_type=MESH_ID)
-
-    def stat_send(layer):
-        for shift in range(1, shards):
-            stat_scatter(layer, shift).start()
-
-    def stat_reduce(layer):
-        summed = stat_part[layer, :, lane_block(me)]
-        for shift in range(1, shards):
-            stat_scatter(layer, shift).wait()
-            summed = summed + stat_in[layer, shift]
-        stat_in[layer, 0] = summed
-        stat_ref[layer, :, lane_block(me)] = summed
-        for shift in range(1, shards):
-            stat_gather(layer, shift).start()
+        wide[0:1, cols] = sum_n
+        wide[1:2, cols] = sum_d
+        weight_start(number + WEIGHT_SLOTS)
+        normed_start(stream + NORM_SLOTS)
+
+    def send_sums(layer):
+        for index in range(groups):
+            cols = pl.ds(index * COLS, COLS)
+            slots[layer, me, index : index + 1] = wide[0:1, cols]
+            slots[layer, me, groups + index : groups + index + 1] = wide[1:2, cols]
+        sums.start(layer)
 
     def next_grad(layer):
-        for shift in range(1, shards):
-            stat_gather(layer, shift).wait()
+        summed = sums.finish(layer)
+        for index in range(groups):
+            cols = pl.ds(index * COLS, COLS)
+            for row in range(2):
+                line = summed[row * groups + index : row * groups + index + 1]
+                stat_ref[layer, row : row + 1, cols] = line
+                wide[2 + row : 3 + row, cols] = line / row_count
 
         def one(index, carry):
+            stream = (2 * layer + 1) * blocks + index
+            normed_copy(normed_2, stream).wait()
+            slot = lax.rem(stream, NORM_SLOTS)
             cols = block_of(index)
-            mean_n = stat_ref[layer, 0:1, cols] / row_count
-            mean_d = stat_ref[layer, 1:2, cols] / row_count
+            mean_n, mean_d = wide[2:3, cols], wide[3:4, cols]
             scale = vecs[layer, 0:1, cols] * vecs[layer, 2:3, cols]
             for chunk in range(rows // BLOCK):
                 part = pl.ds(chunk * BLOCK, BLOCK)
-                grad[part, cols] = ((deriv[part, cols] - mean_d - normed[part, cols] * mean_n) * scale).astype(jnp.bfloat16)
-
-            @pl.when(layer == 0)
-            def _():
-                load_normed(normed_1, index).start()
-
+                grad[1 - layer, part, cols] = ((deriv[part, cols] - mean_d - normed[slot, part] * mean_n) * scale).astype(jnp.bfloat16)
+            normed_start(stream + NORM_SLOTS)
             return carry
 
         lax.fori_loop(0, blocks, one, 0)
-
-    stat_part[...] = jnp.zeros_like(stat_part)
 
     def tick(now, carry):
         for lag, stage in reversed(list(zip(BACK_LAGS, stages))):
-            entered = now - lag
-            layer, place = lax.div(entered, PERIOD), lax.rem(entered, PERIOD)
-
-            @pl.when((entered >= 0) & (entered < enters) & (place < units_full))
-            def _(stage=stage, layer=layer, place=place):
-                stage(layer * units_full + place)
-
-        layer, place = lax.div(now, PERIOD), lax.rem(now, PERIOD)
-
-        @pl.when((layer < 2) & (place < units_full))
-        def _():
-            @pl.when(place == 0)
+            unit = now - lag
+
+            @pl.when((unit >= 0) & (unit < units))
+            def _(stage=stage, unit=unit):
+                stage(unit)
+
+        @pl.when(now < 2 * units_full)
+        def _():
+            @pl.when(lax.rem(now, units_full) == 0)
             def _():
                 load_left.wait()
 
-                @pl.when(layer == 0)
+                @pl.when(now == 0)
                 def _():
                     load_grad.wait()
 
-            produce(layer * units_full + place, left, width // 2)
-            derivative(layer, place)
-
-        @pl.when((now >= 2 * PERIOD) & (now < enters))
-        def _():
-            @pl.when(place == 0)
+            produce(now, left, width // 2)
+
+            @pl.when(now == units_full - 1)
+            def _():
+                pltpu.make_async_copy(left_1, left, load_sems.at[0]).start()
+
+        @pl.when((now >= 2 * units_full) & (now < units))
+        def _():
+            @pl.when(now == 2 * units_full)
             def _():
                 load_feat.wait()
 
-            produce(layer * units_full + place, feat_in, feat_in.shape[1] // 2)
-
-        @pl.when((layer < 2) & (place == units_full))
-        def _():
-            stat_send(layer)
-
-            @pl.when(layer == 0)
+            produce(now, feat_in, feat_in.shape[1] // 2)
+
+        layer, place = lax.div(now, CHAIN), lax.rem(now, CHAIN)
+        steps = blocks // PER_TICK
+
+        @pl.when((layer < 2) & (place < steps))
+        def _():
+            def one(index, carry):
+                derivative(layer, place * PER_TICK + index)
+                return carry
+
+            lax.fori_loop(0, PER_TICK, one, 0)
+
+            @pl.when(place == steps - 1)
             def _():
-                pltpu.make_async_copy(left_1, left, load_sems.at[0]).start()
-                for index in range(blocks):
-                    load_weight(w_mid, index).start()
-
-            stat_reduce(layer)
-
-        @pl.when((layer < 2) & (place == units_full + 3))
+                send_sums(layer)
+
+        @pl.when((layer < 2) & (place == CHAIN - 1))
         def _():
             next_grad(layer)
 
         return carry
 
     lax.fori_loop(0, ticks, tick, 0)
-    last = 2 * units_full + units_last
-    for unit in (last - 2, last - 1):
+    for unit in (units - 2, units - 1):
         ex.copy(unit, PAIR).wait_send()
 
 
-def backward(act_2, grad_z, w_out, normed_2, act_1, w_mid, normed_1, feat, vecs, shards, row_count):
+def backward(act_2, grad_z, w_out, normed_2, act_1, w_mid, normed_1, feat, vectors, inv_std, shards, row_count):
     rows, width = act_2.shape
     feat_dim = feat.shape[1]
     total_rows = 2 * width + feat_dim
@@ -693,35 +711,82 @@
     hbm = pl.BlockSpec(memory_space=pl.ANY)
     return pl.pallas_call(
         functools.partial(backward_kernel, shards, row_count),
-        out_shape=(jax.ShapeDtypeStruct((total_rows, width), jnp.float32), jax.ShapeDtypeStruct((2, 8, width), jnp.float32)),
-        in_specs=[hbm] * 8 + [vmem],
+        out_shape=(jax.ShapeDtypeStruct((total_rows, width), jnp.float32), jax.ShapeDtypeStruct((2, 2, width), jnp.float32)),
+        in_specs=[hbm] * 8 + [vmem] * 5,
         out_specs=(hbm, vmem),
         scratch_shapes=[
+            pltpu.VMEM((2, 8, width), jnp.float32),
             pltpu.VMEM((rows, width), jnp.bfloat16),
             pltpu.VMEM((rows, feat_dim), jnp.bfloat16),
-            pltpu.VMEM((rows, width), jnp.bfloat16),
-            pltpu.VMEM((width, width), jnp.bfloat16),
-            pltpu.VMEM((rows, width), jnp.float32),
+            pltpu.VMEM((2, rows, width), jnp.bfloat16),
+            pltpu.VMEM((WEIGHT_SLOTS, BLOCK, width), jnp.bfloat16),
+            pltpu.VMEM((NORM_SLOTS, rows, BLOCK), jnp.float32),
             pltpu.VMEM((rows, width), jnp.float32),
             pltpu.VMEM((2, UNIT, width), jnp.float32),
             pltpu.VMEM((2, UNIT, width), jnp.float32),
             pltpu.VMEM((DEPTH, UNIT, width), jnp.float32),
-            pltpu.VMEM((DEPTH, 64, width), jnp.float32),
-            pltpu.VMEM((DEPTH, 32, width), jnp.float32),
-            pltpu.VMEM((DEPTH, 16, width), jnp.float32),
-            pltpu.VMEM((2, 8, width), jnp.float32),
-            pltpu.VMEM((2, shards, 8, width // shards), jnp.float32),
+            pltpu.VMEM((DEPTH_1, 64, width), jnp.float32),
+            pltpu.VMEM((DEPTH_2, 32, width), jnp.float32),
+            pltpu.VMEM((DEPTH_3, 16, width), jnp.float32),
+            pltpu.VMEM((8, width), jnp.float32),
+            pltpu.VMEM((2, shards, 8, COLS), jnp.float32),
             pltpu.SemaphoreType.DMA((DEPTH, 9)),
             pltpu.SemaphoreType.DMA((DEPTH, 9)),
             pltpu.SemaphoreType.DMA((3,)),
-            pltpu.SemaphoreType.DMA((width // BLOCK,)),
-            pltpu.SemaphoreType.DMA((width // BLOCK,)),
-            pltpu.SemaphoreType.DMA((4, 2, shards)),
+            pltpu.SemaphoreType.DMA((WEIGHT_SLOTS,)),
+            pltpu.SemaphoreType.DMA((NORM_SLOTS,)),
+            pltpu.SemaphoreType.DMA((2, shards)),
+            pltpu.SemaphoreType.DMA((2, shards)),
         ],
         compiler_params=pltpu.CompilerParams(collective_id=3, has_side_effects=True, vmem_limit_bytes=VMEM_LIMIT),
         cost_estimate=pl.CostEstimate(flops=2 * rows * width * (2 * width + total_rows), bytes_accessed=16 * width * width, transcendentals=0),
         name="backward",
-    )(act_2, grad_z, w_out, normed_2, act_1, w_mid, normed_1, feat, vecs)
+    )(act_2, grad_z, w_out, normed_2, act_1, w_mid, normed_1, feat, *vectors, inv_std)
+
+
+CHUNK = 256
+FLIGHT = 8
+
+
+def output_kernel(sums_ref, emb_ref, stat_ref, emb_out, in_out, mid_out, last_out, gain_1, bias_1, gain_2, bias_2, buffer, read_sems, write_sems):
+    width = mid_out.shape[0]
+    reads, writes = [], []
+    for source, first, target in ((sums_ref, 0, last_out), (sums_ref, width, mid_out), (sums_ref, 2 * width, in_out), (emb_ref, 0, emb_out)):
+        for start in range(0, target.shape[0], CHUNK):
+            slot = len(reads) % FLIGHT
+            reads.append(pltpu.make_async_copy(source.at[pl.ds(first + start, CHUNK)], buffer.at[slot], read_sems.at[slot]))
+            writes.append(pltpu.make_async_copy(buffer.at[slot], target.at[pl.ds(start, CHUNK)], write_sems.at[slot]))
+    for copy in reads[:FLIGHT]:
+        copy.start()
+    gain_1[...] = stat_ref[1, 0:1]
+    bias_1[...] = stat_ref[1, 1:2]
+    gain_2[...] = stat_ref[0, 0:1]
+    bias_2[...] = stat_ref[0, 1:2]
+    behind = FLIGHT // 2
+    for index in range(len(reads) + behind):
+        if index < len(reads):
+            reads[index].wait()
+            writes[index].start()
+        if index >= behind:
+            writes[index - behind].wait()
+            if index - behind + FLIGHT < len(reads):
+                reads[index - behind + FLIGHT].start()
+
+
+def to_outputs(sums, emb_grad, stats, width):
+    feat_dim = sums.shape[0] - 2 * width
+    vmem = pl.BlockSpec(memory_space=pltpu.VMEM)
+    hbm = pl.BlockSpec(memory_space=pl.ANY)
+    row = jax.ShapeDtypeStruct((1, width), jnp.float32)
+    return pl.pallas_call(
+        output_kernel,
+        out_shape=(jax.ShapeDtypeStruct(emb_grad.shape, jnp.float32), jax.ShapeDtypeStruct((feat_dim, width), jnp.float32), jax.ShapeDtypeStruct((width, width), jnp.float32), jax.ShapeDtypeStruct((width, width), jnp.float32)) + (row,) * 4,
+        in_specs=[hbm, hbm, vmem],
+        out_specs=(hbm,) * 4 + (vmem,) * 4,
+        scratch_shapes=[pltpu.VMEM((FLIGHT, CHUNK, width), jnp.float32), pltpu.SemaphoreType.DMA((FLIGHT,)), pltpu.SemaphoreType.DMA((FLIGHT,))],
+        compiler_params=pltpu.CompilerParams(vmem_limit_bytes=VMEM_LIMIT),
+        name="to_outputs",
+    )(sums, emb_grad, stats)
 
 
 def solution(mesh):
@@ -732,15 +797,13 @@
     def local_step(feat_a, feat_b, w_in, w_mid, w_out, t_in, t_mid, t_out, gain_1, bias_1, gain_2, bias_2, off_weight):
         row_count = feat_a.shape[0] * shards
 
-        affine = jnp.stack([gain_1, bias_1, gain_2, bias_2])
-        act_1, act_2, normed_1, normed_2, zh_a, emb_a, emb_b, inv_std = forward_pass(feat_a, feat_b, w_in, t_in, w_mid, t_mid, w_out, t_out, affine, shards, row_count)
+        vectors = [vector.reshape(1, -1) for vector in (gain_1, bias_1, gain_2, bias_2)]
+        act_1, act_2, normed_1, normed_2, zh_a, emb_a, emb_b, inv_std = forward_pass(feat_a, feat_b, w_in, t_in, w_mid, t_mid, w_out, t_out, vectors, shards, row_count)
         width = w_mid.shape[0]
-        inv_1, inv_2 = inv_std[:2, : width // COLS].reshape(2, width)
         grad_emb, grad_z, loss_sums = corr_grad(emb_a, emb_b, zh_a, inv_std, off_weight, shards, row_count)
-        loss_value = jnp.sum(loss_sums)
-        pad = jnp.zeros((5,) + gain_1.shape, jnp.float32)
-        vecs = jnp.stack([jnp.concatenate([jnp.stack([gain_2, bias_2, inv_2]), pad]), jnp.concatenate([jnp.stack([gain_1, bias_1, inv_1]), pad])])
-        sums, stats = backward(act_2, grad_z, w_out, normed_2, act_1, w_mid, normed_1, feat_a, vecs, shards, row_count)
-        return (loss_value, grad_emb, sums[2 * width :], sums[width : 2 * width], sums[:width], stats[1, 0], stats[1, 1], stats[0, 0], stats[0, 1])
+        loss_value = loss_sums[0, 0]
+        sums, stats = backward(act_2, grad_z, w_out, normed_2, act_1, w_mid, normed_1, feat_a, vectors, inv_std, shards, row_count)
+        grad_emb, grad_in, grad_mid, grad_out, *vector_grads = to_outputs(sums, grad_emb, stats, width)
+        return (loss_value, grad_emb, grad_in, grad_mid, grad_out, *[vector.reshape(-1) for vector in vector_grads])
 
     return jax.shard_map(local_step, mesh=mesh, in_specs=(row_part, row_part) + (replicated,) * 11, out_specs=(replicated, row_part) + (replicated,) * 7, check_vma=False)

time: 532 us -> 491 us (0.923)
  local copies, waits for them, and re-layouts: 32.7 us -> 0 us
  Pallas kernels: 494 us -> 487 us
    pallas_call x0 -> x1, Pallas kernels: none -> 32.2 us  [to_outputs(): pl.pallas_call(output_kernel, out_shape=(jax.ShapeDtypeStruct(emb_grad.sh...]
    pallas_call x1, Pallas kernels: 297 us -> 268 us  [backward(): pl.pallas_call(functools.partial(backward_kernel, shards, row_count), out...]
    slice x3 -> x0, local copies, waits for them, and re-layouts: 28.4 us -> none  [the longest x1 22 us: local_step(): sums[:width]]
    pallas_call x1, Pallas kernels: 127 us -> 119 us  [corr_grad(): pl.pallas_call(functools.partial(corr_kernel, shards, row_count), out_sha...]
where the time goes in v4:
time: 491 us; the launch traced here: 490 us
  Pallas kernels  487 us (99%)
    pallas_call x1, Pallas kernels, backward(): pl.pallas_call(functools.partial(backward_kernel, shards, row_count), out...  268 us
    pallas_call x1, Pallas kernels, corr_grad(): pl.pallas_call(functools.partial(corr_kernel, shards, row_count), out_sha...  119 us
    pallas_call x1, Pallas kernels, forward_pass(): pl.pallas_call(functools.partial(forward_kernel, shards, row_count), out_...  68.4 us
    pallas_call x1, Pallas kernels, to_outputs(): pl.pallas_call(output_kernel, out_shape=(jax.ShapeDtypeStruct(emb_grad.sh...  32.2 us

profile of v4, /device:TPU:0, one launch (start us, length us, event | category | flops | bytes accessed | tf_op | source)
XLA Modules:
  0.0 490.4 jit_solution(5131316055656387399)
XLA Ops:
  1.3 68.4 %forward.1 = (bf16[1024,2048]{1,0:T(8,128)(2,1)}, bf16[1024,2048]{1,0:T(8,128)(2,1)}, f32[1024,2048]{1,0:T(8,128)}, f32[1024,2048]{1,0:T(8,128)}, f32[1024,2048]...) custom-call(bf16[1024,512]{1,0:T(8,128)(2,1)} %feat.1, ...), custom_call_target="tpu_custom_call" | custom-call | flops 38654705664 | bytes 100663296 | tf_op jit(solution)/shard_map/forward/pallas_call | solution.py:169
  69.7 118.6 %corr_grad.1 = (f32[1024,2048]{1,0:T(8,128)}, bf16[1024,2048]{1,0:T(8,128)(2,1)}, f32[1,1]{1,0:T(1,128)}) custom-call(f32[1,1]{1,0:T(1,128)} %bitcast.10.off_ref, f32[3,8,512]{2,1,0:T(8,128)} %get-tuple-element.30.inv_ref, bf16[1024,2048]{1,0:T(8,128)(2,1)} %get-tuple-element.31.left_ref, bf16[1024,2048]{1,0:T(8,128)(2,1)} %get-tuple-element.32.right_ref, ...), custom_call_target="tpu_custom_call" | custom-call | flops 17179869184 | bytes 33554432 | tf_op jit(solution)/shard_map/corr_grad/pallas_call | solution.py:447
  188.3 268.1 %backward.1 = (f32[4608,2048]{1,0:T(8,128)}, f32[2,2,2048]{2,1,0:T(2,128)}) custom-call(bf16[1024,2048]{1,0:T(8,128)(2,1)} %get-tuple-element.35.left_2, bf16[1024,2048]{1,0:T(8,128)(2,1)} %get-tuple-element.36.grad_z, bf16[2048,2048]{1,0:T(8,128)(2,1)} %w_out.3, f32[1024,2048]{1,0:T(8,128)} %get-tuple-element.37.normed_2, ...), custom_call_target="tpu_custom_call" | custom-call | flops 36507222016 | bytes 67108864 | tf_op jit(solution)/shard_map/backward/pallas_call | solution.py:712
  456.4 32.2 %to_outputs.1 = (f32[1024,2048]{1,0:T(8,128)}, f32[512,2048]{1,0:T(8,128)}, f32[2048,2048]{1,0:T(8,128)}, f32[2048,2048]{1,0:T(8,128)}, f32[1,2048]{1,0:T(1,128)...) custom-call(f32[4608,2048]{1,0:T(8,128)} %get-tuple-element.40.sums_ref, ...), custom_call_target="tpu_custom_call" | custom-call | tf_op jit(solution)/shard_map/to_outputs/pallas_call | solution.py:781

commit v5 on v4

--- a/solution.py
+++ b/solution.py
@@ -193,6 +193,13 @@
 PAIR, RS1, RS2, RS3, AG3, AG2, AG1, AGP, LOCAL = range(9)
 
 
+PARTS = 2
+
+
+def columns_of(unit, width):
+    return pl.ds(pl.multiple_of(lax.rem(unit, PARTS) * width, UNIT), width)
+
+
 class Exchange:
     def __init__(self, me, ring, halves, gathered, recv_pair, recv_1, recv_2, recv_3, total, send_sems, recv_sems, row_of, depth, send_total=False):
         self.depth, self.send_total = depth, send_total
@@ -233,7 +240,7 @@
                 AG1: (b1 * 64, 64, p1),
                 AGP: (0, 128, partner),
             }[kind]
-            src = dst = self.gathered.at[rows(row + start, size)]
+            src = dst = self.gathered.at[rows(row + start, size), columns_of(unit, total.shape[1])]
             if kind == AG3 and self.send_total:
                 src = total.at[rows(start, size)]
         return pltpu.make_async_remote_copy(src_ref=src, dst_ref=dst, send_sem=self.send_sems.at[slot, kind], recv_sem=self.recv_sems.at[slot, kind], device_id=(peer,), device_id_type=MESH_ID)
@@ -278,38 +285,47 @@
     lax.fori_loop(0, units + max(lags), step, 0)
 
 
-def product_unit(left_ref, right_ref, col_other, col_mine, halves, total, slot, unit, blocks):
+def product_unit(left_ref, right_ref, col_other, col_mine, halves, mine, ring, slot, unit, blocks):
     left = jnp.concatenate([left_ref[:, pl.ds(pl.multiple_of(col_other, UNIT), UNIT)], left_ref[:, pl.ds(pl.multiple_of(col_mine, UNIT), UNIT)]], axis=1)
-    width = right_ref.shape[1] // blocks
+    part = halves.shape[2]
+    width = part // blocks
     for block in range(blocks):
         cols = pl.ds(block * width, width)
-        out = contract_rows(left, right_ref[:, cols])
-        halves[slot, :, cols] = out[:UNIT]
-        total[unit, :, cols] = out[UNIT:]
+        source = pl.ds(pl.multiple_of(lax.rem(unit, PARTS) * part + block * width, UNIT), width)
+        out = contract_rows(left, right_ref[:, source])
+        halves[ring, :, cols] = out[:UNIT]
+        mine[slot, :, cols] = out[UNIT:]
 
 
 RING = 3
-CORR_LAGS = (0, 1, 4, 6, 9, 12, 15, 18, 20)
-
-
-def corr_kernel(shards, row_count, off_ref, inv_ref, left_ref, right_ref, normed, emb_out, back_out, loss_ref, grad_ref, emb_grad, back, norm_in, loss_acc, wide, slots, halves, recv_pair, recv_1, recv_2, recv_3, total, send_sems, recv_sems, sum_send, sum_recv, norm_sems, store_sems):
+CORR_LAGS = (0, 2, 5, 7, 10, 13, 16, 19, 21)
+
+
+def corr_kernel(shards, row_count, off_ref, inv_ref, emb_a, emb_b, normed, emb_out, back_out, loss_ref, left_ref, right_ref, grad_ref, emb_grad, back, norm_in, loss_acc, wide, slots, halves, recv_pair, recv_1, recv_2, recv_3, total, send_sems, recv_sems, sum_send, sum_recv, norm_sems, store_sems):
     me = lax.axis_index(DATA_AXIS)
+    loads = [pltpu.make_async_copy(emb_b, right_ref, store_sems.at[0]), pltpu.make_async_copy(emb_a, left_ref, store_sems.at[1])]
+    for copy in loads:
+        copy.start()
     rows, width = right_ref.shape
     half_rows = width // 2
-    units = half_rows // UNIT
+    units = half_rows // UNIT * PARTS
+    part_width = width // PARTS
     groups = width // COLS
     _, half = flip(me, 1)
     enter_all(me, shards)
-    ex = Exchange(me, RING, halves, grad_ref, recv_pair, recv_1, recv_2, recv_3, total, send_sems, recv_sems, lambda unit, h: h * half_rows + unit * UNIT, units)
+    ex = Exchange(me, RING, halves, grad_ref, recv_pair, recv_1, recv_2, recv_3, total, send_sems, recv_sems, lambda unit, h: h * half_rows + lax.div(unit, PARTS) * UNIT, units)
     sums = SumExchange(me, shards, slots, sum_send, sum_recv)
     loss_acc[...] = jnp.zeros_like(loss_acc)
+    for copy in loads:
+        copy.wait()
 
     def produce(unit):
         @pl.when(unit >= RING)
         def _():
             ex.copy(unit - RING, PAIR).wait_send()
 
-        product_unit(left_ref, right_ref, (1 - half) * half_rows + unit * UNIT, half * half_rows + unit * UNIT, halves, total, lax.rem(unit, RING), unit, 4)
+        local = lax.div(unit, PARTS) * UNIT
+        product_unit(left_ref, right_ref, (1 - half) * half_rows + local, half * half_rows + local, halves, total, lax.rem(unit, RING), unit, unit, 2)
         ex.copy(unit, PAIR).start()
 
     def pair_step(unit):
@@ -322,14 +338,15 @@
         start = ex.owned(unit)
         keep = pl.ds(pl.multiple_of(start, 16), 16)
         corr = (total[unit, keep] + recv_3[unit]) * (1.0 / row_count)
-        row = half * half_rows + unit * UNIT + start
-        on_diag = lax.broadcasted_iota(jnp.int32, (16, width), 0) + row == lax.broadcasted_iota(jnp.int32, (16, width), 1)
+        row = half * half_rows + lax.div(unit, PARTS) * UNIT + start
+        shift = row - lax.rem(unit, PARTS) * part_width
+        on_diag = lax.broadcasted_iota(jnp.int32, (16, part_width), 0) + shift == lax.broadcasted_iota(jnp.int32, (16, part_width), 1)
         off_weight = off_ref[0, 0]
         miss = 1.0 - corr
         terms = jnp.where(on_diag, miss * miss, off_weight * (corr * corr))
         loss_acc[...] += terms[:8] + terms[8:]
         grad = jnp.where(on_diag, -2.0 * miss, 2.0 * off_weight * corr).astype(jnp.bfloat16)
-        grad_ref[pl.ds(pl.multiple_of(row, 16), 16)] = grad
+        grad_ref[pl.ds(pl.multiple_of(row, 16), 16), columns_of(unit, part_width)] = grad
         ex.copy(unit, AG3).start()
 
     def forward(kind):
@@ -339,8 +356,12 @@
                 ex.copy(unit, kind + 1).start()
 
             if kind == AG1:
-                for side in range(2):
-                    load_norm(row_of(unit, side), lax.rem(unit, 2), side).start()
+
+                @pl.when(lax.rem(unit, PARTS) == PARTS - 1)
+                def _():
+                    block = lax.div(unit, PARTS)
+                    for side in range(2):
+                        load_norm(row_of(block, side), lax.rem(block, 2), side).start()
 
         return stage
 
@@ -353,8 +374,14 @@
     def load_norm(start, slot, side):
         return pltpu.make_async_copy(normed.at[:, lanes(start)], norm_in.at[slot, side], norm_sems.at[slot, side])
 
+    def arrive(unit):
+        ex.copy(unit, AGP).wait()
+
+        @pl.when(lax.rem(unit, PARTS) == PARTS - 1)
+        def _():
+            embed(lax.div(unit, PARTS))
+
     def embed(unit):
-        ex.copy(unit, AGP).wait()
         slot = lax.rem(unit, 2)
         starts = [row_of(unit, side) for side in range(2)]
         rhs = jnp.concatenate([grad_ref[lanes(start)] for start in starts], axis=0)
@@ -374,11 +401,11 @@
             wide[0:1, lanes(starts[side])] = plain[side]
             wide[1:2, lanes(starts[side])] = crossed[side]
 
-    pipeline(units, CORR_LAGS, [produce, pair_step, lambda u: ex.reduce_step(u, RS1), lambda u: ex.reduce_step(u, RS2), finish, forward(AG3), forward(AG2), forward(AG1), embed])
+    pipeline(units, CORR_LAGS, [produce, pair_step, lambda u: ex.reduce_step(u, RS1), lambda u: ex.reduce_step(u, RS2), finish, forward(AG3), forward(AG2), forward(AG1), arrive])
     for unit in range(units - RING, units):
         ex.copy(unit, PAIR).wait_send()
     folded = loss_acc[:, :UNIT]
-    for index in range(1, width // UNIT):
+    for index in range(1, part_width // UNIT):
         folded = folded + loss_acc[:, index * UNIT : (index + 1) * UNIT]
     slots[0, me, :, COLS:] = folded
     for index in range(groups):
@@ -447,18 +474,20 @@
     return pl.pallas_call(
         functools.partial(corr_kernel, shards, row_count),
         out_shape=(jax.ShapeDtypeStruct((rows, width), jnp.float32), jax.ShapeDtypeStruct((rows, width), jnp.bfloat16), jax.ShapeDtypeStruct((1, 1), jnp.float32)),
-        in_specs=[pl.BlockSpec(memory_space=pltpu.SMEM), vmem, vmem, vmem, hbm],
+        in_specs=[pl.BlockSpec(memory_space=pltpu.SMEM), vmem, hbm, hbm, hbm],
         out_specs=(hbm, hbm, pl.BlockSpec(memory_space=pltpu.SMEM)),
         scratch_shapes=[
+            pltpu.VMEM((rows, width), jnp.bfloat16),
+            pltpu.VMEM((rows, width), jnp.bfloat16),
             pltpu.VMEM((width, width), jnp.bfloat16),
             pltpu.VMEM((rows, width), jnp.float32),
             pltpu.VMEM((rows, width), jnp.bfloat16),
             pltpu.VMEM((2, 2, rows, UNIT), jnp.float32),
-            pltpu.VMEM((8, width), jnp.float32),
+            pltpu.VMEM((8, width // PARTS), jnp.float32),
             pltpu.VMEM((8, width), jnp.float32),
             pltpu.VMEM((1, shards, 8, COLS + UNIT), jnp.float32),
         ]
-        + exchange_scratch(width // 2 // UNIT, width)
+        + exchange_scratch(width // 2 // UNIT * PARTS, width // PARTS)
         + [pltpu.SemaphoreType.DMA((1, shards)), pltpu.SemaphoreType.DMA((1, shards)), pltpu.SemaphoreType.DMA((2, 2)), pltpu.SemaphoreType.DMA((2,))],
         compiler_params=pltpu.CompilerParams(collective_id=2, has_side_effects=True, vmem_limit_bytes=VMEM_LIMIT),
         cost_estimate=pl.CostEstimate(flops=4 * rows * width * width, bytes_accessed=8 * width * width, transcendentals=0),
@@ -466,14 +495,14 @@
     )(off_weight.reshape(1, 1), inv_std, emb_a, emb_b, normed)
 
 
-DEPTH = 18
-DEPTH_1, DEPTH_2, DEPTH_3 = 15, 9, 6
-CHAIN = 6
-PER_TICK = 2
+DEPTH = 36
+DEPTH_1, DEPTH_2, DEPTH_3 = 21, 12, 6
+CHAIN = 11
+PER_TICK = 1
 BLOCK = 256
 NORM_SLOTS = 3
 WEIGHT_SLOTS = 3
-BACK_LAGS = (1, 4, 6, 7, 9, 12, 16, 18)
+BACK_LAGS = (1, 4, 6, 8, 11, 15, 20, 24)
 
 
 def backward_kernel(shards, row_count, left_2, grad_z, w_out, normed_2, left_1, w_mid, normed_1, feat, gain_1, bias_1, gain_2, bias_2, inv_ref, out_ref, stat_ref, vecs, left, feat_in, grad, weight, normed, deriv, halves, mine, total, recv_1, recv_2, recv_3, wide, slots, send_sems, recv_sems, load_sems, weight_sems, normed_sems, sum_send, sum_recv):
@@ -482,8 +511,9 @@
     rows, width = left.shape
     groups = width // COLS
     blocks = width // BLOCK
-    units_full = width // 2 // UNIT
-    units_last = feat_in.shape[1] // 2 // UNIT
+    units_full = width // 2 // UNIT * PARTS
+    units_last = feat_in.shape[1] // 2 // UNIT * PARTS
+    part_width = width // PARTS
     units = 2 * units_full + units_last
     ticks = units + max(BACK_LAGS)
 
@@ -537,7 +567,7 @@
     def row_of(unit, h):
         layer = lax.div(unit, units_full)
         part = width // 2 - (width // 2 - feat_in.shape[1] // 2) * lax.div(layer, 2)
-        return layer * width + h * part + lax.rem(unit, units_full) * UNIT
+        return layer * width + h * part + lax.div(lax.rem(unit, units_full), PARTS) * UNIT
 
     ex = Exchange(me, 2, halves, out_ref, total, recv_1, recv_2, recv_3, total, send_sems, recv_sems, row_of, DEPTH, send_total=True)
     sums = SumExchange(me, shards, slots, sum_send, sum_recv)
@@ -548,16 +578,9 @@
             ex.copy(unit - 2, PAIR).wait_send()
 
         which = lax.rem(lax.div(unit, units_full), 2)
-        local = lax.rem(unit, units_full) * UNIT
+        local = lax.div(lax.rem(unit, units_full), PARTS) * UNIT
         ring = lax.rem(unit, 2)
-        col_other, col_mine = (1 - half) * part + local, half * part + local
-        lhs = jnp.concatenate([source[:, pl.ds(pl.multiple_of(col_other, UNIT), UNIT)], source[:, pl.ds(pl.multiple_of(col_mine, UNIT), UNIT)]], axis=1)
-        chunk = width // 4
-        for index in range(4):
-            cols = pl.ds(index * chunk, chunk)
-            prod = contract_rows(lhs, grad[which, :, cols])
-            halves[ring, :, cols] = prod[:UNIT]
-            mine[ring, :, cols] = prod[UNIT:]
+        product_unit(source, grad.at[which], (1 - half) * part + local, half * part + local, halves, mine, ring, ring, unit, 2)
         ex.copy(unit, PAIR).start()
 
     def pair_step(unit):
@@ -569,7 +592,7 @@
     def to_out(unit):
         start = ex.owned(unit)
         slot = lax.rem(unit, DEPTH)
-        return pltpu.make_async_copy(total.at[slot, pl.ds(pl.multiple_of(start, 16), 16)], out_ref.at[pl.ds(pl.multiple_of(row_of(unit, half) + start, 16), 16)], send_sems.at[slot, LOCAL])
+        return pltpu.make_async_copy(total.at[slot, pl.ds(pl.multiple_of(start, 16), 16)], out_ref.at[pl.ds(pl.multiple_of(row_of(unit, half) + start, 16), 16), columns_of(unit, part_width)], send_sems.at[slot, LOCAL])
 
     def finish(unit):
         ex.copy(unit, RS3).wait()
@@ -722,12 +745,12 @@
             pltpu.VMEM((WEIGHT_SLOTS, BLOCK, width), jnp.bfloat16),
             pltpu.VMEM((NORM_SLOTS, rows, BLOCK), jnp.float32),
             pltpu.VMEM((rows, width), jnp.float32),
-            pltpu.VMEM((2, UNIT, width), jnp.float32),
-            pltpu.VMEM((2, UNIT, width), jnp.float32),
-            pltpu.VMEM((DEPTH, UNIT, width), jnp.float32),
-            pltpu.VMEM((DEPTH_1, 64, width), jnp.float32),
-            pltpu.VMEM((DEPTH_2, 32, width), jnp.float32),
-            pltpu.VMEM((DEPTH_3, 16, width), jnp.float32),
+            pltpu.VMEM((2, UNIT, width // PARTS), jnp.float32),
+            pltpu.VMEM((2, UNIT, width // PARTS), jnp.float32),
+            pltpu.VMEM((DEPTH, UNIT, width // PARTS), jnp.float32),
+            pltpu.VMEM((DEPTH_1, 64, width // PARTS), jnp.float32),
+            pltpu.VMEM((DEPTH_2, 32, width // PARTS), jnp.float32),
+            pltpu.VMEM((DEPTH_3, 16, width // PARTS), jnp.float32),
             pltpu.VMEM((8, width), jnp.float32),
             pltpu.VMEM((2, shards, 8, COLS), jnp.float32),
             pltpu.SemaphoreType.DMA((DEPTH, 9)),

time: 491 us -> 484 us (0.986)
  Pallas kernels: 487 us -> 480 us
where the time goes in v5:
time: 484 us; the launch traced here: 483 us
  Pallas kernels  480 us (99%)
    pallas_call x1, Pallas kernels, backward(): pl.pallas_call(functools.partial(backward_kernel, shards, row_count), out...  265 us
    pallas_call x1, Pallas kernels, corr_grad(): pl.pallas_call(functools.partial(corr_kernel, shards, row_count), out_sha...  115 us
    pallas_call x1, Pallas kernels, forward_pass(): pl.pallas_call(functools.partial(forward_kernel, shards, row_count), out_...  68.4 us
    pallas_call x1, Pallas kernels, to_outputs(): pl.pallas_call(output_kernel, out_shape=(jax.ShapeDtypeStruct(emb_grad.sh...  32.2 us

profile of v5, /device:TPU:0, one launch (start us, length us, event | category | flops | bytes accessed | tf_op | source)
XLA Modules:
  0.0 483.2 jit_solution(13115232924364456312)
XLA Ops:
  1.3 68.4 %forward.1 = (bf16[1024,2048]{1,0:T(8,128)(2,1)}, bf16[1024,2048]{1,0:T(8,128)(2,1)}, f32[1024,2048]{1,0:T(8,128)}, f32[1024,2048]{1,0:T(8,128)}, f32[1024,2048]...) custom-call(bf16[1024,512]{1,0:T(8,128)(2,1)} %feat.1, ...), custom_call_target="tpu_custom_call" | custom-call | flops 38654705664 | bytes 100663296 | tf_op jit(solution)/shard_map/forward/pallas_call | solution.py:169
  69.7 114.7 %corr_grad.1 = (f32[1024,2048]{1,0:T(8,128)}, bf16[1024,2048]{1,0:T(8,128)(2,1)}, f32[1,1]{1,0:T(1,128)}) custom-call(f32[1,1]{1,0:T(1,128)} %bitcast.10.off_ref, f32[3,8,512]{2,1,0:T(8,128)} %get-tuple-element.30.inv_ref, bf16[1024,2048]{1,0:T(8,128)(2,1)} %get-tuple-element.31.emb_a, bf16[1024,2048]{1,0:T(8,128)(2,1)} %get-tuple-element.32.emb_b, ...), custom_call_target="tpu_custom_call" | custom-call | flops 17179869184 | bytes 33554432 | tf_op jit(solution)/shard_map/corr_grad/pallas_call | solution.py:474
  184.4 264.8 %backward.1 = (f32[4608,2048]{1,0:T(8,128)}, f32[2,2,2048]{2,1,0:T(2,128)}) custom-call(bf16[1024,2048]{1,0:T(8,128)(2,1)} %get-tuple-element.35.left_2, bf16[1024,2048]{1,0:T(8,128)(2,1)} %get-tuple-element.36.grad_z, bf16[2048,2048]{1,0:T(8,128)(2,1)} %w_out.3, f32[1024,2048]{1,0:T(8,128)} %get-tuple-element.37.normed_2, ...), custom_call_target="tpu_custom_call" | custom-call | flops 36507222016 | bytes 67108864 | tf_op jit(solution)/shard_map/backward/pallas_call | solution.py:735
  449.2 32.2 %to_outputs.1 = (f32[1024,2048]{1,0:T(8,128)}, f32[512,2048]{1,0:T(8,128)}, f32[2048,2048]{1,0:T(8,128)}, f32[2048,2048]{1,0:T(8,128)}, f32[1,2048]{1,0:T(1,128)...) custom-call(f32[4608,2048]{1,0:T(8,128)} %get-tuple-element.40.sums_ref, ...), custom_call_target="tpu_custom_call" | custom-call | tf_op jit(solution)/shard_map/to_outputs/pallas_call | solution.py:804

commit v6 on v5

--- a/solution.py
+++ b/solution.py
@@ -67,7 +67,7 @@
     rows, width = act_1.shape
     groups = width // COLS
     copies = [pltpu.make_async_copy(src, dst, load_sems.at[index]) for index, (src, dst) in enumerate([(feat_a, feat.at[0]), (w_in, weight_in.at[0]), (feat_b, feat.at[1]), (t_in, weight_in.at[1]), (w_mid, weight.at[0]), (t_mid, weight.at[1]), (w_out, weight.at[0]), (t_out, weight.at[1])])]
-    for index in range(6):
+    for index in range(4):
         copies[index].start()
     enter_all(me, shards)
     ex = SumExchange(me, shards, slots, send_sems, recv_sems)
@@ -123,6 +123,8 @@
 
     copies[0].wait()
     copies[1].wait()
+    copies[4].start()
+    copies[5].start()
     product(0, feat.at[0], weight_in.at[0], pre.at[0])
     copies[2].wait()
     copies[3].wait()
@@ -298,10 +300,11 @@
 
 
 RING = 3
+BACK_ROWS = 1024
 CORR_LAGS = (0, 2, 5, 7, 10, 13, 16, 19, 21)
 
 
-def corr_kernel(shards, row_count, off_ref, inv_ref, emb_a, emb_b, normed, emb_out, back_out, loss_ref, left_ref, right_ref, grad_ref, emb_grad, back, norm_in, loss_acc, wide, slots, halves, recv_pair, recv_1, recv_2, recv_3, total, send_sems, recv_sems, sum_send, sum_recv, norm_sems, store_sems):
+def corr_kernel(shards, row_count, off_ref, inv_ref, emb_a, emb_b, normed, emb_out, back_out, loss_ref, left_ref, right_ref, grad_ref, emb_grad, back, norm_in, loss_acc, wide, slots, halves, recv_pair, recv_1, recv_2, recv_3, total, send_sems, recv_sems, sum_send, sum_recv, norm_sems, store_sems, back_sems):
     me = lax.axis_index(DATA_AXIS)
     loads = [pltpu.make_async_copy(emb_b, right_ref, store_sems.at[0]), pltpu.make_async_copy(emb_a, left_ref, store_sems.at[1])]
     for copy in loads:
@@ -364,6 +367,13 @@
                         load_norm(row_of(block, side), lax.rem(block, 2), side).start()
 
         return stage
+
+    for index in range(groups):
+        wide[2:3, index * COLS : (index + 1) * COLS] = inv_ref[2, index : index + 1]
+
+    def packed(which):
+        piece = width // 8
+        return [(4 * row + 2 * side + index, row, pl.ds(side * half_rows + (2 * which + index) * piece, piece)) for row in range(2) for side in range(2) for index in range(2)]
 
     def row_of(unit, side):
         return (half + side * (1 - 2 * half)) * half_rows + unit * UNIT
@@ -401,57 +411,70 @@
             wide[0:1, lanes(starts[side])] = plain[side]
             wide[1:2, lanes(starts[side])] = crossed[side]
 
+        @pl.when(unit == half_rows // UNIT // 2 - 1)
+        def _():
+            for line, row, cols in packed(0):
+                slots[0, me, line : line + 1, : width // 8] = wide[row : row + 1, cols]
+            slots[0, me, :, width // 8 :] = jnp.zeros((8, UNIT), jnp.float32)
+            sums.start(0)
+
     pipeline(units, CORR_LAGS, [produce, pair_step, lambda u: ex.reduce_step(u, RS1), lambda u: ex.reduce_step(u, RS2), finish, forward(AG3), forward(AG2), forward(AG1), arrive])
     for unit in range(units - RING, units):
         ex.copy(unit, PAIR).wait_send()
     folded = loss_acc[:, :UNIT]
     for index in range(1, part_width // UNIT):
         folded = folded + loss_acc[:, index * UNIT : (index + 1) * UNIT]
-    slots[0, me, :, COLS:] = folded
-    for index in range(groups):
-        cols = pl.ds(index * COLS, COLS)
-        slots[0, me, index : index + 1, :COLS] = wide[0:1, cols]
-        slots[0, me, groups + index : groups + index + 1, :COLS] = wide[1:2, cols]
-    sums.start(0)
+    for line, row, cols in packed(1):
+        slots[1, me, line : line + 1, : width // 8] = wide[row : row + 1, cols]
+    slots[1, me, :, width // 8 :] = folded
+    sums.start(1)
     store_emb = pltpu.make_async_copy(emb_grad, emb_out, store_sems.at[0])
     store_emb.start()
-
-    def load_block(index, slot):
-        return [load_norm((2 * index + side) * UNIT, slot, side) for side in range(2)]
-
-    for copy in load_block(0, 0) + load_block(1, 1):
-        copy.start()
-    summed = sums.finish(0)
-    loss_ref[0, 0] = jnp.sum(summed[:, COLS:])
-    means = summed[:, :COLS] / row_count
-    for index in range(groups):
-        cols = pl.ds(index * COLS, COLS)
-        wide[0:1, cols] = means[index : index + 1]
-        wide[1:2, cols] = means[groups + index : groups + index + 1]
-        wide[2:3, cols] = inv_ref[2, index : index + 1]
-
-    def norm_back(index, carry):
-        slot = lax.rem(index, 2)
-        for side, copy in enumerate(load_block(index, slot)):
+    steps = width // (2 * UNIT)
+
+    def block_at(position):
+        place = lax.rem(position, steps // 2)
+        return 2 * lax.div(position, steps // 2) + lax.rem(place, 2) + (steps // 2) * lax.div(place, 2)
+
+    def load_block(position):
+        return [load_norm((2 * block_at(position) + side) * UNIT, lax.rem(position, 2), side) for side in range(2)]
+
+    def store_block(position):
+        cols = pl.ds(pl.multiple_of(2 * block_at(position) * UNIT, 2 * UNIT), 2 * UNIT)
+        return pltpu.make_async_copy(back.at[:, cols], back_out.at[:, cols], back_sems.at[position])
+
+    for position in range(2):
+        for copy in load_block(position):
+            copy.start()
+
+    def norm_back(position, carry):
+        slot = lax.rem(position, 2)
+        for side, copy in enumerate(load_block(position)):
             copy.wait()
-            start = (2 * index + side) * UNIT
+            start = (2 * block_at(position) + side) * UNIT
             mean_g, mean_gn, inv = wide[0:1, lanes(start)], wide[1:2, lanes(start)], wide[2:3, lanes(start)]
-            for chunk in range(rows // ROWS):
-                part = pl.ds(chunk * ROWS, ROWS)
+            for chunk in range(rows // BACK_ROWS):
+                part = pl.ds(chunk * BACK_ROWS, BACK_ROWS)
                 back[part, lanes(start)] = ((emb_grad[part, lanes(start)] - mean_g - norm_in[slot, side, part] * mean_gn) * inv).astype(jnp.bfloat16)
-
-        @pl.when(index + 2 < width // (2 * UNIT))
-        def _():
-            for copy in load_block(index + 2, slot):
+        store_block(position).start()
+
+        @pl.when(position + 2 < steps)
+        def _():
+            for copy in load_block(position + 2):
                 copy.start()
 
         return carry
 
-    lax.fori_loop(0, width // (2 * UNIT), norm_back, 0)
-    store_back = pltpu.make_async_copy(back, back_out, store_sems.at[1])
-    store_back.start()
+    for which in range(2):
+        summed = sums.finish(which)
+        if which == 1:
+            loss_ref[0, 0] = jnp.sum(summed[:, width // 8 :])
+        for line, row, cols in packed(which):
+            wide[row : row + 1, cols] = summed[line : line + 1, : width // 8] / row_count
+        lax.fori_loop(which * (steps // 2), (which + 1) * (steps // 2), norm_back, 0)
+    for position in range(steps):
+        store_block(position).wait()
     store_emb.wait()
-    store_back.wait()
 
 
 def exchange_scratch(units, width):
@@ -485,10 +508,10 @@
             pltpu.VMEM((2, 2, rows, UNIT), jnp.float32),
             pltpu.VMEM((8, width // PARTS), jnp.float32),
             pltpu.VMEM((8, width), jnp.float32),
-            pltpu.VMEM((1, shards, 8, COLS + UNIT), jnp.float32),
+            pltpu.VMEM((2, shards, 8, width // 8 + UNIT), jnp.float32),
         ]
         + exchange_scratch(width // 2 // UNIT * PARTS, width // PARTS)
-        + [pltpu.SemaphoreType.DMA((1, shards)), pltpu.SemaphoreType.DMA((1, shards)), pltpu.SemaphoreType.DMA((2, 2)), pltpu.SemaphoreType.DMA((2,))],
+        + [pltpu.SemaphoreType.DMA((2, shards)), pltpu.SemaphoreType.DMA((2, shards)), pltpu.SemaphoreType.DMA((2, 2)), pltpu.SemaphoreType.DMA((2,)), pltpu.SemaphoreType.DMA((width // (2 * UNIT),))],
         compiler_params=pltpu.CompilerParams(collective_id=2, has_side_effects=True, vmem_limit_bytes=VMEM_LIMIT),
         cost_estimate=pl.CostEstimate(flops=4 * rows * width * width, bytes_accessed=8 * width * width, transcendentals=0),
         name="corr_grad",
@@ -499,10 +522,11 @@
 DEPTH_1, DEPTH_2, DEPTH_3 = 21, 12, 6
 CHAIN = 11
 PER_TICK = 1
+CHAIN_START = 2
 BLOCK = 256
 NORM_SLOTS = 3
 WEIGHT_SLOTS = 3
-BACK_LAGS = (1, 4, 6, 8, 11, 15, 20, 24)
+BACK_LAGS = (1, 4, 6, 8, 11, 14, 18, 21)
 
 
 def backward_kernel(shards, row_count, left_2, grad_z, w_out, normed_2, left_1, w_mid, normed_1, feat, gain_1, bias_1, gain_2, bias_2, inv_ref, out_ref, stat_ref, vecs, left, feat_in, grad, weight, normed, deriv, halves, mine, total, recv_1, recv_2, recv_3, wide, slots, send_sems, recv_sems, load_sems, weight_sems, normed_sems, sum_send, sum_recv):
@@ -552,11 +576,6 @@
 
     load_left.start()
     load_grad.start()
-    for number in range(WEIGHT_SLOTS):
-        weight_copy(w_out, number).start()
-    for number in range(NORM_SLOTS):
-        normed_copy(normed_2, number).start()
-    load_feat.start()
     for layer, (gain, bias) in enumerate(((gain_2, bias_2), (gain_1, bias_1))):
         vecs[layer, 0:1] = gain[...]
         vecs[layer, 1:2] = bias[...]
@@ -685,6 +704,11 @@
                 @pl.when(now == 0)
                 def _():
                     load_grad.wait()
+                    for number in range(WEIGHT_SLOTS):
+                        weight_copy(w_out, number).start()
+                    for number in range(NORM_SLOTS):
+                        normed_copy(normed_2, number).start()
+                    load_feat.start()
 
             produce(now, left, width // 2)
 
@@ -700,10 +724,10 @@
 
             produce(now, feat_in, feat_in.shape[1] // 2)
 
-        layer, place = lax.div(now, CHAIN), lax.rem(now, CHAIN)
+        layer, place = lax.div(now - CHAIN_START, CHAIN), lax.rem(now - CHAIN_START, CHAIN)
         steps = blocks // PER_TICK
 
-        @pl.when((layer < 2) & (place < steps))
+        @pl.when((now >= CHAIN_START) & (layer < 2) & (place < steps))
         def _():
             def one(index, carry):
                 derivative(layer, place * PER_TICK + index)
@@ -715,7 +739,7 @@
             def _():
                 send_sums(layer)
 
-        @pl.when((layer < 2) & (place == CHAIN - 1))
+        @pl.when((now >= CHAIN_START) & (layer < 2) & (place == CHAIN - 1))
         def _():
             next_grad(layer)
 
@@ -767,8 +791,8 @@
     )(act_2, grad_z, w_out, normed_2, act_1, w_mid, normed_1, feat, *vectors, inv_std)
 
 
-CHUNK = 256
-FLIGHT = 8
+CHUNK = 128
+FLIGHT = 12
 
 
 def output_kernel(sums_ref, emb_ref, stat_ref, emb_out, in_out, mid_out, last_out, gain_1, bias_1, gain_2, bias_2, buffer, read_sems, write_sems):

time: 484 us -> 482 us (level)
  no operation moved by 1% of the time
where the time goes in v6:
time: 482 us; the launch traced here: 481 us
  Pallas kernels  478 us (99%)
    pallas_call x1, Pallas kernels, backward(): pl.pallas_call(functools.partial(backward_kernel, shards, row_count), out...  264 us
    pallas_call x1, Pallas kernels, corr_grad(): pl.pallas_call(functools.partial(corr_kernel, shards, row_count), out_sha...  114 us
    pallas_call x1, Pallas kernels, forward_pass(): pl.pallas_call(functools.partial(forward_kernel, shards, row_count), out_...  68.4 us
    pallas_call x1, Pallas kernels, to_outputs(): pl.pallas_call(output_kernel, out_shape=(jax.ShapeDtypeStruct(emb_grad.sh...  31.7 us

profile of v6, /device:TPU:0, one launch (start us, length us, event | category | flops | bytes accessed | tf_op | source)
XLA Modules:
  0.0 481.1 jit_solution(15219027366854632370)
XLA Ops:
  1.3 68.4 %forward.1 = (bf16[1024,2048]{1,0:T(8,128)(2,1)}, bf16[1024,2048]{1,0:T(8,128)(2,1)}, f32[1024,2048]{1,0:T(8,128)}, f32[1024,2048]{1,0:T(8,128)}, f32[1024,2048]...) custom-call(bf16[1024,512]{1,0:T(8,128)(2,1)} %feat.1, ...), custom_call_target="tpu_custom_call" | custom-call | flops 38654705664 | bytes 100663296 | tf_op jit(solution)/shard_map/forward/pallas_call | solution.py:171
  69.7 114.4 %corr_grad.1 = (f32[1024,2048]{1,0:T(8,128)}, bf16[1024,2048]{1,0:T(8,128)(2,1)}, f32[1,1]{1,0:T(1,128)}) custom-call(f32[1,1]{1,0:T(1,128)} %bitcast.10.off_ref, f32[3,8,512]{2,1,0:T(8,128)} %get-tuple-element.30.inv_ref, bf16[1024,2048]{1,0:T(8,128)(2,1)} %get-tuple-element.31.emb_a, bf16[1024,2048]{1,0:T(8,128)(2,1)} %get-tuple-element.32.emb_b, ...), custom_call_target="tpu_custom_call" | custom-call | flops 17179869184 | bytes 33554432 | tf_op jit(solution)/shard_map/corr_grad/pallas_call | solution.py:497
  184.1 263.5 %backward.1 = (f32[4608,2048]{1,0:T(8,128)}, f32[2,2,2048]{2,1,0:T(2,128)}) custom-call(bf16[1024,2048]{1,0:T(8,128)(2,1)} %get-tuple-element.35.left_2, bf16[1024,2048]{1,0:T(8,128)(2,1)} %get-tuple-element.36.grad_z, bf16[2048,2048]{1,0:T(8,128)(2,1)} %w_out.3, f32[1024,2048]{1,0:T(8,128)} %get-tuple-element.37.normed_2, ...), custom_call_target="tpu_custom_call" | custom-call | flops 36507222016 | bytes 67108864 | tf_op jit(solution)/shard_map/backward/pallas_call | solution.py:759
  447.7 31.7 %to_outputs.1 = (f32[1024,2048]{1,0:T(8,128)}, f32[512,2048]{1,0:T(8,128)}, f32[2048,2048]{1,0:T(8,128)}, f32[2048,2048]{1,0:T(8,128)}, f32[1,2048]{1,0:T(1,128)...) custom-call(f32[4608,2048]{1,0:T(8,128)} %get-tuple-element.40.sums_ref, ...), custom_call_target="tpu_custom_call" | custom-call | tf_op jit(solution)/shard_map/to_outputs/pallas_call | solution.py:828

commit v7 on v6

--- a/solution.py
+++ b/solution.py
@@ -90,7 +90,7 @@
         lax.fori_loop(0, groups, group, 0)
         ex.start(index)
 
-    def normalise(index, source, target, layer, keep):
+    def normalise(index, source, target, layer, keep, out_group=None):
         summed = ex.finish(index) / row_count
         mean = summed[:groups]
         inv = lax.rsqrt(summed[groups:] - mean * mean + NORM_EPS)
@@ -112,6 +112,8 @@
                     gain, bias = ((gain_1, bias_1), (gain_2, bias_2))[layer]
                     out = jnp.maximum(out * gain[:, cols] + bias[:, cols], 0.0)
                 target[part, cols] = out.astype(jnp.bfloat16)
+            if out_group is not None:
+                out_group(number).start()
             return carry
 
         lax.fori_loop(0, groups, group, 0)
@@ -154,9 +156,13 @@
     normalise(4, pre.at[1], act.at[0], 2, normed_z)
     out_z = store(4, pre.at[1], normed_z)
     out_a = store(5, act.at[0], emb_a)
-    normalise(5, pre.at[2], act.at[1], 2, None)
-    out_b = store(6, act.at[1], emb_b)
-    for copy in (out_z, out_a, out_b):
+
+    def last_group(number):
+        cols = pl.ds(pl.multiple_of(number * COLS, COLS), COLS)
+        return pltpu.make_async_copy(act.at[1, :, cols], emb_b.at[:, cols], store_sems.at[6 + number])
+
+    normalise(5, pre.at[2], act.at[1], 2, None, last_group)
+    for copy in [out_z, out_a] + [last_group(number) for number in range(groups)]:
         copy.wait()
 
 
@@ -184,7 +190,7 @@
             pltpu.SemaphoreType.DMA((6, shards)),
             pltpu.SemaphoreType.DMA((6, shards)),
             pltpu.SemaphoreType.DMA((8,)),
-            pltpu.SemaphoreType.DMA((7,)),
+            pltpu.SemaphoreType.DMA((6 + groups,)),
         ],
         compiler_params=pltpu.CompilerParams(collective_id=4, has_side_effects=True, vmem_limit_bytes=VMEM_LIMIT),
         cost_estimate=pl.CostEstimate(flops=4 * rows * width * (2 * width + feat_dim), bytes_accessed=24 * width * width, transcendentals=0),

time: 482 us -> 481 us (level)
  no operation moved by 1% of the time
where the time goes in v7:
time: 481 us; the launch traced here: 480 us
  Pallas kernels  477 us (99%)
    pallas_call x1, Pallas kernels, backward(): pl.pallas_call(functools.partial(backward_kernel, shards, row_count), out...  263 us
    pallas_call x1, Pallas kernels, corr_grad(): pl.pallas_call(functools.partial(corr_kernel, shards, row_count), out_sha...  114 us
    pallas_call x1, Pallas kernels, forward_pass(): pl.pallas_call(functools.partial(forward_kernel, shards, row_count), out_...  67.9 us
    pallas_call x1, Pallas kernels, to_outputs(): pl.pallas_call(output_kernel, out_shape=(jax.ShapeDtypeStruct(emb_grad.sh...  31.7 us

profile of v7, /device:TPU:0, one launch (start us, length us, event | category | flops | bytes accessed | tf_op | source)
XLA Modules:
  0.0 480.4 jit_solution(5099352196246629624)
XLA Ops:
  1.3 67.9 %forward.1 = (bf16[1024,2048]{1,0:T(8,128)(2,1)}, bf16[1024,2048]{1,0:T(8,128)(2,1)}, f32[1024,2048]{1,0:T(8,128)}, f32[1024,2048]{1,0:T(8,128)}, f32[1024,2048]...) custom-call(bf16[1024,512]{1,0:T(8,128)(2,1)} %feat.1, ...), custom_call_target="tpu_custom_call" | custom-call | flops 38654705664 | bytes 100663296 | tf_op jit(solution)/shard_map/forward/pallas_call | solution.py:177
  69.2 114.3 %corr_grad.1 = (f32[1024,2048]{1,0:T(8,128)}, bf16[1024,2048]{1,0:T(8,128)(2,1)}, f32[1,1]{1,0:T(1,128)}) custom-call(f32[1,1]{1,0:T(1,128)} %bitcast.10.off_ref, f32[3,8,512]{2,1,0:T(8,128)} %get-tuple-element.30.inv_ref, bf16[1024,2048]{1,0:T(8,128)(2,1)} %get-tuple-element.31.emb_a, bf16[1024,2048]{1,0:T(8,128)(2,1)} %get-tuple-element.32.emb_b, ...), custom_call_target="tpu_custom_call" | custom-call | flops 17179869184 | bytes 33554432 | tf_op jit(solution)/shard_map/corr_grad/pallas_call | solution.py:503
  183.5 263.4 %backward.1 = (f32[4608,2048]{1,0:T(8,128)}, f32[2,2,2048]{2,1,0:T(2,128)}) custom-call(bf16[1024,2048]{1,0:T(8,128)(2,1)} %get-tuple-element.35.left_2, bf16[1024,2048]{1,0:T(8,128)(2,1)} %get-tuple-element.36.grad_z, bf16[2048,2048]{1,0:T(8,128)(2,1)} %w_out.3, f32[1024,2048]{1,0:T(8,128)} %get-tuple-element.37.normed_2, ...), custom_call_target="tpu_custom_call" | custom-call | flops 36507222016 | bytes 67108864 | tf_op jit(solution)/shard_map/backward/pallas_call | solution.py:765
  447.0 31.7 %to_outputs.1 = (f32[1024,2048]{1,0:T(8,128)}, f32[512,2048]{1,0:T(8,128)}, f32[2048,2048]{1,0:T(8,128)}, f32[2048,2048]{1,0:T(8,128)}, f32[1,2048]{1,0:T(1,128)...) custom-call(f32[4608,2048]{1,0:T(8,128)} %get-tuple-element.40.sums_ref, ...), custom_call_target="tpu_custom_call" | custom-call | tf_op jit(solution)/shard_map/to_outputs/pallas_call | solution.py:834
